TPU v7x, 128 devices: a whole 4x4x4 slice. The times are simulated.
128 devices in a mesh: dp: 64 (over z_hi, x, y, core), mp: 2 (over z_lo).
Axes of the slice: x: 4, y: 4, z: 4 (z_hi: 2, z_lo: 2; z = z_hi * 2 + z_lo), core: 2. Of those that a mesh axis runs over, the one named last changes fastest.
Arguments:
- inputs: bfloat16 [8192, 1792], P('dp', 'mp'), may hold values from -6 to 6
- cotangent: bfloat16 [8192, 1792], P('dp', 'mp'), may hold values from -6 to 6
- gate_weight: bfloat16 [9472, 1792], P(('mp', 'dp')), may hold values from -0.125 to 0.125
- up_weight: bfloat16 [9472, 1792], P(('mp', 'dp')), may hold values from -0.125 to 0.125
- down_weight: bfloat16 [9472, 1792], P(('mp', 'dp')), may hold values from -0.0625 to 0.0625
Outputs:
- input_grad: bfloat16 [8192, 1792], P('dp', 'mp')
- gate_grad: bfloat16 [9472, 1792], P(('mp', 'dp'))
All inputs are finite; a program needn't handle non-finite values.
Results may differ from a plain program's by a relative error of at most 0.009.
Values may be sent and summed in bfloat16 or wider, within the bound.
No kernel may reach another device: no remote copies, remote signals or barrier semaphores. Data moves between devices by JAX's collectives and lax.ppermute only.
A program may use at most 320 MiB of HBM per device.

v0:
```python
import jax
import jax.numpy as jnp
from jax import lax
from jax.sharding import Mesh
from jax.sharding import PartitionSpec as P

DP = ("dp_0", "dp_1", "dp_2", "dp_3")
MP_DP = ("mp", "dp_0", "dp_1", "dp_2", "dp_3")


def side_by_side(arrays, axis, dim, along):
    widths = [a.shape[along] for a in arrays]
    both = jnp.concatenate(arrays, axis=along)
    filled = lax.all_gather(both, axis, axis=dim, tiled=True)
    return tuple(jnp.split(filled, [sum(widths[:k]) for k in range(1, len(widths))], axis=along))


def split_up(x, dim, peers):
    lengths = x.shape
    pieces = x.reshape(*lengths[:dim], peers, lengths[dim] // peers, *lengths[dim + 1 :])
    return jnp.moveaxis(pieces, dim, 0)


def sent_and_summed(x, axis, dim):
    peers = lax.axis_size(axis)
    pieces = lax.all_to_all(split_up(x, dim, peers), axis, 0, 0, tiled=True)
    return jnp.sum(pieces.astype(jnp.float32), axis=0)


def in_order(pieces, dim):
    pieces = jnp.moveaxis(pieces, 0, dim)
    lengths = pieces.shape
    return pieces.reshape(*lengths[:dim], lengths[dim] * lengths[dim + 1], *lengths[dim + 2 :])


def moved_by_axis(pieces, axes, turns):
    lengths = [lax.axis_size(a) for a in axes]
    pieces = pieces.reshape(*lengths, *pieces.shape[1:])
    for k in turns:
        pieces = lax.all_to_all(pieces, axes[k], split_axis=k, concat_axis=k, tiled=True)
    return pieces.reshape(-1, *pieces.shape[len(axes) :])


def exchange_by_chip(x, groups, turns, split_dim, concat_dim):
    peers = lax.axis_size(groups[0]) * lax.axis_size(groups[1])
    pieces = split_up(x, split_dim, peers)
    return in_order(moved_by_axis(pieces, groups, turns), concat_dim)


def tdot(left, right):
    return lax.dot_general(
        left, right, (((0,), (0,)), ((), ())), preferred_element_type=jnp.float32
    )


def rdot(left, right):
    return lax.dot_general(
        left, right, (((1,), (1,)), ((), ())), preferred_element_type=jnp.float32
    )


def per_device(inputs, cotangent, gate_weight, up_weight, down_weight):
    full_in, full_cot = side_by_side((inputs, cotangent), "mp", 1, 0)
    pieces = lax.all_gather((gate_weight, up_weight), DP, axis=0, tiled=True)
    stacked = jnp.stack([rdot(full_in, pieces[0]), rdot(full_in, pieces[1])])
    gate = stacked[0]
    up = stacked[1]
    dhidden = rdot(full_cot, lax.all_gather(down_weight, DP, axis=0, tiled=True))
    sig = jax.nn.sigmoid(gate)
    act = gate * sig
    dup = (dhidden * act).astype(jnp.bfloat16)
    dgate = (dhidden * up * sig * (1.0 + gate * (1.0 - sig))).astype(jnp.bfloat16)
    owned = exchange_by_chip(dgate, (("dp_0", "dp_1", "dp_2"), "dp_3"), (1, 0), 1, 0)
    gate_sum = tdot(owned, lax.all_gather(full_in, DP, axis=0, tiled=True))
    pieces = (
        lax.all_gather(gate_weight, DP, axis=0, tiled=True),
        lax.all_gather(up_weight, DP, axis=0, tiled=True),
    )
    total = jnp.dot(dgate, pieces[0], preferred_element_type=jnp.float32)
    partial_value = total + jnp.dot(dup, pieces[1], preferred_element_type=jnp.float32)
    input_grad = sent_and_summed(partial_value.astype(jnp.bfloat16), "mp", 1).astype(jnp.bfloat16)
    gate_grad = gate_sum.astype(jnp.bfloat16)
    return (input_grad, gate_grad)


def solution(mesh):
    torus = Mesh(
        mesh.devices.reshape(2, 4, 4, 2, mesh.shape["mp"]), ("dp_0", "dp_1", "dp_2", "dp_3", "mp")
    )
    return jax.shard_map(
        per_device,
        mesh=torus,
        in_specs=(P(DP, "mp"), P(DP, "mp"), P(MP_DP, None), P(MP_DP, None), P(MP_DP, None)),
        out_specs=(P(DP, "mp"), P(MP_DP, None)),
        check_vma=False,
    )
```

profile of v0, /device:TPU:1, one launch (start us, length us, event | category | flops | bytes accessed | tf_op | source)
XLA Modules:
  0.0 530.3 jit_solution(8056646707947620844)
XLA Ops:
  7.2 0.0 all-gather.10.cloned.1.call-start
  7.2 0.7 all-gather.10.cloned.1.call-update
  7.9 0.0 all-gather.12.cloned.1.call-start
  7.9 0.7 all-gather.12.cloned.1.call-update
  8.6 0.0 all-gather.14.cloned.1.call-start
  8.7 0.7 all-gather.14.cloned.1.call-update
  9.4 0.0 all-gather.8.cloned.1.call-start
  9.4 1.1 pad_maximum_fusion
  10.5 13.4 %all_gather.17 = bf16[256,1792]{1,0:T(8,128)(2,1)S(1)} all-gather(bf16[256,896]{1,0:T(8,128)(2,1)S(1)} %pad_maximum_fusion), channel_id=1, replica_groups=mesh['dp_0'=2,'dp_1'=4,'dp_2'=4,'dp_3'=2,'mp'=2] {'mp'}, dimensions={1}, use_global_device_ids=true | all-gather | bytes 1376256 | tf_op jit(solution)/shard_map/all_gather | solution.py:14
  23.9 0.8 split.9
  24.7 0.0 all-gather.8.cloned.1.call-update
  24.7 100.6 %all-gather.10.cloned.1.call-done = bf16[64,74,1792]{2,1,0:T(8,128)(2,1)} async-done(((bf16[1,74,1792]{2,1,0:T(8,128)(2,1)}), bf16[64,74,1792]{2,1,0:T(8,128)(2,1)}) %all-gather.10.cloned.1.call-update) | async-done | bytes 16973840 | tf_op jit(solution)/shard_map/all_gather | solution.py:68
  125.3 19.3 %reshape.17 = bf16[4736,1792]{1,0:T(8,128)(2,1)} reshape(bf16[64,74,1792]{2,1,0:T(8,128)(2,1)} %all-gather.10.cloned.1.call-done) | data formatting | bytes 33947648
  144.6 92.0 %all-gather.12.cloned.1.call-done = bf16[64,74,1792]{2,1,0:T(8,128)(2,1)} async-done(((bf16[1,74,1792]{2,1,0:T(8,128)(2,1)}), bf16[64,74,1792]{2,1,0:T(8,128)(2,1)}) %all-gather.12.cloned.1.call-update) | async-done | bytes 16973840 | tf_op jit(solution)/shard_map/all_gather | solution.py:64
  236.6 19.3 %reshape.19 = bf16[4736,1792]{1,0:T(8,128)(2,1)} reshape(bf16[64,74,1792]{2,1,0:T(8,128)(2,1)} %all-gather.12.cloned.1.call-done) | data formatting | bytes 33947648
  255.9 92.0 %all-gather.14.cloned.1.call-done = bf16[64,74,1792]{2,1,0:T(8,128)(2,1)} async-done(((bf16[1,74,1792]{2,1,0:T(8,128)(2,1)}), bf16[64,74,1792]{2,1,0:T(8,128)(2,1)}) %all-gather.14.cloned.1.call-update) | async-done | bytes 16973840 | tf_op jit(solution)/shard_map/all_gather | solution.py:64
  347.9 19.4 %reshape.21 = bf16[4736,1792]{1,0:T(8,128)(2,1)} reshape(bf16[64,74,1792]{2,1,0:T(8,128)(2,1)} %all-gather.14.cloned.1.call-done) | data formatting | bytes 33947648
  367.3 12.8 %fusion.5 = f32[128,4736]{1,0:T(8,128)} fusion(bf16[4736,1792]{1,0:T(8,128)(2,1)} %reshape.17, bf16[256,1792]{1,0:T(8,128)(2,1)S(1)} %all_gather.17), kind=kOutput, calls=%fused_computation.11 | convolution fusion | flops 2172649472 | bytes 19857408 | tf_op jit(solution)/shard_map/dot_general | solution.py:57
  380.0 13.2 %fusion.8 = f32[128,4736]{1,0:T(8,128)} fusion(bf16[4736,1792]{1,0:T(8,128)(2,1)} %reshape.21, bf16[256,1792]{1,0:T(8,128)(2,1)S(1)} %all_gather.17), kind=kOutput, calls=%fused_computation.15 | convolution fusion | flops 2172649472 | bytes 19857408 | tf_op jit(solution)/shard_map/dot_general | solution.py:57
  393.3 13.2 %fusion.2 = bf16[128,4736]{1,0:T(8,128)(2,1)S(1)} fusion(f32[128,4736]{1,0:T(8,128)} %fusion.5, bf16[4736,1792]{1,0:T(8,128)(2,1)} %reshape.19, f32[128,4736]{1,0:T(8,128)} %fusion.8, bf16[256,1792]{1,0:T(8,128)(2,1)S(1)} %all_gather.17), kind=kOutput, calls=%fused_computation.3 | convolution fusion | flops 2178711552 | bytes 23494656 | tf_op jit(solution)/shard_map/dot_general | solution.py:57
  406.4 1.5 copy.10
  407.9 0.0 copy-start
  407.9 0.0 copy-start.1
  407.9 8.4 %fusion.11 = f32[128,1792]{1,0:T(8,128)S(1)} fusion(bf16[128,4736]{1,0:T(8,128)(2,1)S(1)} %fusion.2, bf16[4736,1792]{1,0:T(8,128)(2,1)} %reshape.21), kind=kOutput, calls=%fused_computation.18 | convolution fusion | flops 2172649472 | bytes 19103744 | tf_op jit(solution)/shard_map/dot_general | solution.py:79
  416.4 0.0 copy-done
  416.4 0.0 copy-done.1
  416.4 9.6 %fusion.3 = bf16[128,1792]{1,0:T(8,128)(2,1)S(1)} fusion(f32[128,1792]{1,0:T(8,128)S(1)} %fusion.11, bf16[4736,1792]{1,0:T(8,128)(2,1)} %reshape.19, f32[128,4736]{1,0:T(8,128)S(1)} %copy-done, f32[128,4736]{1,0:T(8,128)S(1)} %copy-done.1), kind=kOutput, calls=%fused_computation.7 | convolution fusion | flops 2176745472 | bytes 23199744 | tf_op jit(solution)/shard_map/dot_general | solution.py:80
  426.0 0.8 copy.16
  426.8 0.3 reshape.14
  427.2 0.5 copy.11
  427.7 4.6 all_to_all.15
  432.2 3.5 all-to-all-start
  435.7 2.4 copy.12
  438.1 11.0 %all-to-all-done = bf16[2,128,896]{2,1,0:T(8,128)(2,1)S(1)} async-done(((bf16[2,128,896]{2,1,0:T(8,128)(2,1)}), bf16[2,128,896]{2,1,0:T(8,128)(2,1)S(1)}, u32[]{:S(2)}, u32[]{:S(2)}) %all-to-all-start) | async-done | bytes 458784 | tf_op jit(solution)/shard_map/all_to_all | solution.py:26
  449.0 7.4 %all-to-all-start.2 = ((bf16[32,2,128,74]{2,1,3,0:T(2,128)(2,1)}), bf16[32,2,128,74]{2,1,3,0:T(2,128)(2,1)S(1)}, u32[]{:S(2)}, u32[]{:S(2)}) async-start(bf16[32,2,128,74]{2,1,3,0:T(2,128)(2,1)} %copy.12), calls=%async_computation.2 | async-start | bytes 2424832 | tf_op jit(solution)/shard_map/all_to_all | solution.py:40
  456.4 0.8 reduce_sum.12
  457.2 17.5 %all-to-all-done.2 = bf16[32,2,128,74]{2,1,3,0:T(2,128)(2,1)S(1)} async-done(((bf16[32,2,128,74]{2,1,3,0:T(2,128)(2,1)}), bf16[32,2,128,74]{2,1,3,0:T(2,128)(2,1)S(1)}, u32[]{:S(2)}, u32[]{:S(2)}) %all-to-all-start.2) | async-done | bytes 1212448 | tf_op jit(solution)/shard_map/all_to_all | solution.py:40
  474.7 1.3 copy.13
  476.0 0.7 reshape_reshape.3
  476.8 34.3 %all-gather.8.cloned.1.call-done = bf16[8192,1792]{1,0:T(8,128)(2,1)} async-done(((bf16[128,1792]{1,0:T(8,128)(2,1)}), bf16[8192,1792]{1,0:T(8,128)(2,1)}) %all-gather.8.cloned.1.call-update) | async-done | bytes 29360144 | tf_op jit(solution)/shard_map/all_gather | solution.py:74
  511.1 12.7 %convolution_convert_fusion = bf16[74,1792]{1,0:T(8,128)(2,1)} fusion(bf16[8192,74]{0,1:T(8,128)(2,1)S(1)} %reshape_reshape.3, bf16[8192,1792]{1,0:T(8,128)(2,1)} %all-gather.8.cloned.1.call-done), kind=kOutput, calls=%fused_computation.8 | convolution fusion | flops 2172782080 | bytes 30837760 | tf_op jit(solution)/shard_map/dot_general | solution.py:51
Async XLA Ops:
  7.2 118.1 %all-gather.10.cloned.1.call-start = ((), (), s32[]{:S(2)}) async-start(), calls=%async_computation.4 | async-start | bytes 18636800 | tf_op jit(solution)/shard_map/all_gather | solution.py:68
  7.9 228.7 %all-gather.12.cloned.1.call-start = ((), (), s32[]{:S(2)}) async-start(), calls=%async_computation.5 | async-start | bytes 18636800 | tf_op jit(solution)/shard_map/all_gather | solution.py:64
  8.6 339.2 %all-gather.14.cloned.1.call-start = ((), (), s32[]{:S(2)}) async-start(), calls=%async_computation.6 | async-start | bytes 18636800 | tf_op jit(solution)/shard_map/all_gather | solution.py:64
  9.4 501.7 %all-gather.8.cloned.1.call-start = ((), (), s32[]{:S(2)}) async-start(), calls=%async_computation.3 | async-start | bytes 29818880 | tf_op jit(solution)/shard_map/all_gather | solution.py:74
  407.9 8.4 %copy-start = (f32[128,4736]{1,0:T(8,128)S(1)}, f32[128,4736]{1,0:T(8,128)}, u32[]{:S(2)}) copy-start(f32[128,4736]{1,0:T(8,128)} %fusion.5) | copy-start | bytes 7274500
  407.9 8.4 %copy-start.1 = (f32[128,4736]{1,0:T(8,128)S(1)}, f32[128,4736]{1,0:T(8,128)}, u32[]{:S(2)}) copy-start(f32[128,4736]{1,0:T(8,128)} %fusion.8) | copy-start | bytes 7274500
  432.2 16.8 %all-to-all-start = ((bf16[2,128,896]{2,1,0:T(8,128)(2,1)}), bf16[2,128,896]{2,1,0:T(8,128)(2,1)S(1)}, u32[]{:S(2)}, u32[]{:S(2)}) async-start(bf16[2,128,896]{2,1,0:T(8,128)(2,1)} %bitcast.24), calls=%async_computation | async-start | bytes 917504 | tf_op jit(solution)/shard_map/all_to_all | solution.py:26
  449.0 25.7 %all-to-all-start.2 = ((bf16[32,2,128,74]{2,1,3,0:T(2,128)(2,1)}), bf16[32,2,128,74]{2,1,3,0:T(2,128)(2,1)S(1)}, u32[]{:S(2)}, u32[]{:S(2)}) async-start(bf16[32,2,128,74]{2,1,3,0:T(2,128)(2,1)} %copy.12), calls=%async_computation.2 | async-start | bytes 2424832 | tf_op jit(solution)/shard_map/all_to_all | solution.py:40
Sparse Core Ops, SparseCore 0:
  11.1 114.1 all-gather.9
  128.4 108.1 all-gather.11
  239.7 108.1 all-gather.13
  350.9 160.2 all-gather.7
where the time goes:
time: 532 us; the launch traced here: 530 us
  waiting for transfers between devices  349 us (66%)
  matrix products  69.9 us (13%)
  local copies, waits for them, and re-layouts  66.4 us (12%)
  blocking collectives  17.9 us (3%)
  between operations  13.9 us (3%)
  starting transfers between devices  11 us (2%)
    all_gather x2, waiting for transfers between devices, per_device(): pieces = lax.all_gather((gate_weight, up_weight), DP, axis=0, tiled=True)  184 us
    all_gather x1, waiting for transfers between devices, per_device(): lax.all_gather(down_weight, DP, axis=0, tiled=True)  101 us
    unnamed x7, local copies, waits for them, and re-layouts  58 us
    dot_general x3, matrix products, rdot(): lax.dot_general(left, right, (((1,), (1,)), ((), ())), preferred_element_...  39.2 us
    all_gather x1, waiting for transfers between devices, per_device(): gate_sum = tdot(owned, lax.all_gather(full_in, DP, axis=0, tiled=True))  34.3 us
    all_to_all x1, waiting for transfers between devices, moved_by_axis(): lax.all_to_all(pieces, axes[k], split_axis=k, concat_axis=k, tiled=True)  17.5 us
    all_gather x1, blocking collectives, side_by_side(): filled = lax.all_gather(both, axis, axis=dim, tiled=True)  13.4 us
    dot_general x1, matrix products, tdot(): lax.dot_general(left, right, (((0,), (0,)), ((), ())), preferred_element_...  12.7 us
  transfers between devices with their start and end apart: 6, of which 6 were waited for; matrix products, arithmetic and copies ran while one was open for 24% of the time, Pallas kernels for 0%

commit v1 on v0

v1 whole, which is shorter than its diff:
```python
import itertools

import jax
import jax.numpy as jnp
from jax import lax
from jax.experimental import pallas as pl
from jax.experimental.pallas import tpu as pltpu
from jax.sharding import Mesh
from jax.sharding import PartitionSpec as P

DP = ("dp_0", "dp_1", "dp_2", "dp_3")
MP_DP = ("mp", "dp_0", "dp_1", "dp_2", "dp_3")
X, CORE = "dp_1", "dp_3"
PLANE = ("dp_0", "dp_2", "dp_3", "mp")
SIZES = (2, 4, 2, 2)


F32, BF16 = jnp.float32, jnp.bfloat16
ROWS = 80
VMEM = pl.BlockSpec(memory_space=pltpu.VMEM)
SMEM = pl.BlockSpec(memory_space=pltpu.SMEM)

MOVES = {
    "y+": lambda z, y: (z, (y + 1) % 4),
    "y-": lambda z, y: (z, (y - 1) % 4),
    "y2": lambda z, y: (z, (y + 2) % 4),
    "P": lambda z, y: (z ^ 1, y),
    "Q": lambda z, y: (3 - z, y),
    "PQ": lambda z, y: (z ^ 2, y),
}


def fetch(x, on_core_0, on_core_1, cross=False):
    pairs = []

    def index(zh, y, core, zl):
        return ((zh * SIZES[1] + y) * SIZES[2] + core) * SIZES[3] + zl

    for zh, y, core, zl in itertools.product(*(range(n) for n in SIZES)):
        sender = 1 - core if cross else core
        z_from, y_from = MOVES[on_core_1 if sender else on_core_0](zh * 2 + zl, y)
        pairs.append((index(z_from // 2, y_from, sender, z_from % 2), index(zh, y, core, zl)))
    return lax.ppermute(x, PLANE, pairs)


def shift(x, axis, by):
    n = lax.axis_size(axis)
    return lax.ppermute(x, axis, [(i, (i - by) % n) for i in range(n)])


def rdot(left, right):
    return lax.dot_general(left, right, (((1,), (1,)), ((), ())), preferred_element_type=F32)


def total(*parts):
    out = parts[0].astype(F32)
    for p in parts[1:]:
        out = out + p.astype(F32)
    return out.astype(BF16)


def prepare_body(side_ref, g_ref, u_ref, d_ref, out_ref):
    n, full = g_ref.shape
    half = full // 2
    side = side_ref[0]
    out_ref[...] = jnp.zeros_like(out_ref)
    for s in range(2):

        @pl.when(side == s)
        def _():
            for k, ref in enumerate((g_ref, u_ref, d_ref)):
                for f in range(2):
                    src = (f + s) % 2
                    out_ref[k * ROWS : k * ROWS + n, f * half : (f + 1) * half] = ref[
                        :, src * half : (src + 1) * half
                    ]


def prepare(side, gate_weight, up_weight, down_weight):
    full = gate_weight.shape[1]
    return pl.pallas_call(
        prepare_body,
        out_shape=jax.ShapeDtypeStruct((3 * ROWS, full), BF16),
        in_specs=[SMEM, VMEM, VMEM, VMEM],
        out_specs=VMEM,
        compiler_params=pltpu.CompilerParams(vmem_limit_bytes=8 * 1024 * 1024),
        cost_estimate=pl.CostEstimate(flops=2_000_000, bytes_accessed=1_700_000, transcendentals=0),
        name="prepare",
    )(side.reshape(1), gate_weight, up_weight, down_weight)


def assemble_body(core_ref, m0, m1, m2, m3, r0, r1, r2, r3, x0_ref, x1_ref, c0_ref, c1_ref):
    mine, received = (m0, m1, m2, m3), (r0, r1, r2, r3)
    half = m0.shape[1]
    t = m3.shape[0] // 4
    core = core_ref[0]
    position = {(0, 0): 0, (0, 1): 1, (1, 0): 3, (1, 1): 2}

    for k in range(2):

        @pl.when(core == k)
        def _():
            inputs, cotangent = (mine, received) if k == 0 else (received, mine)
            for g, y, f in itertools.product(range(2), range(4), range(2)):
                block = g * 4 + y if k == 0 else y * 2 + g
                z = position[g, f]
                x_ref, c_ref = ((x0_ref, c0_ref), (x1_ref, c1_ref))[block // 4]
                block = block % 4
                rows, cols = slice(block * t, (block + 1) * t), slice(f * half, (f + 1) * half)
                x_ref[rows, cols] = inputs[z][y * t : (y + 1) * t]
                c_ref[rows, cols] = cotangent[y][z * t : (z + 1) * t]


def assemble(core, mine, received):
    rows, half = mine[3].shape
    shape = jax.ShapeDtypeStruct((rows, 2 * half), BF16)
    return pl.pallas_call(
        assemble_body,
        out_shape=(shape,) * 4,
        in_specs=[SMEM] + [VMEM] * 8,
        out_specs=(VMEM,) * 4,
        compiler_params=pltpu.CompilerParams(vmem_limit_bytes=30 * 1024 * 1024),
        cost_estimate=pl.CostEstimate(flops=4_000_000, bytes_accessed=15_000_000, transcendentals=0),
        name="assemble",
    )(core.reshape(1), *mine, *received)


def per_device(inputs, cotangent, gate_weight, up_weight, down_weight):
    t, half = inputs.shape
    side, core = lax.axis_index("mp"), lax.axis_index(CORE)
    cat = jnp.concatenate
    hold = lax.optimization_barrier

    keep = jnp.where(core == 0, inputs, cotangent)
    give = jnp.where(core == 0, cotangent, inputs)
    first = cat([keep, shift(give, CORE, 1)])
    ring = [first, fetch(first, "y+", "P"), fetch(first, "y-", "Q"), fetch(first, "y2", "PQ")]
    g = hold(cat([v[:t] for v in ring] + [v[t:] for v in ring]))
    a, b = fetch(g, "P", "y+"), fetch(g, "Q", "y-")
    n = 4 * t
    far = fetch(a[:n], "Q", "y+")
    far_received = fetch(b[n:], "P", "y-", cross=True)
    mine = (g, a, b, far)
    received = (shift(g[n:], CORE, 1), shift(a[n:], CORE, 1), shift(b[n:], CORE, 1), far_received)

    own_w = prepare(side, gate_weight, up_weight, down_weight)
    wf, wb = shift(own_w, X, 1), shift(own_w, X, -1)
    wff = cat([shift(wf[:128], X, 1), shift(wb[128:], X, -1)])
    pieces = []
    for w in (own_w, wf, wb, wff):
        pieces += [w, shift(w, CORE, 1)]
    wgu = hold(cat([w[:ROWS] for w in pieces] + [w[ROWS : 2 * ROWS] for w in pieces]))
    wd = hold(cat([w[2 * ROWS :] for w in pieces]))
    ff = wd.shape[0]

    x0, x1, c0, c1 = assemble(core, mine, received)

    def hidden_grads(x, c):
        gate = rdot(wgu[:ff], x)
        up = rdot(wgu[ff:], x)
        dhidden = rdot(wd, c)
        sig = jax.nn.sigmoid(gate)
        act = gate * sig
        dup = (dhidden * act).astype(BF16)
        dgate = (dhidden * up * sig * (1.0 + gate * (1.0 - sig))).astype(BF16)
        return hold((dgate, dup))

    def input_partials(dgate, dup, order):
        gi = hold(
            lax.dot_general(
                cat([dgate, dup]), wgu, (((0,), (0,)), ((), ())), preferred_element_type=F32
            ).astype(BF16)
        )
        on_0 = (gi[:, :half], gi[:, half:])
        on_1 = []
        for k in order:
            v = gi[2 * k * t : 2 * (k + 1) * t]
            on_1.append(cat([v[:t, :half], v[:t, half:], v[t:, half:], v[t:, :half]]))
        return hold(tuple(jnp.where(core == 0, u, v) for u, v in zip(on_0, on_1)))

    dg1, du1 = hidden_grads(x1, c1)
    far_part, back_part = input_partials(dg1, du1, (1, 0))
    got_far = fetch(far_part, "PQ", "y2")
    got_back = fetch(back_part, "Q", "y+")
    x0, c0, far_part, back_part = hold((x0, c0, far_part, back_part))
    dg0, du0 = hidden_grads(x0, c0)
    own_part, fwd_part = input_partials(dg0, du0, (0, 1))
    got_fwd = fetch(fwd_part, "P", "y-")

    gg = hold(
        (
            jnp.dot(dg0, x0, preferred_element_type=F32)
            + jnp.dot(dg1, x1, preferred_element_type=F32)
        ).astype(BF16)
    )
    r = ROWS
    own = cat([gg[2 * k * r : (2 * k + 1) * r] for k in range(4)])
    theirs = cat([gg[(2 * k + 1) * r : (2 * k + 2) * r] for k in range(4)])
    theirs = shift(theirs, CORE, 1)
    cg = hold(total(own, theirs))
    gw = total(
        cg[:r],
        shift(cg[r : 2 * r], X, -1),
        shift(cg[2 * r : 3 * r], X, 1),
        shift(cg[3 * r :], X, 2),
    )

    s = total(own_part, got_fwd, got_back, got_far)
    s = hold(tuple(s[k * t : (k + 1) * t] for k in range(4)))
    input_grad = total(
        s[0], fetch(s[1], "y-", "P"), fetch(s[2], "y+", "Q"), fetch(s[3], "y2", "PQ")
    )

    gw = gw[: gate_weight.shape[0]]
    gate_grad = jnp.where(side == 0, gw, cat([gw[:, half:], gw[:, :half]], axis=1))
    return input_grad, gate_grad


def solution(mesh):
    torus = Mesh(
        mesh.devices.reshape(2, 4, 4, 2, mesh.shape["mp"]), ("dp_0", "dp_1", "dp_2", "dp_3", "mp")
    )

    return jax.shard_map(
        per_device,
        mesh=torus,
        in_specs=(P(DP, "mp"), P(DP, "mp"), P(MP_DP, None), P(MP_DP, None), P(MP_DP, None)),
        out_specs=(P(DP, "mp"), P(MP_DP, None)),
        check_vma=False,
    )
```

time: 532 us -> 127 us (0.24)
  waiting for transfers between devices: 349 us -> 47.2 us
  local copies, waits for them, and re-layouts: 66.4 us -> 5.27 us
  matrix products: 69.9 us -> 17.1 us
  starting transfers between devices: 11 us -> 48.6 us
  blocking collectives: 17.9 us -> 0 us
  between operations: 13.9 us -> 1.11 us
    all_gather x4 -> x0, waiting for transfers between devices: 319 us -> none  [the longest x2 184 us: per_device(): pieces = lax.all_gather((gate_weight, up_weight), DP, axis=0, tiled=True)]
    unnamed x7 -> x30, local copies, waits for them, and re-layouts: 58 us -> 4.19 us
    ppermute x0 -> x29, starting transfers between devices: none -> 48.6 us  [the longest x16 26.7 us: shift(): return lax.ppermute(x, axis, [(i, (i - by) % n) for i in range(n)])]
    ppermute x0 -> x29, waiting for transfers between devices: none -> 47.2 us  [the longest x13 35.8 us: fetch(): return lax.ppermute(x, PLANE, pairs)]
    dot_general x3 -> x6, matrix products: 39.2 us -> 9.07 us  [rdot(): lax.dot_general(left, right, (((1,), (1,)), ((), ())), preferred_element_...]
    all_to_all x2 -> x0, waiting for transfers between devices: 28.4 us -> none  [the longest x1 17.5 us: moved_by_axis(): lax.all_to_all(pieces, axes[k], split_axis=k, concat_axis=k, tiled=True)]
    dot_general x3 -> x4, matrix products: 30.7 us -> 8 us  [the longest x2 5.3 us: input_partials(): lax.dot_general(cat([dgate, dup]), wgu, (((0,), (0,)), ((), ())), preferr...]
    all_gather x1 -> x0, blocking collectives: 13.4 us -> none  [side_by_side(): filled = lax.all_gather(both, axis, axis=dim, tiled=True)]
  transfers between devices with their start and end apart: 6 -> 29, of which waited for: 6 -> 12; matrix products, arithmetic and copies ran while one was open for 24% -> 12% of each run, Pallas kernels for 0% -> 0%
where the time goes in v1:
time: 127 us; the launch traced here: 126 us
  starting transfers between devices  48.6 us (38%)
  waiting for transfers between devices  47.2 us (37%)
  matrix products  17.1 us (13%)
  other arithmetic  5.79 us (5%)
  local copies, waits for them, and re-layouts  5.27 us (4%)
    ppermute x13, waiting for transfers between devices, fetch(): return lax.ppermute(x, PLANE, pairs)  35.8 us
    ppermute x16, starting transfers between devices, shift(): return lax.ppermute(x, axis, [(i, (i - by) % n) for i in range(n)])  26.7 us
    ppermute x13, starting transfers between devices, fetch(): return lax.ppermute(x, PLANE, pairs)  21.9 us
    ppermute x16, waiting for transfers between devices, shift(): return lax.ppermute(x, axis, [(i, (i - by) % n) for i in range(n)])  11.5 us
    dot_general x6, matrix products, rdot(): lax.dot_general(left, right, (((1,), (1,)), ((), ())), preferred_element_...  9.07 us
    dot_general x2, matrix products, input_partials(): lax.dot_general(cat([dgate, dup]), wgu, (((0,), (0,)), ((), ())), preferr...  5.3 us
    unnamed x30, local copies, waits for them, and re-layouts  4.19 us
    convert_element_type x4, other arithmetic, total(): return out.astype(BF16)  2.89 us
  transfers between devices with their start and end apart: 29, of which 12 were waited for; matrix products, arithmetic and copies ran while one was open for 12% of the time, Pallas kernels for 0%

profile of v1, /device:TPU:1, one launch (start us, length us, event | category | flops | bytes accessed | tf_op | source)
XLA Modules:
  0.0 125.9 jit_solution(10115461285708908790)
XLA Ops:
  0.6 1.1 constant_dynamic-update-slice_fusion.3
  1.8 1.5 %collective-permute-start.8 = (bf16[128,896]{1,0:T(8,128)(2,1)S(1)}, bf16[128,896]{1,0:T(8,128)(2,1)S(1)}, u32[]{:S(2)}, u32[]{:S(2)}) collective-permute-start(bf16[128,896]{1,0:T(8,128)(2,1)S(1)} %get-tuple-element.87), channel_id=1, source_target_pairs={{0,2},{2,0},{1,3},{3,1},{4,6},{6,4},{5,7},{7,5},{8,10},{10,8},{9,1... | collective-permute-start | bytes 688136 | tf_op jit(solution)/shard_map/ppermute | solution.py:48
  3.2 1.0 copy-done
  4.2 1.0 copy-done.1
  5.2 1.0 copy-done.2
  6.1 0.1 prepare.1
  6.2 0.1 collective-permute-start
  6.3 2.7 %collective-permute-start.1 = (bf16[240,1792]{1,0:T(8,128)(2,1)S(1)}, bf16[240,1792]{1,0:T(8,128)(2,1)S(1)}, u32[]{:S(2)}, u32[]{:S(2)}) collective-permute-start(bf16[240,1792]{1,0:T(8,128)(2,1)S(1)} %prepare.1), channel_id=1, source_target_pairs={{0,48},{16,0},{32,16},{48,32},{1,49},{17,1},{33,17},{49,33},{2,50}... | collective-permute-start | bytes 2580488 | tf_op jit(solution)/shard_map/ppermute | solution.py:48
  9.0 1.7 %collective-permute-start.9 = (bf16[256,896]{1,0:T(8,128)(2,1)S(1)}, bf16[256,896]{1,0:T(8,128)(2,1)S(1)}, u32[]{:S(2)}, u32[]{:S(2)}) collective-permute-start(bf16[256,896]{1,0:T(8,128)(2,1)S(1)} %pad_maximum_fusion.1), channel_id=1, source_target_pairs={{4,0},{5,1},{3,2},{2,3},{8,4},{9,5},{7,6},{6,7},{12,8},{13,9},{11,... | collective-permute-start | bytes 1376264 | tf_op jit(solution)/shard_map/ppermute | solution.py:43
  10.7 2.2 %collective-permute-start.10 = (bf16[256,896]{1,0:T(8,128)(2,1)S(1)}, bf16[256,896]{1,0:T(8,128)(2,1)S(1)}, u32[]{:S(2)}, u32[]{:S(2)}) collective-permute-start(bf16[256,896]{1,0:T(8,128)(2,1)S(1)} %pad_maximum_fusion.1), channel_id=1, source_target_pairs={{12,0},{13,1},{67,2},{66,3},{0,4},{1,5},{71,6},{70,7},{4,8},{5,9},... | collective-permute-start | bytes 1376264 | tf_op jit(solution)/shard_map/ppermute | solution.py:43
  13.0 3.9 %collective-permute-done.9 = bf16[256,896]{1,0:T(8,128)(2,1)S(1)} collective-permute-done((bf16[256,896]{1,0:T(8,128)(2,1)S(1)}, bf16[256,896]{1,0:T(8,128)(2,1)S(1)}, u32[]{:S(2)}, u32[]{:S(2)}) %collective-permute-start.9) | collective-permute-done | bytes 458784 | tf_op jit(solution)/shard_map/ppermute | solution.py:43
  16.9 3.4 %collective-permute-start.11 = (bf16[256,896]{1,0:T(8,128)(2,1)S(1)}, bf16[256,896]{1,0:T(8,128)(2,1)S(1)}, u32[]{:S(2)}, u32[]{:S(2)}) collective-permute-start(bf16[256,896]{1,0:T(8,128)(2,1)S(1)} %pad_maximum_fusion.1), channel_id=1, source_target_pairs={{8,0},{9,1},{66,2},{67,3},{12,4},{13,5},{70,6},{71,7},{0,8},{1,9},... | collective-permute-start | bytes 1376264 | tf_op jit(solution)/shard_map/ppermute | solution.py:43
  20.4 6.1 %collective-permute-done.11 = bf16[256,896]{1,0:T(8,128)(2,1)S(1)} collective-permute-done((bf16[256,896]{1,0:T(8,128)(2,1)S(1)}, bf16[256,896]{1,0:T(8,128)(2,1)S(1)}, u32[]{:S(2)}, u32[]{:S(2)}) %collective-permute-start.11) | collective-permute-done | bytes 458784 | tf_op jit(solution)/shard_map/ppermute | solution.py:43
  26.7 2.8 %collective-permute-start.12 = (bf16[1024,896]{1,0:T(8,128)(2,1)S(1)}, bf16[1024,896]{1,0:T(8,128)(2,1)S(1)}, u32[]{:S(2)}, u32[]{:S(2)}) collective-permute-start(bf16[1024,896]{1,0:T(8,128)(2,1)S(1)} %slice_dynamic-update-slice_fusion.24.m0), channel_id=1, source_target_pairs={{1,0},{0,1},{6,2},{7,3},{5,4},{4,5},{10,6},{11,7},{9,8},{8,9},{14,... | collective-permute-start | bytes 5505032 | tf_op jit(solution)/shard_map/ppermute | solution.py:43
  29.6 2.7 %collective-permute-start.6 = (bf16[128,1792]{1,0:T(8,128)(2,1)S(1)}, bf16[128,1792]{1,0:T(8,128)(2,1)S(1)}, u32[]{:S(2)}, u32[]{:S(2)}) collective-permute-start(bf16[128,1792]{1,0:T(8,128)(2,1)S(1)} %slice.333), channel_id=1, source_target_pairs={{0,48},{16,0},{32,16},{48,32},{1,49},{17,1},{33,17},{49,33},{2,50}... | collective-permute-start | bytes 1376264 | tf_op jit(solution)/shard_map/ppermute | solution.py:48
  32.5 4.7 %collective-permute-start.2 = (bf16[240,1792]{1,0:T(8,128)(2,1)S(1)}, bf16[240,1792]{1,0:T(8,128)(2,1)S(1)}, u32[]{:S(2)}, u32[]{:S(2)}) collective-permute-start(bf16[240,1792]{1,0:T(8,128)(2,1)S(1)} %collective-permute-done.1), channel_id=1, source_target_pairs={{0,2},{2,0},{1,3},{3,1},{4,6},{6,4},{5,7},{7,5},{8,10},{10,8},{9,1... | collective-permute-start | bytes 2580488 | tf_op jit(solution)/shard_map/ppermute | solution.py:48
  37.2 0.6 collective-permute-done.6
  37.8 5.3 %collective-permute-start.15 = (bf16[512,896]{1,0:T(8,128)(2,1)S(1)}, bf16[512,896]{1,0:T(8,128)(2,1)S(1)}, u32[]{:S(2)}, u32[]{:S(2)}) collective-permute-start(bf16[512,896]{1,0:T(8,128)(2,1)S(1)} %slice.342), channel_id=1, source_target_pairs={{0,2},{2,0},{1,3},{3,1},{4,6},{6,4},{5,7},{7,5},{8,10},{10,8},{9,1... | collective-permute-start | bytes 2752520 | tf_op jit(solution)/shard_map/ppermute | solution.py:48
  43.1 3.0 %collective-permute-start.4 = (bf16[240,1792]{1,0:T(8,128)(2,1)S(1)}, bf16[240,1792]{1,0:T(8,128)(2,1)S(1)}, u32[]{:S(2)}, u32[]{:S(2)}) collective-permute-start(bf16[240,1792]{1,0:T(8,128)(2,1)S(1)} %collective-permute-done.3), channel_id=1, source_target_pairs={{0,2},{2,0},{1,3},{3,1},{4,6},{6,4},{5,7},{7,5},{8,10},{10,8},{9,1... | collective-permute-start | bytes 2580488 | tf_op jit(solution)/shard_map/ppermute | solution.py:48
  46.1 0.1 collective-permute-start.7
  46.3 1.8 %collective-permute-done.4 = bf16[240,1792]{1,0:T(8,128)(2,1)S(1)} collective-permute-done((bf16[240,1792]{1,0:T(8,128)(2,1)S(1)}, bf16[240,1792]{1,0:T(8,128)(2,1)S(1)}, u32[]{:S(2)}, u32[]{:S(2)}) %collective-permute-start.4) | collective-permute-done | bytes 860192 | tf_op jit(solution)/shard_map/ppermute | solution.py:48
  48.2 1.2 collective-permute-done.7
  49.7 3.4 %collective-permute-done.13.m2 = bf16[1024,896]{1,0:T(8,128)(2,1)S(1)} collective-permute-done((bf16[1024,896]{1,0:T(8,128)(2,1)S(1)}, bf16[1024,896]{1,0:T(8,128)(2,1)S(1)}, u32[]{:S(2)}, u32[]{:S(2)}) %collective-permute-start.13) | collective-permute-done | bytes 1835040 | tf_op jit(solution)/shard_map/ppermute | solution.py:43
  53.1 2.4 %collective-permute-start.17 = (bf16[512,896]{1,0:T(8,128)(2,1)S(1)}, bf16[512,896]{1,0:T(8,128)(2,1)S(1)}, u32[]{:S(2)}, u32[]{:S(2)}) collective-permute-start(bf16[512,896]{1,0:T(8,128)(2,1)S(1)} %slice.344), channel_id=1, source_target_pairs={{0,2},{2,0},{1,3},{3,1},{4,6},{6,4},{5,7},{7,5},{8,10},{10,8},{9,1... | collective-permute-start | bytes 2752520 | tf_op jit(solution)/shard_map/ppermute | solution.py:48
  55.6 0.9 collective-permute-start.18
  56.4 0.1 fusion.45
  56.6 3.2 %collective-permute-start.14 = (bf16[512,896]{1,0:T(8,128)(2,1)S(1)}, bf16[512,896]{1,0:T(8,128)(2,1)S(1)}, u32[]{:S(2)}, u32[]{:S(2)}) collective-permute-start(bf16[512,896]{1,0:T(8,128)(2,1)S(1)} %get-tuple-element.65), channel_id=1, source_target_pairs={{65,0},{64,1},{6,2},{7,3},{69,4},{68,5},{10,6},{11,7},{73,8},{72,9... | collective-permute-start | bytes 2752520 | tf_op jit(solution)/shard_map/ppermute | solution.py:43
  59.9 10.2 %collective-permute-done.14.m3 = bf16[512,896]{1,0:T(8,128)(2,1)S(1)} collective-permute-done((bf16[512,896]{1,0:T(8,128)(2,1)S(1)}, bf16[512,896]{1,0:T(8,128)(2,1)S(1)}, u32[]{:S(2)}, u32[]{:S(2)}) %collective-permute-start.14) | collective-permute-done | bytes 917536 | tf_op jit(solution)/shard_map/ppermute | solution.py:43
  70.2 0.7 assemble.1
  70.9 1.4 %fusion.2 = f32[640,512]{1,0:T(8,128)S(1)} fusion(bf16[512,1792]{1,0:T(8,128)(2,1)S(1)} %get-tuple-element.23, bf16[1280,1792]{1,0:T(8,128)(2,1)S(1)} %get-tuple-element.74), kind=kOutput, calls=%fused_computation.6 | convolution fusion | flops 1174405120 | bytes 5439488 | tf_op jit(solution)/shard_map/dot_general | solution.py:52
  72.3 1.5 %multiply_convert_fusion.1 = (bf16[640,512]{1,0:T(8,128)(2,1)S(1)}, f32[640,512]{1,0:T(8,128)S(1)}) fusion(f32[640,512]{1,0:T(8,128)S(1)} %fusion.2, bf16[640,1792]{1,0:T(8,128)(2,1)S(1)} %get-tuple-element.73, bf16[512,1792]{1,0:T(8,128)(2,1)S(1)} %get-tuple-element.22), kind=kOutput, calls=%fused_computation.29 | convolution fusion | flops 1176371200 | bytes 7405568 | tf_op jit(solution)/shard_map/dot_general | solution.py:52
  73.8 1.7 %fusion.26 = bf16[640,512]{1,0:T(8,128)(2,1)S(1)} fusion(f32[640,512]{1,0:T(8,128)S(1)} %get-tuple-element.91, bf16[512,1792]{1,0:T(8,128)(2,1)S(1)} %get-tuple-element.23, bf16[1280,1792]{1,0:T(8,128)(2,1)S(1)} %get-tuple-element.74, f32[640,512]{1,0:T(8,128)S(1)} %fusion.2), kind=kOutput, calls=%fused_computation.19 | convolution fusion | flops 1177681920 | bytes 7405568 | tf_op jit(solution)/shard_map/dot_general | solution.py:52
  75.5 2.6 %convolution_convert_fusion.1 = bf16[512,1792]{1,0:T(8,128)(2,1)S(1)} fusion(bf16[1280,1792]{1,0:T(8,128)(2,1)S(1)} %get-tuple-element.74, bf16[640,512]{1,0:T(8,128)(2,1)S(1)} %get-tuple-element.25, bf16[640,512]{1,0:T(8,128)(2,1)S(1)} %fusion.26), kind=kOutput, calls=%fused_computation.2 | convolution fusion | flops 2352349184 | bytes 7733248 | tf_op jit(solution)/shard_map/dot_general | solution.py:170
  78.1 0.1 fusion.43
  78.3 0.4 slice_select_fusion.2
  78.7 3.1 %collective-permute-start.21 = (bf16[512,896]{1,0:T(8,128)(2,1)S(1)}, bf16[512,896]{1,0:T(8,128)(2,1)S(1)}, u32[]{:S(2)}, u32[]{:S(2)}) collective-permute-start(bf16[512,896]{1,0:T(8,128)(2,1)S(1)} %get-tuple-element.26), channel_id=1, source_target_pairs={{64,0},{65,1},{10,2},{11,3},{68,4},{69,5},{14,6},{15,7},{72,8},{73... | collective-permute-start | bytes 2752520 | tf_op jit(solution)/shard_map/ppermute | solution.py:43
  81.9 0.7 collective-permute-start.20
  82.5 1.4 %fusion = f32[640,512]{1,0:T(8,128)S(1)} fusion(bf16[512,1792]{1,0:T(8,128)(2,1)S(1)} %get-tuple-element.29, bf16[1280,1792]{1,0:T(8,128)(2,1)S(1)} %get-tuple-element.74), kind=kOutput, calls=%fused_computation.4 | convolution fusion | flops 1174405120 | bytes 5439488 | tf_op jit(solution)/shard_map/dot_general | solution.py:52
  83.9 1.5 %multiply_convert_fusion = (bf16[640,512]{1,0:T(8,128)(2,1)S(1)}, f32[640,512]{1,0:T(8,128)S(1)}) fusion(f32[640,512]{1,0:T(8,128)S(1)} %fusion, bf16[640,1792]{1,0:T(8,128)(2,1)S(1)} %get-tuple-element.73, bf16[512,1792]{1,0:T(8,128)(2,1)S(1)} %get-tuple-element.28), kind=kOutput, calls=%fused_computation.27 | convolution fusion | flops 1176371200 | bytes 7405568 | tf_op jit(solution)/shard_map/dot_general | solution.py:52
  85.4 1.7 %fusion.29 = bf16[640,512]{1,0:T(8,128)(2,1)S(1)} fusion(f32[640,512]{1,0:T(8,128)S(1)} %get-tuple-element.93, bf16[512,1792]{1,0:T(8,128)(2,1)S(1)} %get-tuple-element.29, bf16[1280,1792]{1,0:T(8,128)(2,1)S(1)} %get-tuple-element.74, f32[640,512]{1,0:T(8,128)S(1)} %fusion), kind=kOutput, calls=%fused_computation.20 | convolution fusion | flops 1177681920 | bytes 7405568 | tf_op jit(solution)/shard_map/dot_general | solution.py:52
  87.1 2.7 %convolution_convert_fusion = bf16[512,1792]{1,0:T(8,128)(2,1)S(1)} fusion(bf16[1280,1792]{1,0:T(8,128)(2,1)S(1)} %get-tuple-element.74, bf16[640,512]{1,0:T(8,128)(2,1)S(1)} %get-tuple-element.31, bf16[640,512]{1,0:T(8,128)(2,1)S(1)} %fusion.29), kind=kOutput, calls=%fused_computation.1 | convolution fusion | flops 2352349184 | bytes 7733248 | tf_op jit(solution)/shard_map/dot_general | solution.py:170
  89.7 0.1 fusion.41
  89.9 1.4 %fusion.49 = f32[640,1792]{1,0:T(8,128)S(1)} fusion(bf16[640,512]{1,0:T(8,128)(2,1)S(1)} %fusion.29, bf16[512,1792]{1,0:T(8,128)(2,1)S(1)} %get-tuple-element.29), kind=kOutput, calls=%fused_computation.87 | convolution fusion | flops 1174405120 | bytes 7077888 | tf_op jit(solution)/shard_map/dot_general | solution.py:192
  91.3 0.4 slice_select_fusion
  91.7 0.9 collective-permute-start.19
  92.6 1.4 %add_convert_fusion = bf16[640,1792]{1,0:T(8,128)(2,1)S(1)} fusion(f32[640,1792]{1,0:T(8,128)S(1)} %fusion.49, bf16[640,512]{1,0:T(8,128)(2,1)S(1)} %fusion.26, bf16[512,1792]{1,0:T(8,128)(2,1)S(1)} %get-tuple-element.23), kind=kOutput, calls=%fused_computation | convolution fusion | flops 1176698880 | bytes 9371648 | tf_op jit(solution)/shard_map/dot_general | solution.py:193
  93.9 0.2 fusion.40
  94.2 0.1 collective-permute-start.25
  94.3 9.5 %collective-permute-done.20 = bf16[512,896]{1,0:T(8,128)(2,1)S(1)} collective-permute-done((bf16[512,896]{1,0:T(8,128)(2,1)S(1)}, bf16[512,896]{1,0:T(8,128)(2,1)S(1)}, u32[]{:S(2)}, u32[]{:S(2)}) %collective-permute-start.20) | collective-permute-done | bytes 917536 | tf_op jit(solution)/shard_map/ppermute | solution.py:43
  103.8 1.5 %collective-permute-done.19 = bf16[512,896]{1,0:T(8,128)(2,1)S(1)} collective-permute-done((bf16[512,896]{1,0:T(8,128)(2,1)S(1)}, bf16[512,896]{1,0:T(8,128)(2,1)S(1)}, u32[]{:S(2)}, u32[]{:S(2)}) %collective-permute-start.19) | collective-permute-done | bytes 917536 | tf_op jit(solution)/shard_map/ppermute | solution.py:43
  105.2 0.5 add_convert_fusion.2
  105.8 2.1 %collective-permute-start.24 = (bf16[128,896]{1,0:T(8,128)(2,1)S(1)}, bf16[128,896]{1,0:T(8,128)(2,1)S(1)}, u32[]{:S(2)}, u32[]{:S(2)}) collective-permute-start(bf16[128,896]{1,0:T(8,128)(2,1)S(1)} %get-tuple-element.37), channel_id=1, source_target_pairs={{8,0},{9,1},{66,2},{67,3},{12,4},{13,5},{70,6},{71,7},{0,8},{1,9},... | collective-permute-start | bytes 688136 | tf_op jit(solution)/shard_map/ppermute | solution.py:43
  107.9 0.4 collective-permute-start.23
  108.3 0.4 collective-permute-start.22
  108.7 0.3 add_convert_fusion.1
  109.1 2.4 %collective-permute-start.28 = (bf16[80,1792]{1,0:T(8,128)(2,1)S(1)}, bf16[80,1792]{1,0:T(8,128)(2,1)S(1)}, u32[]{:S(2)}, u32[]{:S(2)}) collective-permute-start(bf16[80,1792]{1,0:T(8,128)(2,1)S(1)} %get-tuple-element.67), channel_id=1, source_target_pairs={{0,32},{16,48},{32,0},{48,16},{1,33},{17,49},{33,1},{49,17},{2,34}... | collective-permute-start | bytes 860168 | tf_op jit(solution)/shard_map/ppermute | solution.py:48
  111.4 1.0 collective-permute-start.27
  112.6 0.7 copy-done.3
  113.2 0.8 collective-permute-start.26
  114.0 1.1 collective-permute-done.23
  115.1 2.0 %add_convert_fusion.4 = bf16[128,896]{1,0:T(8,128)(2,1)} fusion(bf16[128,896]{1,0:T(8,128)(2,1)} %copy-done.3, bf16[128,896]{1,0:T(8,128)(2,1)} %collective-permute-done.23, bf16[128,896]{1,0:T(8,128)(2,1)} %collective-permute-done.22, bf16[128,896]{1,0:T(8,128)(2,1)S(1)} %get-tuple-element.34), kind=kLoop, calls=%fused_computation.38 | loop fusion | flops 917504 | bytes 1146880 | tf_op jit(solution)/shard_map/convert_element_type | solution.py:59
  117.1 7.9 %collective-permute-done.27 = bf16[80,1792]{1,0:T(8,128)(2,1)S(1)} collective-permute-done((bf16[80,1792]{1,0:T(8,128)(2,1)S(1)}, bf16[80,1792]{1,0:T(8,128)(2,1)S(1)}, u32[]{:S(2)}, u32[]{:S(2)}) %collective-permute-start.27) | collective-permute-done | bytes 286752 | tf_op jit(solution)/shard_map/ppermute | solution.py:48
  125.0 0.1 add_convert_fusion.3
  125.1 0.8 slice_select_fusion.4
  (62 shorter events, 1.6 us)
Async XLA Ops:
  1.8 7.2 %collective-permute-start.8 = (bf16[128,896]{1,0:T(8,128)(2,1)S(1)}, bf16[128,896]{1,0:T(8,128)(2,1)S(1)}, u32[]{:S(2)}, u32[]{:S(2)}) collective-permute-start(bf16[128,896]{1,0:T(8,128)(2,1)S(1)} %get-tuple-element.87), channel_id=1, source_target_pairs={{0,2},{2,0},{1,3},{3,1},{4,6},{6,4},{5,7},{7,5},{8,10},{10,8},{9,1... | collective-permute-start | bytes 688136 | tf_op jit(solution)/shard_map/ppermute | solution.py:48
  3.2 1.0 copy-start
  4.2 1.0 copy-start.1
  5.2 1.0 copy-start.2
  6.2 26.2 %collective-permute-start = (bf16[240,1792]{1,0:T(8,128)(2,1)S(1)}, bf16[240,1792]{1,0:T(8,128)(2,1)S(1)}, u32[]{:S(2)}, u32[]{:S(2)}) collective-permute-start(bf16[240,1792]{1,0:T(8,128)(2,1)S(1)} %prepare.1), channel_id=1, source_target_pairs={{0,2},{2,0},{1,3},{3,1},{4,6},{6,4},{5,7},{7,5},{8,10},{10,8},{9,1... | collective-permute-start | bytes 2580488 | tf_op jit(solution)/shard_map/ppermute | solution.py:48
  6.3 23.2 %collective-permute-start.1 = (bf16[240,1792]{1,0:T(8,128)(2,1)S(1)}, bf16[240,1792]{1,0:T(8,128)(2,1)S(1)}, u32[]{:S(2)}, u32[]{:S(2)}) collective-permute-start(bf16[240,1792]{1,0:T(8,128)(2,1)S(1)} %prepare.1), channel_id=1, source_target_pairs={{0,48},{16,0},{32,16},{48,32},{1,49},{17,1},{33,17},{49,33},{2,50}... | collective-permute-start | bytes 2580488 | tf_op jit(solution)/shard_map/ppermute | solution.py:48
  9.0 23.3 %collective-permute-start.3 = (bf16[240,1792]{1,0:T(8,128)(2,1)S(1)}, bf16[240,1792]{1,0:T(8,128)(2,1)S(1)}, u32[]{:S(2)}, u32[]{:S(2)}) collective-permute-start(bf16[240,1792]{1,0:T(8,128)(2,1)S(1)} %prepare.1), channel_id=1, source_target_pairs={{0,16},{16,32},{32,48},{48,0},{1,17},{17,33},{33,49},{49,1},{2,18}... | collective-permute-start | bytes 2580488 | tf_op jit(solution)/shard_map/ppermute | solution.py:48
  9.0 7.9 %collective-permute-start.9 = (bf16[256,896]{1,0:T(8,128)(2,1)S(1)}, bf16[256,896]{1,0:T(8,128)(2,1)S(1)}, u32[]{:S(2)}, u32[]{:S(2)}) collective-permute-start(bf16[256,896]{1,0:T(8,128)(2,1)S(1)} %pad_maximum_fusion.1), channel_id=1, source_target_pairs={{4,0},{5,1},{3,2},{2,3},{8,4},{9,5},{7,6},{6,7},{12,8},{13,9},{11,... | collective-permute-start | bytes 1376264 | tf_op jit(solution)/shard_map/ppermute | solution.py:43
  10.7 9.6 %collective-permute-start.10 = (bf16[256,896]{1,0:T(8,128)(2,1)S(1)}, bf16[256,896]{1,0:T(8,128)(2,1)S(1)}, u32[]{:S(2)}, u32[]{:S(2)}) collective-permute-start(bf16[256,896]{1,0:T(8,128)(2,1)S(1)} %pad_maximum_fusion.1), channel_id=1, source_target_pairs={{12,0},{13,1},{67,2},{66,3},{0,4},{1,5},{71,6},{70,7},{4,8},{5,9},... | collective-permute-start | bytes 1376264 | tf_op jit(solution)/shard_map/ppermute | solution.py:43
  16.9 9.6 %collective-permute-start.11 = (bf16[256,896]{1,0:T(8,128)(2,1)S(1)}, bf16[256,896]{1,0:T(8,128)(2,1)S(1)}, u32[]{:S(2)}, u32[]{:S(2)}) collective-permute-start(bf16[256,896]{1,0:T(8,128)(2,1)S(1)} %pad_maximum_fusion.1), channel_id=1, source_target_pairs={{8,0},{9,1},{66,2},{67,3},{12,4},{13,5},{70,6},{71,7},{0,8},{1,9},... | collective-permute-start | bytes 1376264 | tf_op jit(solution)/shard_map/ppermute | solution.py:43
  26.7 29.8 %collective-permute-start.12 = (bf16[1024,896]{1,0:T(8,128)(2,1)S(1)}, bf16[1024,896]{1,0:T(8,128)(2,1)S(1)}, u32[]{:S(2)}, u32[]{:S(2)}) collective-permute-start(bf16[1024,896]{1,0:T(8,128)(2,1)S(1)} %slice_dynamic-update-slice_fusion.24.m0), channel_id=1, source_target_pairs={{1,0},{0,1},{6,2},{7,3},{5,4},{4,5},{10,6},{11,7},{9,8},{8,9},{14,... | collective-permute-start | bytes 5505032 | tf_op jit(solution)/shard_map/ppermute | solution.py:43
  29.5 23.6 %collective-permute-start.13 = (bf16[1024,896]{1,0:T(8,128)(2,1)S(1)}, bf16[1024,896]{1,0:T(8,128)(2,1)S(1)}, u32[]{:S(2)}, u32[]{:S(2)}) collective-permute-start(bf16[1024,896]{1,0:T(8,128)(2,1)S(1)} %slice_dynamic-update-slice_fusion.24.m0), channel_id=1, source_target_pairs={{65,0},{64,1},{14,2},{15,3},{69,4},{68,5},{2,6},{3,7},{73,8},{72,9... | collective-permute-start | bytes 5505032 | tf_op jit(solution)/shard_map/ppermute | solution.py:43
  29.6 8.2 %collective-permute-start.6 = (bf16[128,1792]{1,0:T(8,128)(2,1)S(1)}, bf16[128,1792]{1,0:T(8,128)(2,1)S(1)}, u32[]{:S(2)}, u32[]{:S(2)}) collective-permute-start(bf16[128,1792]{1,0:T(8,128)(2,1)S(1)} %slice.333), channel_id=1, source_target_pairs={{0,48},{16,0},{32,16},{48,32},{1,49},{17,1},{33,17},{49,33},{2,50}... | collective-permute-start | bytes 1376264 | tf_op jit(solution)/shard_map/ppermute | solution.py:48
  32.4 10.7 %collective-permute-start.5 = (bf16[112,1792]{1,0:T(8,128)(2,1)S(1)}, bf16[112,1792]{1,0:T(8,128)(2,1)S(1)}, u32[]{:S(2)}, u32[]{:S(2)}) collective-permute-start(bf16[112,1792]{1,0:T(8,128)(2,1)S(1)} %slice.331), channel_id=1, source_target_pairs={{0,16},{16,32},{32,48},{48,0},{1,17},{17,33},{33,49},{49,1},{2,18}... | collective-permute-start | bytes 1204232 | tf_op jit(solution)/shard_map/ppermute | solution.py:48
  32.5 13.7 %collective-permute-start.2 = (bf16[240,1792]{1,0:T(8,128)(2,1)S(1)}, bf16[240,1792]{1,0:T(8,128)(2,1)S(1)}, u32[]{:S(2)}, u32[]{:S(2)}) collective-permute-start(bf16[240,1792]{1,0:T(8,128)(2,1)S(1)} %collective-permute-done.1), channel_id=1, source_target_pairs={{0,2},{2,0},{1,3},{3,1},{4,6},{6,4},{5,7},{7,5},{8,10},{10,8},{9,1... | collective-permute-start | bytes 2580488 | tf_op jit(solution)/shard_map/ppermute | solution.py:48
  37.8 22.2 %collective-permute-start.15 = (bf16[512,896]{1,0:T(8,128)(2,1)S(1)}, bf16[512,896]{1,0:T(8,128)(2,1)S(1)}, u32[]{:S(2)}, u32[]{:S(2)}) collective-permute-start(bf16[512,896]{1,0:T(8,128)(2,1)S(1)} %slice.342), channel_id=1, source_target_pairs={{0,2},{2,0},{1,3},{3,1},{4,6},{6,4},{5,7},{7,5},{8,10},{10,8},{9,1... | collective-permute-start | bytes 2752520 | tf_op jit(solution)/shard_map/ppermute | solution.py:48
  43.1 5.0 %collective-permute-start.4 = (bf16[240,1792]{1,0:T(8,128)(2,1)S(1)}, bf16[240,1792]{1,0:T(8,128)(2,1)S(1)}, u32[]{:S(2)}, u32[]{:S(2)}) collective-permute-start(bf16[240,1792]{1,0:T(8,128)(2,1)S(1)} %collective-permute-done.3), channel_id=1, source_target_pairs={{0,2},{2,0},{1,3},{3,1},{4,6},{6,4},{5,7},{7,5},{8,10},{10,8},{9,1... | collective-permute-start | bytes 2580488 | tf_op jit(solution)/shard_map/ppermute | solution.py:48
  46.1 3.2 %collective-permute-start.7 = (bf16[240,1792]{1,0:T(8,128)(2,1)S(1)}, bf16[240,1792]{1,0:T(8,128)(2,1)S(1)}, u32[]{:S(2)}, u32[]{:S(2)}) collective-permute-start(bf16[240,1792]{1,0:T(8,128)(2,1)S(1)} %constant_dynamic-update-slice_fusion), channel_id=1, source_target_pairs={{0,2},{2,0},{1,3},{3,1},{4,6},{6,4},{5,7},{7,5},{8,10},{10,8},{9,1... | collective-permute-start | bytes 2580488 | tf_op jit(solution)/shard_map/ppermute | solution.py:48
  53.1 17.1 %collective-permute-start.17 = (bf16[512,896]{1,0:T(8,128)(2,1)S(1)}, bf16[512,896]{1,0:T(8,128)(2,1)S(1)}, u32[]{:S(2)}, u32[]{:S(2)}) collective-permute-start(bf16[512,896]{1,0:T(8,128)(2,1)S(1)} %slice.344), channel_id=1, source_target_pairs={{0,2},{2,0},{1,3},{3,1},{4,6},{6,4},{5,7},{7,5},{8,10},{10,8},{9,1... | collective-permute-start | bytes 2752520 | tf_op jit(solution)/shard_map/ppermute | solution.py:48
  55.6 14.6 %collective-permute-start.18 = (bf16[512,896]{1,0:T(8,128)(2,1)S(1)}, bf16[512,896]{1,0:T(8,128)(2,1)S(1)}, u32[]{:S(2)}, u32[]{:S(2)}) collective-permute-start(bf16[512,896]{1,0:T(8,128)(2,1)S(1)} %slice.344), channel_id=1, source_target_pairs={{14,0},{15,1},{1,2},{0,3},{2,4},{3,5},{5,6},{4,7},{6,8},{7,9},{9,1... | collective-permute-start | bytes 2752520 | tf_op jit(solution)/shard_map/ppermute | solution.py:43
  56.6 13.6 %collective-permute-start.14 = (bf16[512,896]{1,0:T(8,128)(2,1)S(1)}, bf16[512,896]{1,0:T(8,128)(2,1)S(1)}, u32[]{:S(2)}, u32[]{:S(2)}) collective-permute-start(bf16[512,896]{1,0:T(8,128)(2,1)S(1)} %get-tuple-element.65), channel_id=1, source_target_pairs={{65,0},{64,1},{6,2},{7,3},{69,4},{68,5},{10,6},{11,7},{73,8},{72,9... | collective-permute-start | bytes 2752520 | tf_op jit(solution)/shard_map/ppermute | solution.py:43
  59.8 10.3 %collective-permute-start.16 = (bf16[512,896]{1,0:T(8,128)(2,1)S(1)}, bf16[512,896]{1,0:T(8,128)(2,1)S(1)}, u32[]{:S(2)}, u32[]{:S(2)}) collective-permute-start(bf16[512,896]{1,0:T(8,128)(2,1)S(1)} %get-tuple-element.64), channel_id=1, source_target_pairs={{0,2},{2,0},{1,3},{3,1},{4,6},{6,4},{5,7},{7,5},{8,10},{10,8},{9,1... | collective-permute-start | bytes 2752520 | tf_op jit(solution)/shard_map/ppermute | solution.py:48
  78.7 15.5 %collective-permute-start.21 = (bf16[512,896]{1,0:T(8,128)(2,1)S(1)}, bf16[512,896]{1,0:T(8,128)(2,1)S(1)}, u32[]{:S(2)}, u32[]{:S(2)}) collective-permute-start(bf16[512,896]{1,0:T(8,128)(2,1)S(1)} %get-tuple-element.26), channel_id=1, source_target_pairs={{64,0},{65,1},{10,2},{11,3},{68,4},{69,5},{14,6},{15,7},{72,8},{73... | collective-permute-start | bytes 2752520 | tf_op jit(solution)/shard_map/ppermute | solution.py:43
  81.9 21.9 %collective-permute-start.20 = (bf16[512,896]{1,0:T(8,128)(2,1)S(1)}, bf16[512,896]{1,0:T(8,128)(2,1)S(1)}, u32[]{:S(2)}, u32[]{:S(2)}) collective-permute-start(bf16[512,896]{1,0:T(8,128)(2,1)S(1)} %get-tuple-element.27), channel_id=1, source_target_pairs={{65,0},{64,1},{6,2},{7,3},{69,4},{68,5},{10,6},{11,7},{73,8},{72,9... | collective-permute-start | bytes 2752520 | tf_op jit(solution)/shard_map/ppermute | solution.py:43
  91.7 13.5 %collective-permute-start.19 = (bf16[512,896]{1,0:T(8,128)(2,1)S(1)}, bf16[512,896]{1,0:T(8,128)(2,1)S(1)}, u32[]{:S(2)}, u32[]{:S(2)}) collective-permute-start(bf16[512,896]{1,0:T(8,128)(2,1)S(1)} %get-tuple-element.33), channel_id=1, source_target_pairs={{1,0},{0,1},{14,2},{15,3},{5,4},{4,5},{2,6},{3,7},{9,8},{8,9},{6,1... | collective-permute-start | bytes 2752520 | tf_op jit(solution)/shard_map/ppermute | solution.py:43
  94.2 14.5 %collective-permute-start.25 = (bf16[320,1792]{1,0:T(8,128)(2,1)S(1)}, bf16[320,1792]{1,0:T(8,128)(2,1)S(1)}, u32[]{:S(2)}, u32[]{:S(2)}) collective-permute-start(bf16[320,1792]{1,0:T(8,128)(2,1)S(1)} %pad_maximum_fusion), channel_id=1, source_target_pairs={{0,2},{2,0},{1,3},{3,1},{4,6},{6,4},{5,7},{7,5},{8,10},{10,8},{9,1... | collective-permute-start | bytes 3440648 | tf_op jit(solution)/shard_map/ppermute | solution.py:48
  105.8 6.8 %collective-permute-start.24 = (bf16[128,896]{1,0:T(8,128)(2,1)S(1)}, bf16[128,896]{1,0:T(8,128)(2,1)S(1)}, u32[]{:S(2)}, u32[]{:S(2)}) collective-permute-start(bf16[128,896]{1,0:T(8,128)(2,1)S(1)} %get-tuple-element.37), channel_id=1, source_target_pairs={{8,0},{9,1},{66,2},{67,3},{12,4},{13,5},{70,6},{71,7},{0,8},{1,9},... | collective-permute-start | bytes 688136 | tf_op jit(solution)/shard_map/ppermute | solution.py:43
  107.9 7.2 %collective-permute-start.23 = (bf16[128,896]{1,0:T(8,128)(2,1)S(1)}, bf16[128,896]{1,0:T(8,128)(2,1)}, u32[]{:S(2)}, u32[]{:S(2)}) collective-permute-start(bf16[128,896]{1,0:T(8,128)(2,1)S(1)} %get-tuple-element.36), channel_id=1, source_target_pairs={{4,0},{5,1},{67,2},{66,3},{8,4},{9,5},{71,6},{70,7},{12,8},{13,9},... | collective-permute-start | bytes 688136 | tf_op jit(solution)/shard_map/ppermute | solution.py:43
  108.3 6.8 %collective-permute-start.22 = (bf16[128,896]{1,0:T(8,128)(2,1)S(1)}, bf16[128,896]{1,0:T(8,128)(2,1)}, u32[]{:S(2)}, u32[]{:S(2)}) collective-permute-start(bf16[128,896]{1,0:T(8,128)(2,1)S(1)} %get-tuple-element.35), channel_id=1, source_target_pairs={{12,0},{13,1},{3,2},{2,3},{0,4},{1,5},{7,6},{6,7},{4,8},{5,9},{11,... | collective-permute-start | bytes 688136 | tf_op jit(solution)/shard_map/ppermute | solution.py:43
  109.1 8.0 %collective-permute-start.28 = (bf16[80,1792]{1,0:T(8,128)(2,1)S(1)}, bf16[80,1792]{1,0:T(8,128)(2,1)S(1)}, u32[]{:S(2)}, u32[]{:S(2)}) collective-permute-start(bf16[80,1792]{1,0:T(8,128)(2,1)S(1)} %get-tuple-element.67), channel_id=1, source_target_pairs={{0,32},{16,48},{32,0},{48,16},{1,33},{17,49},{33,1},{49,17},{2,34}... | collective-permute-start | bytes 860168 | tf_op jit(solution)/shard_map/ppermute | solution.py:48
  111.4 13.5 %collective-permute-start.27 = (bf16[80,1792]{1,0:T(8,128)(2,1)S(1)}, bf16[80,1792]{1,0:T(8,128)(2,1)S(1)}, u32[]{:S(2)}, u32[]{:S(2)}) collective-permute-start(bf16[80,1792]{1,0:T(8,128)(2,1)S(1)} %get-tuple-element.68), channel_id=1, source_target_pairs={{0,48},{16,0},{32,16},{48,32},{1,49},{17,1},{33,17},{49,33},{2,50}... | collective-permute-start | bytes 860168 | tf_op jit(solution)/shard_map/ppermute | solution.py:48
  112.6 0.7 copy-start.3
  113.2 11.7 %collective-permute-start.26 = (bf16[80,1792]{1,0:T(8,128)(2,1)S(1)}, bf16[80,1792]{1,0:T(8,128)(2,1)S(1)}, u32[]{:S(2)}, u32[]{:S(2)}) collective-permute-start(bf16[80,1792]{1,0:T(8,128)(2,1)S(1)} %get-tuple-element.66), channel_id=1, source_target_pairs={{0,16},{16,32},{32,48},{48,0},{1,17},{17,33},{33,49},{49,1},{2,18}... | collective-permute-start | bytes 860168 | tf_op jit(solution)/shard_map/ppermute | solution.py:48

commit v2 on v1

--- a/solution.py
+++ b/solution.py
@@ -134,14 +134,21 @@
     keep = jnp.where(core == 0, inputs, cotangent)
     give = jnp.where(core == 0, cotangent, inputs)
     first = cat([keep, shift(give, CORE, 1)])
-    ring = [first, fetch(first, "y+", "P"), fetch(first, "y-", "Q"), fetch(first, "y2", "PQ")]
-    g = hold(cat([v[:t] for v in ring] + [v[t:] for v in ring]))
-    a, b = fetch(g, "P", "y+"), fetch(g, "Q", "y-")
-    n = 4 * t
-    far = fetch(a[:n], "Q", "y+")
-    far_received = fetch(b[n:], "P", "y-", cross=True)
-    mine = (g, a, b, far)
-    received = (shift(g[n:], CORE, 1), shift(a[n:], CORE, 1), shift(b[n:], CORE, 1), far_received)
+    f, b = fetch(first, "y+", "P"), fetch(first, "y-", "Q")
+    far = fetch(first, "y2", "PQ")
+    g_own = hold(cat([v[:t] for v in (first, f, b, far)]))
+    g_other = hold(cat([v[t:] for v in (first, f, b, far)]))
+    a_own = fetch(g_own, "P", "y+")
+    b_other = fetch(g_other, "Q", "y-")
+    a_other = fetch(g_other, "P", "y+")
+    b_own = fetch(g_own, "Q", "y-")
+    mine = (g_own, a_own, b_own, fetch(a_own, "Q", "y+"))
+    received = (
+        shift(g_other, CORE, 1),
+        shift(a_other, CORE, 1),
+        shift(b_other, CORE, 1),
+        fetch(b_other, "P", "y-", cross=True),
+    )
 
     own_w = prepare(side, gate_weight, up_weight, down_weight)
     wf, wb = shift(own_w, X, 1), shift(own_w, X, -1)
@@ -186,6 +193,7 @@
     dg0, du0 = hidden_grads(x0, c0)
     own_part, fwd_part = input_partials(dg0, du0, (0, 1))
     got_fwd = fetch(fwd_part, "P", "y-")
+    dg0, dg1, own_part, fwd_part = hold((dg0, dg1, own_part, fwd_part))
 
     gg = hold(
         (

time: 127 us -> 137 us (1.079); the launches traced: 126 us -> 134 us
  waiting for transfers between devices: 47.2 us -> 53 us
  starting transfers between devices: 48.6 us -> 51.8 us
    ppermute x13 -> x15, waiting for transfers between devices: 35.8 us -> 42.3 us  [fetch(): return lax.ppermute(x, PLANE, pairs)]
    ppermute x13 -> x15, starting transfers between devices: 21.9 us -> 27.7 us  [fetch(): return lax.ppermute(x, PLANE, pairs)]
    ppermute x16, starting transfers between devices: 26.7 us -> 24 us  [shift(): return lax.ppermute(x, axis, [(i, (i - by) % n) for i in range(n)])]
    unnamed x30 -> x24, local copies, waits for them, and re-layouts: 4.19 us -> 4.03 us
  transfers between devices with their start and end apart: 29 -> 31, of which waited for: 12 -> 13; matrix products, arithmetic and copies ran while one was open for 12% -> 5% of each run, Pallas kernels for 0% -> 0%
where the time goes in v2:
time: 137 us; the launch traced here: 134 us
  waiting for transfers between devices  53 us (39%)
  starting transfers between devices  51.8 us (38%)
  matrix products  17.1 us (12%)
  other arithmetic  5.88 us (4%)
  local copies, waits for them, and re-layouts  4.89 us (4%)
    ppermute x15, waiting for transfers between devices, fetch(): return lax.ppermute(x, PLANE, pairs)  42.3 us
    ppermute x15, starting transfers between devices, fetch(): return lax.ppermute(x, PLANE, pairs)  27.7 us
    ppermute x16, starting transfers between devices, shift(): return lax.ppermute(x, axis, [(i, (i - by) % n) for i in range(n)])  24 us
    ppermute x16, waiting for transfers between devices, shift(): return lax.ppermute(x, axis, [(i, (i - by) % n) for i in range(n)])  10.7 us
    dot_general x6, matrix products, rdot(): lax.dot_general(left, right, (((1,), (1,)), ((), ())), preferred_element_...  9.09 us
    dot_general x2, matrix products, input_partials(): lax.dot_general(cat([dgate, dup]), wgu, (((0,), (0,)), ((), ())), preferr...  5.28 us
    unnamed x24, local copies, waits for them, and re-layouts  4.03 us
    convert_element_type x4, other arithmetic, total(): return out.astype(BF16)  2.86 us
  transfers between devices with their start and end apart: 31, of which 13 were waited for; matrix products, arithmetic and copies ran while one was open for 5% of the time, Pallas kernels for 0%

profile of v2, /device:TPU:1, one launch (start us, length us, event | category | flops | bytes accessed | tf_op | source)
XLA Modules:
  0.0 134.5 jit_solution(6299703736926994081)
XLA Ops:
  0.6 1.1 broadcast_select_fusion.1
  1.7 1.5 %collective-permute-start.8 = (bf16[128,896]{1,0:T(8,128)(2,1)S(1)}, bf16[128,896]{1,0:T(8,128)(2,1)S(1)}, u32[]{:S(2)}, u32[]{:S(2)}) collective-permute-start(bf16[128,896]{1,0:T(8,128)(2,1)S(1)} %get-tuple-element.96), channel_id=1, source_target_pairs={{0,2},{2,0},{1,3},{3,1},{4,6},{6,4},{5,7},{7,5},{8,10},{10,8},{9,1... | collective-permute-start | bytes 688136 | tf_op jit(solution)/shard_map/ppermute | solution.py:48
  3.2 1.0 copy-done
  4.2 1.0 copy-done.1
  5.1 1.0 copy-done.2
  6.1 0.1 prepare.1
  6.3 2.7 %collective-permute-start.1 = (bf16[240,1792]{1,0:T(8,128)(2,1)S(1)}, bf16[240,1792]{1,0:T(8,128)(2,1)S(1)}, u32[]{:S(2)}, u32[]{:S(2)}) collective-permute-start(bf16[240,1792]{1,0:T(8,128)(2,1)S(1)} %prepare.1), channel_id=1, source_target_pairs={{0,48},{16,0},{32,16},{48,32},{1,49},{17,1},{33,17},{49,33},{2,50}... | collective-permute-start | bytes 2580488 | tf_op jit(solution)/shard_map/ppermute | solution.py:48
  9.0 1.7 %collective-permute-start.9 = (bf16[256,896]{1,0:T(8,128)(2,1)S(1)}, bf16[256,896]{1,0:T(8,128)(2,1)S(1)}, u32[]{:S(2)}, u32[]{:S(2)}) collective-permute-start(bf16[256,896]{1,0:T(8,128)(2,1)S(1)} %pad_maximum_fusion.3), channel_id=1, source_target_pairs={{4,0},{5,1},{3,2},{2,3},{8,4},{9,5},{7,6},{6,7},{12,8},{13,9},{11,... | collective-permute-start | bytes 1376264 | tf_op jit(solution)/shard_map/ppermute | solution.py:43
  10.7 2.2 %collective-permute-start.10 = (bf16[256,896]{1,0:T(8,128)(2,1)S(1)}, bf16[256,896]{1,0:T(8,128)(2,1)S(1)}, u32[]{:S(2)}, u32[]{:S(2)}) collective-permute-start(bf16[256,896]{1,0:T(8,128)(2,1)S(1)} %pad_maximum_fusion.3), channel_id=1, source_target_pairs={{12,0},{13,1},{67,2},{66,3},{0,4},{1,5},{71,6},{70,7},{4,8},{5,9},... | collective-permute-start | bytes 1376264 | tf_op jit(solution)/shard_map/ppermute | solution.py:43
  13.0 3.9 %collective-permute-done.9 = bf16[256,896]{1,0:T(8,128)(2,1)S(1)} collective-permute-done((bf16[256,896]{1,0:T(8,128)(2,1)S(1)}, bf16[256,896]{1,0:T(8,128)(2,1)S(1)}, u32[]{:S(2)}, u32[]{:S(2)}) %collective-permute-start.9) | collective-permute-done | bytes 458784 | tf_op jit(solution)/shard_map/ppermute | solution.py:43
  16.9 3.4 %collective-permute-start.11 = (bf16[256,896]{1,0:T(8,128)(2,1)S(1)}, bf16[256,896]{1,0:T(8,128)(2,1)S(1)}, u32[]{:S(2)}, u32[]{:S(2)}) collective-permute-start(bf16[256,896]{1,0:T(8,128)(2,1)S(1)} %pad_maximum_fusion.3), channel_id=1, source_target_pairs={{8,0},{9,1},{66,2},{67,3},{12,4},{13,5},{70,6},{71,7},{0,8},{1,9},... | collective-permute-start | bytes 1376264 | tf_op jit(solution)/shard_map/ppermute | solution.py:43
  20.4 6.1 %collective-permute-done.11 = bf16[256,896]{1,0:T(8,128)(2,1)S(1)} collective-permute-done((bf16[256,896]{1,0:T(8,128)(2,1)S(1)}, bf16[256,896]{1,0:T(8,128)(2,1)S(1)}, u32[]{:S(2)}, u32[]{:S(2)}) %collective-permute-start.11) | collective-permute-done | bytes 458784 | tf_op jit(solution)/shard_map/ppermute | solution.py:43
  26.6 1.1 collective-permute-start.18
  27.7 1.8 %collective-permute-start.16 = (bf16[512,896]{1,0:T(8,128)(2,1)S(1)}, bf16[512,896]{1,0:T(8,128)(2,1)S(1)}, u32[]{:S(2)}, u32[]{:S(2)}) collective-permute-start(bf16[512,896]{1,0:T(8,128)(2,1)S(1)} %pad_maximum_fusion.2), channel_id=1, source_target_pairs={{1,0},{0,1},{6,2},{7,3},{5,4},{4,5},{10,6},{11,7},{9,8},{8,9},{14,... | collective-permute-start | bytes 2752520 | tf_op jit(solution)/shard_map/ppermute | solution.py:43
  29.6 2.7 %collective-permute-start.6 = (bf16[128,1792]{1,0:T(8,128)(2,1)S(1)}, bf16[128,1792]{1,0:T(8,128)(2,1)S(1)}, u32[]{:S(2)}, u32[]{:S(2)}) collective-permute-start(bf16[128,1792]{1,0:T(8,128)(2,1)S(1)} %slice.316), channel_id=1, source_target_pairs={{0,48},{16,0},{32,16},{48,32},{1,49},{17,1},{33,17},{49,33},{2,50}... | collective-permute-start | bytes 1376264 | tf_op jit(solution)/shard_map/ppermute | solution.py:48
  32.5 4.2 %collective-permute-start.2 = (bf16[240,1792]{1,0:T(8,128)(2,1)S(1)}, bf16[240,1792]{1,0:T(8,128)(2,1)S(1)}, u32[]{:S(2)}, u32[]{:S(2)}) collective-permute-start(bf16[240,1792]{1,0:T(8,128)(2,1)S(1)} %collective-permute-done.1), channel_id=1, source_target_pairs={{0,2},{2,0},{1,3},{3,1},{4,6},{6,4},{5,7},{7,5},{8,10},{10,8},{9,1... | collective-permute-start | bytes 2580488 | tf_op jit(solution)/shard_map/ppermute | solution.py:48
  36.7 1.7 %collective-permute-done.6 = bf16[128,1792]{1,0:T(8,128)(2,1)S(1)} collective-permute-done((bf16[128,1792]{1,0:T(8,128)(2,1)S(1)}, bf16[128,1792]{1,0:T(8,128)(2,1)S(1)}, u32[]{:S(2)}, u32[]{:S(2)}) %collective-permute-start.6) | collective-permute-done | bytes 458784 | tf_op jit(solution)/shard_map/ppermute | solution.py:48
  38.4 4.7 %collective-permute-start.15 = (bf16[512,896]{1,0:T(8,128)(2,1)S(1)}, bf16[512,896]{1,0:T(8,128)(2,1)S(1)}, u32[]{:S(2)}, u32[]{:S(2)}) collective-permute-start(bf16[512,896]{1,0:T(8,128)(2,1)S(1)} %pad_maximum_fusion.2), channel_id=1, source_target_pairs={{0,2},{2,0},{1,3},{3,1},{4,6},{6,4},{5,7},{7,5},{8,10},{10,8},{9,1... | collective-permute-start | bytes 2752520 | tf_op jit(solution)/shard_map/ppermute | solution.py:48
  43.1 2.8 %collective-permute-start.12 = (bf16[512,896]{1,0:T(8,128)(2,1)S(1)}, bf16[512,896]{1,0:T(8,128)(2,1)S(1)}, u32[]{:S(2)}, u32[]{:S(2)}) collective-permute-start(bf16[512,896]{1,0:T(8,128)(2,1)S(1)} %pad_maximum_fusion.1.m0), channel_id=1, source_target_pairs={{1,0},{0,1},{6,2},{7,3},{5,4},{4,5},{10,6},{11,7},{9,8},{8,9},{14,... | collective-permute-start | bytes 2752520 | tf_op jit(solution)/shard_map/ppermute | solution.py:43
  46.0 1.8 %collective-permute-start.4 = (bf16[240,1792]{1,0:T(8,128)(2,1)S(1)}, bf16[240,1792]{1,0:T(8,128)(2,1)S(1)}, u32[]{:S(2)}, u32[]{:S(2)}) collective-permute-start(bf16[240,1792]{1,0:T(8,128)(2,1)S(1)} %collective-permute-done.3), channel_id=1, source_target_pairs={{0,2},{2,0},{1,3},{3,1},{4,6},{6,4},{5,7},{7,5},{8,10},{10,8},{9,1... | collective-permute-start | bytes 2580488 | tf_op jit(solution)/shard_map/ppermute | solution.py:48
  47.8 2.0 %collective-permute-done.4 = bf16[240,1792]{1,0:T(8,128)(2,1)S(1)} collective-permute-done((bf16[240,1792]{1,0:T(8,128)(2,1)S(1)}, bf16[240,1792]{1,0:T(8,128)(2,1)S(1)}, u32[]{:S(2)}, u32[]{:S(2)}) %collective-permute-start.4) | collective-permute-done | bytes 860192 | tf_op jit(solution)/shard_map/ppermute | solution.py:48
  49.8 0.4 collective-permute-start.7
  50.2 0.8 collective-permute-start.13
  51.0 1.1 collective-permute-done.7
  52.2 0.4 collective-permute-start.19
  52.9 3.4 %collective-permute-done.12.m1 = bf16[512,896]{1,0:T(8,128)(2,1)S(1)} collective-permute-done((bf16[512,896]{1,0:T(8,128)(2,1)S(1)}, bf16[512,896]{1,0:T(8,128)(2,1)S(1)}, u32[]{:S(2)}, u32[]{:S(2)}) %collective-permute-start.12) | collective-permute-done | bytes 917536 | tf_op jit(solution)/shard_map/ppermute | solution.py:43
  56.3 3.4 %collective-permute-start.20 = (bf16[512,896]{1,0:T(8,128)(2,1)S(1)}, bf16[512,896]{1,0:T(8,128)(2,1)S(1)}, u32[]{:S(2)}, u32[]{:S(2)}) collective-permute-start(bf16[512,896]{1,0:T(8,128)(2,1)S(1)} %collective-permute-done.18), channel_id=1, source_target_pairs={{14,0},{15,1},{1,2},{0,3},{2,4},{3,5},{5,6},{4,7},{6,8},{7,9},{9,1... | collective-permute-start | bytes 2752520 | tf_op jit(solution)/shard_map/ppermute | solution.py:43
  59.7 1.9 %collective-permute-start.14 = (bf16[512,896]{1,0:T(8,128)(2,1)S(1)}, bf16[512,896]{1,0:T(8,128)(2,1)S(1)}, u32[]{:S(2)}, u32[]{:S(2)}) collective-permute-start(bf16[512,896]{1,0:T(8,128)(2,1)S(1)} %collective-permute-done.12.m1), channel_id=1, source_target_pairs={{65,0},{64,1},{6,2},{7,3},{69,4},{68,5},{10,6},{11,7},{73,8},{72,9... | collective-permute-start | bytes 2752520 | tf_op jit(solution)/shard_map/ppermute | solution.py:43
  61.6 0.6 collective-permute-start.17
  62.3 2.5 %collective-permute-done.13.m2 = bf16[512,896]{1,0:T(8,128)(2,1)S(1)} collective-permute-done((bf16[512,896]{1,0:T(8,128)(2,1)S(1)}, bf16[512,896]{1,0:T(8,128)(2,1)S(1)}, u32[]{:S(2)}, u32[]{:S(2)}) %collective-permute-start.13) | collective-permute-done | bytes 917536 | tf_op jit(solution)/shard_map/ppermute | solution.py:43
  64.8 7.2 %collective-permute-done.20.r3 = bf16[512,896]{1,0:T(8,128)(2,1)S(1)} collective-permute-done((bf16[512,896]{1,0:T(8,128)(2,1)S(1)}, bf16[512,896]{1,0:T(8,128)(2,1)S(1)}, u32[]{:S(2)}, u32[]{:S(2)}) %collective-permute-start.20) | collective-permute-done | bytes 917536 | tf_op jit(solution)/shard_map/ppermute | solution.py:43
  72.0 0.2 collective-permute-done.14.m3
  72.2 0.7 assemble.1
  72.9 1.4 %fusion.2 = f32[640,512]{1,0:T(8,128)S(1)} fusion(bf16[512,1792]{1,0:T(8,128)(2,1)S(1)} %get-tuple-element.26, bf16[1280,1792]{1,0:T(8,128)(2,1)S(1)} %get-tuple-element.76), kind=kOutput, calls=%fused_computation.6 | convolution fusion | flops 1174405120 | bytes 5439488 | tf_op jit(solution)/shard_map/dot_general | solution.py:52
  74.3 1.5 %multiply_convert_fusion.1 = (bf16[640,512]{1,0:T(8,128)(2,1)S(1)}, f32[640,512]{1,0:T(8,128)S(1)}) fusion(f32[640,512]{1,0:T(8,128)S(1)} %fusion.2, bf16[640,1792]{1,0:T(8,128)(2,1)S(1)} %get-tuple-element.75, bf16[512,1792]{1,0:T(8,128)(2,1)S(1)} %get-tuple-element.25), kind=kOutput, calls=%fused_computation.29 | convolution fusion | flops 1176371200 | bytes 7405568 | tf_op jit(solution)/shard_map/dot_general | solution.py:52
  75.8 1.7 %fusion.26 = bf16[640,512]{1,0:T(8,128)(2,1)S(1)} fusion(f32[640,512]{1,0:T(8,128)S(1)} %get-tuple-element.100, bf16[512,1792]{1,0:T(8,128)(2,1)S(1)} %get-tuple-element.26, bf16[1280,1792]{1,0:T(8,128)(2,1)S(1)} %get-tuple-element.76, f32[640,512]{1,0:T(8,128)S(1)} %fusion.2), kind=kOutput, calls=%fused_computation.19 | convolution fusion | flops 1177681920 | bytes 7405568 | tf_op jit(solution)/shard_map/dot_general | solution.py:52
  77.5 2.6 %convolution_convert_fusion.1 = bf16[512,1792]{1,0:T(8,128)(2,1)S(1)} fusion(bf16[1280,1792]{1,0:T(8,128)(2,1)S(1)} %get-tuple-element.76, bf16[640,512]{1,0:T(8,128)(2,1)S(1)} %get-tuple-element.28, bf16[640,512]{1,0:T(8,128)(2,1)S(1)} %fusion.26), kind=kOutput, calls=%fused_computation.2 | convolution fusion | flops 2352349184 | bytes 7733248 | tf_op jit(solution)/shard_map/dot_general | solution.py:177
  80.3 0.4 slice_select_fusion.2
  80.8 1.4 %fusion = f32[640,512]{1,0:T(8,128)S(1)} fusion(bf16[512,1792]{1,0:T(8,128)(2,1)S(1)} %get-tuple-element.32, bf16[1280,1792]{1,0:T(8,128)(2,1)S(1)} %get-tuple-element.76), kind=kOutput, calls=%fused_computation.4 | convolution fusion | flops 1174405120 | bytes 5439488 | tf_op jit(solution)/shard_map/dot_general | solution.py:52
  82.1 1.5 %multiply_convert_fusion = (bf16[640,512]{1,0:T(8,128)(2,1)S(1)}, f32[640,512]{1,0:T(8,128)S(1)}) fusion(f32[640,512]{1,0:T(8,128)S(1)} %fusion, bf16[640,1792]{1,0:T(8,128)(2,1)S(1)} %get-tuple-element.75, bf16[512,1792]{1,0:T(8,128)(2,1)S(1)} %get-tuple-element.31), kind=kOutput, calls=%fused_computation.27 | convolution fusion | flops 1176371200 | bytes 7405568 | tf_op jit(solution)/shard_map/dot_general | solution.py:52
  83.6 1.7 %fusion.29 = bf16[640,512]{1,0:T(8,128)(2,1)S(1)} fusion(f32[640,512]{1,0:T(8,128)S(1)} %get-tuple-element.102, bf16[512,1792]{1,0:T(8,128)(2,1)S(1)} %get-tuple-element.32, bf16[1280,1792]{1,0:T(8,128)(2,1)S(1)} %get-tuple-element.76, f32[640,512]{1,0:T(8,128)S(1)} %fusion), kind=kOutput, calls=%fused_computation.20 | convolution fusion | flops 1177681920 | bytes 7405568 | tf_op jit(solution)/shard_map/dot_general | solution.py:52
  85.3 2.6 %convolution_convert_fusion = bf16[512,1792]{1,0:T(8,128)(2,1)S(1)} fusion(bf16[1280,1792]{1,0:T(8,128)(2,1)S(1)} %get-tuple-element.76, bf16[640,512]{1,0:T(8,128)(2,1)S(1)} %get-tuple-element.34, bf16[640,512]{1,0:T(8,128)(2,1)S(1)} %fusion.29), kind=kOutput, calls=%fused_computation.1 | convolution fusion | flops 2352349184 | bytes 7733248 | tf_op jit(solution)/shard_map/dot_general | solution.py:177
  88.1 3.3 %collective-permute-start.22 = (bf16[512,896]{1,0:T(8,128)(2,1)S(1)}, bf16[512,896]{1,0:T(8,128)(2,1)S(1)}, u32[]{:S(2)}, u32[]{:S(2)}) collective-permute-start(bf16[512,896]{1,0:T(8,128)(2,1)S(1)} %get-tuple-element.30), channel_id=1, source_target_pairs={{65,0},{64,1},{6,2},{7,3},{69,4},{68,5},{10,6},{11,7},{73,8},{72,9... | collective-permute-start | bytes 2752520 | tf_op jit(solution)/shard_map/ppermute | solution.py:43
  91.4 0.9 collective-permute-start.23
  92.4 0.4 slice_select_fusion
  92.8 0.6 collective-permute-start.21
  93.4 1.4 %fusion.51 = f32[640,1792]{1,0:T(8,128)S(1)} fusion(bf16[640,512]{1,0:T(8,128)(2,1)S(1)} %fusion.29, bf16[512,1792]{1,0:T(8,128)(2,1)S(1)} %get-tuple-element.32), kind=kOutput, calls=%fused_computation.83 | convolution fusion | flops 1174405120 | bytes 7077888 | tf_op jit(solution)/shard_map/dot_general | solution.py:200
  94.8 1.4 %add_convert_fusion = bf16[640,1792]{1,0:T(8,128)(2,1)S(1)} fusion(f32[640,1792]{1,0:T(8,128)S(1)} %fusion.51, bf16[640,512]{1,0:T(8,128)(2,1)S(1)} %fusion.26, bf16[512,1792]{1,0:T(8,128)(2,1)S(1)} %get-tuple-element.26), kind=kOutput, calls=%fused_computation | convolution fusion | flops 1176698880 | bytes 9371648 | tf_op jit(solution)/shard_map/dot_general | solution.py:201
  96.1 0.2 fusion.40
  96.4 2.3 %collective-permute-start.27 = (bf16[320,1792]{1,0:T(8,128)(2,1)S(1)}, bf16[320,1792]{1,0:T(8,128)(2,1)S(1)}, u32[]{:S(2)}, u32[]{:S(2)}) collective-permute-start(bf16[320,1792]{1,0:T(8,128)(2,1)S(1)} %pad_maximum_fusion), channel_id=1, source_target_pairs={{0,2},{2,0},{1,3},{3,1},{4,6},{6,4},{5,7},{7,5},{8,10},{10,8},{9,1... | collective-permute-start | bytes 3440648 | tf_op jit(solution)/shard_map/ppermute | solution.py:48
  98.6 16.4 %collective-permute-done.21 = bf16[512,896]{1,0:T(8,128)(2,1)S(1)} collective-permute-done((bf16[512,896]{1,0:T(8,128)(2,1)S(1)}, bf16[512,896]{1,0:T(8,128)(2,1)S(1)}, u32[]{:S(2)}, u32[]{:S(2)}) %collective-permute-start.21) | collective-permute-done | bytes 917536 | tf_op jit(solution)/shard_map/ppermute | solution.py:43
  115.1 0.5 add_convert_fusion.2
  115.6 1.4 %collective-permute-start.24 = (bf16[128,896]{1,0:T(8,128)(2,1)S(1)}, bf16[128,896]{1,0:T(8,128)(2,1)S(1)}, u32[]{:S(2)}, u32[]{:S(2)}) collective-permute-start(bf16[128,896]{1,0:T(8,128)(2,1)S(1)} %get-tuple-element.39), channel_id=1, source_target_pairs={{12,0},{13,1},{3,2},{2,3},{0,4},{1,5},{7,6},{6,7},{4,8},{5,9},{11,... | collective-permute-start | bytes 688136 | tf_op jit(solution)/shard_map/ppermute | solution.py:43
  117.0 1.2 collective-permute-start.25
  118.2 1.1 collective-permute-start.26
  119.3 0.3 add_convert_fusion.1
  119.7 2.7 %collective-permute-start.29 = (bf16[80,1792]{1,0:T(8,128)(2,1)S(1)}, bf16[80,1792]{1,0:T(8,128)(2,1)S(1)}, u32[]{:S(2)}, u32[]{:S(2)}) collective-permute-start(bf16[80,1792]{1,0:T(8,128)(2,1)S(1)} %get-tuple-element.70), channel_id=1, source_target_pairs={{0,48},{16,0},{32,16},{48,32},{1,49},{17,1},{33,17},{49,33},{2,50}... | collective-permute-start | bytes 860168 | tf_op jit(solution)/shard_map/ppermute | solution.py:48
  122.4 0.7 copy-done.3
  123.1 2.5 %collective-permute-done.25 = bf16[128,896]{1,0:T(8,128)(2,1)} collective-permute-done((bf16[128,896]{1,0:T(8,128)(2,1)S(1)}, bf16[128,896]{1,0:T(8,128)(2,1)}, u32[]{:S(2)}, u32[]{:S(2)}) %collective-permute-start.25) | collective-permute-done | bytes 229408 | tf_op jit(solution)/shard_map/ppermute | solution.py:43
  125.6 2.0 %add_convert_fusion.4 = bf16[128,896]{1,0:T(8,128)(2,1)} fusion(bf16[128,896]{1,0:T(8,128)(2,1)} %collective-permute-done.26, bf16[128,896]{1,0:T(8,128)(2,1)} %collective-permute-done.25, bf16[128,896]{1,0:T(8,128)(2,1)} %copy-done.3, bf16[128,896]{1,0:T(8,128)(2,1)S(1)} %get-tuple-element.38), kind=kLoop, calls=%fused_computation.40 | loop fusion | flops 917504 | bytes 1146880 | tf_op jit(solution)/shard_map/convert_element_type | solution.py:59
  127.6 0.8 collective-permute-done.29
  128.3 5.1 %collective-permute-done.30 = bf16[80,1792]{1,0:T(8,128)(2,1)S(1)} collective-permute-done((bf16[80,1792]{1,0:T(8,128)(2,1)S(1)}, bf16[80,1792]{1,0:T(8,128)(2,1)S(1)}, u32[]{:S(2)}, u32[]{:S(2)}) %collective-permute-start.30) | collective-permute-done | bytes 286752 | tf_op jit(solution)/shard_map/ppermute | solution.py:48
  133.5 0.1 add_convert_fusion.3
  133.7 0.8 slice_select_fusion.4
  (61 shorter events, 1.8 us)
Async XLA Ops:
  1.7 7.2 %collective-permute-start.8 = (bf16[128,896]{1,0:T(8,128)(2,1)S(1)}, bf16[128,896]{1,0:T(8,128)(2,1)S(1)}, u32[]{:S(2)}, u32[]{:S(2)}) collective-permute-start(bf16[128,896]{1,0:T(8,128)(2,1)S(1)} %get-tuple-element.96), channel_id=1, source_target_pairs={{0,2},{2,0},{1,3},{3,1},{4,6},{6,4},{5,7},{7,5},{8,10},{10,8},{9,1... | collective-permute-start | bytes 688136 | tf_op jit(solution)/shard_map/ppermute | solution.py:48
  3.2 1.0 copy-start
  4.2 1.0 copy-start.1
  5.1 1.0 copy-start.2
  6.2 26.3 %collective-permute-start = (bf16[240,1792]{1,0:T(8,128)(2,1)S(1)}, bf16[240,1792]{1,0:T(8,128)(2,1)S(1)}, u32[]{:S(2)}, u32[]{:S(2)}) collective-permute-start(bf16[240,1792]{1,0:T(8,128)(2,1)S(1)} %prepare.1), channel_id=1, source_target_pairs={{0,2},{2,0},{1,3},{3,1},{4,6},{6,4},{5,7},{7,5},{8,10},{10,8},{9,1... | collective-permute-start | bytes 2580488 | tf_op jit(solution)/shard_map/ppermute | solution.py:48
  6.3 23.2 %collective-permute-start.1 = (bf16[240,1792]{1,0:T(8,128)(2,1)S(1)}, bf16[240,1792]{1,0:T(8,128)(2,1)S(1)}, u32[]{:S(2)}, u32[]{:S(2)}) collective-permute-start(bf16[240,1792]{1,0:T(8,128)(2,1)S(1)} %prepare.1), channel_id=1, source_target_pairs={{0,48},{16,0},{32,16},{48,32},{1,49},{17,1},{33,17},{49,33},{2,50}... | collective-permute-start | bytes 2580488 | tf_op jit(solution)/shard_map/ppermute | solution.py:48
  9.0 23.4 %collective-permute-start.3 = (bf16[240,1792]{1,0:T(8,128)(2,1)S(1)}, bf16[240,1792]{1,0:T(8,128)(2,1)S(1)}, u32[]{:S(2)}, u32[]{:S(2)}) collective-permute-start(bf16[240,1792]{1,0:T(8,128)(2,1)S(1)} %prepare.1), channel_id=1, source_target_pairs={{0,16},{16,32},{32,48},{48,0},{1,17},{17,33},{33,49},{49,1},{2,18}... | collective-permute-start | bytes 2580488 | tf_op jit(solution)/shard_map/ppermute | solution.py:48
  9.0 7.9 %collective-permute-start.9 = (bf16[256,896]{1,0:T(8,128)(2,1)S(1)}, bf16[256,896]{1,0:T(8,128)(2,1)S(1)}, u32[]{:S(2)}, u32[]{:S(2)}) collective-permute-start(bf16[256,896]{1,0:T(8,128)(2,1)S(1)} %pad_maximum_fusion.3), channel_id=1, source_target_pairs={{4,0},{5,1},{3,2},{2,3},{8,4},{9,5},{7,6},{6,7},{12,8},{13,9},{11,... | collective-permute-start | bytes 1376264 | tf_op jit(solution)/shard_map/ppermute | solution.py:43
  10.7 9.6 %collective-permute-start.10 = (bf16[256,896]{1,0:T(8,128)(2,1)S(1)}, bf16[256,896]{1,0:T(8,128)(2,1)S(1)}, u32[]{:S(2)}, u32[]{:S(2)}) collective-permute-start(bf16[256,896]{1,0:T(8,128)(2,1)S(1)} %pad_maximum_fusion.3), channel_id=1, source_target_pairs={{12,0},{13,1},{67,2},{66,3},{0,4},{1,5},{71,6},{70,7},{4,8},{5,9},... | collective-permute-start | bytes 1376264 | tf_op jit(solution)/shard_map/ppermute | solution.py:43
  16.9 9.6 %collective-permute-start.11 = (bf16[256,896]{1,0:T(8,128)(2,1)S(1)}, bf16[256,896]{1,0:T(8,128)(2,1)S(1)}, u32[]{:S(2)}, u32[]{:S(2)}) collective-permute-start(bf16[256,896]{1,0:T(8,128)(2,1)S(1)} %pad_maximum_fusion.3), channel_id=1, source_target_pairs={{8,0},{9,1},{66,2},{67,3},{12,4},{13,5},{70,6},{71,7},{0,8},{1,9},... | collective-permute-start | bytes 1376264 | tf_op jit(solution)/shard_map/ppermute | solution.py:43
  26.6 23.6 %collective-permute-start.18 = (bf16[512,896]{1,0:T(8,128)(2,1)S(1)}, bf16[512,896]{1,0:T(8,128)(2,1)S(1)}, u32[]{:S(2)}, u32[]{:S(2)}) collective-permute-start(bf16[512,896]{1,0:T(8,128)(2,1)S(1)} %pad_maximum_fusion.2), channel_id=1, source_target_pairs={{65,0},{64,1},{14,2},{15,3},{69,4},{68,5},{2,6},{3,7},{73,8},{72,9... | collective-permute-start | bytes 2752520 | tf_op jit(solution)/shard_map/ppermute | solution.py:43
  27.7 32.0 %collective-permute-start.16 = (bf16[512,896]{1,0:T(8,128)(2,1)S(1)}, bf16[512,896]{1,0:T(8,128)(2,1)S(1)}, u32[]{:S(2)}, u32[]{:S(2)}) collective-permute-start(bf16[512,896]{1,0:T(8,128)(2,1)S(1)} %pad_maximum_fusion.2), channel_id=1, source_target_pairs={{1,0},{0,1},{6,2},{7,3},{5,4},{4,5},{10,6},{11,7},{9,8},{8,9},{14,... | collective-permute-start | bytes 2752520 | tf_op jit(solution)/shard_map/ppermute | solution.py:43
  29.6 8.8 %collective-permute-start.6 = (bf16[128,1792]{1,0:T(8,128)(2,1)S(1)}, bf16[128,1792]{1,0:T(8,128)(2,1)S(1)}, u32[]{:S(2)}, u32[]{:S(2)}) collective-permute-start(bf16[128,1792]{1,0:T(8,128)(2,1)S(1)} %slice.316), channel_id=1, source_target_pairs={{0,48},{16,0},{32,16},{48,32},{1,49},{17,1},{33,17},{49,33},{2,50}... | collective-permute-start | bytes 1376264 | tf_op jit(solution)/shard_map/ppermute | solution.py:48
  32.4 10.7 %collective-permute-start.5 = (bf16[112,1792]{1,0:T(8,128)(2,1)S(1)}, bf16[112,1792]{1,0:T(8,128)(2,1)S(1)}, u32[]{:S(2)}, u32[]{:S(2)}) collective-permute-start(bf16[112,1792]{1,0:T(8,128)(2,1)S(1)} %slice.314), channel_id=1, source_target_pairs={{0,16},{16,32},{32,48},{48,0},{1,17},{17,33},{33,49},{49,1},{2,18}... | collective-permute-start | bytes 1204232 | tf_op jit(solution)/shard_map/ppermute | solution.py:48
  32.5 13.5 %collective-permute-start.2 = (bf16[240,1792]{1,0:T(8,128)(2,1)S(1)}, bf16[240,1792]{1,0:T(8,128)(2,1)S(1)}, u32[]{:S(2)}, u32[]{:S(2)}) collective-permute-start(bf16[240,1792]{1,0:T(8,128)(2,1)S(1)} %collective-permute-done.1), channel_id=1, source_target_pairs={{0,2},{2,0},{1,3},{3,1},{4,6},{6,4},{5,7},{7,5},{8,10},{10,8},{9,1... | collective-permute-start | bytes 2580488 | tf_op jit(solution)/shard_map/ppermute | solution.py:48
  38.4 23.2 %collective-permute-start.15 = (bf16[512,896]{1,0:T(8,128)(2,1)S(1)}, bf16[512,896]{1,0:T(8,128)(2,1)S(1)}, u32[]{:S(2)}, u32[]{:S(2)}) collective-permute-start(bf16[512,896]{1,0:T(8,128)(2,1)S(1)} %pad_maximum_fusion.2), channel_id=1, source_target_pairs={{0,2},{2,0},{1,3},{3,1},{4,6},{6,4},{5,7},{7,5},{8,10},{10,8},{9,1... | collective-permute-start | bytes 2752520 | tf_op jit(solution)/shard_map/ppermute | solution.py:48
  43.1 13.2 %collective-permute-start.12 = (bf16[512,896]{1,0:T(8,128)(2,1)S(1)}, bf16[512,896]{1,0:T(8,128)(2,1)S(1)}, u32[]{:S(2)}, u32[]{:S(2)}) collective-permute-start(bf16[512,896]{1,0:T(8,128)(2,1)S(1)} %pad_maximum_fusion.1.m0), channel_id=1, source_target_pairs={{1,0},{0,1},{6,2},{7,3},{5,4},{4,5},{10,6},{11,7},{9,8},{8,9},{14,... | collective-permute-start | bytes 2752520 | tf_op jit(solution)/shard_map/ppermute | solution.py:43
  46.0 3.8 %collective-permute-start.4 = (bf16[240,1792]{1,0:T(8,128)(2,1)S(1)}, bf16[240,1792]{1,0:T(8,128)(2,1)S(1)}, u32[]{:S(2)}, u32[]{:S(2)}) collective-permute-start(bf16[240,1792]{1,0:T(8,128)(2,1)S(1)} %collective-permute-done.3), channel_id=1, source_target_pairs={{0,2},{2,0},{1,3},{3,1},{4,6},{6,4},{5,7},{7,5},{8,10},{10,8},{9,1... | collective-permute-start | bytes 2580488 | tf_op jit(solution)/shard_map/ppermute | solution.py:48
  49.8 2.4 %collective-permute-start.7 = (bf16[240,1792]{1,0:T(8,128)(2,1)S(1)}, bf16[240,1792]{1,0:T(8,128)(2,1)S(1)}, u32[]{:S(2)}, u32[]{:S(2)}) collective-permute-start(bf16[240,1792]{1,0:T(8,128)(2,1)S(1)} %constant_dynamic-update-slice_fusion), channel_id=1, source_target_pairs={{0,2},{2,0},{1,3},{3,1},{4,6},{6,4},{5,7},{7,5},{8,10},{10,8},{9,1... | collective-permute-start | bytes 2580488 | tf_op jit(solution)/shard_map/ppermute | solution.py:48
  50.2 14.6 %collective-permute-start.13 = (bf16[512,896]{1,0:T(8,128)(2,1)S(1)}, bf16[512,896]{1,0:T(8,128)(2,1)S(1)}, u32[]{:S(2)}, u32[]{:S(2)}) collective-permute-start(bf16[512,896]{1,0:T(8,128)(2,1)S(1)} %pad_maximum_fusion.1.m0), channel_id=1, source_target_pairs={{65,0},{64,1},{14,2},{15,3},{69,4},{68,5},{2,6},{3,7},{73,8},{72,9... | collective-permute-start | bytes 2752520 | tf_op jit(solution)/shard_map/ppermute | solution.py:43
  52.2 12.6 %collective-permute-start.19 = (bf16[512,896]{1,0:T(8,128)(2,1)S(1)}, bf16[512,896]{1,0:T(8,128)(2,1)S(1)}, u32[]{:S(2)}, u32[]{:S(2)}) collective-permute-start(bf16[512,896]{1,0:T(8,128)(2,1)S(1)} %collective-permute-done.18), channel_id=1, source_target_pairs={{0,2},{2,0},{1,3},{3,1},{4,6},{6,4},{5,7},{7,5},{8,10},{10,8},{9,1... | collective-permute-start | bytes 2752520 | tf_op jit(solution)/shard_map/ppermute | solution.py:48
  56.3 15.7 %collective-permute-start.20 = (bf16[512,896]{1,0:T(8,128)(2,1)S(1)}, bf16[512,896]{1,0:T(8,128)(2,1)S(1)}, u32[]{:S(2)}, u32[]{:S(2)}) collective-permute-start(bf16[512,896]{1,0:T(8,128)(2,1)S(1)} %collective-permute-done.18), channel_id=1, source_target_pairs={{14,0},{15,1},{1,2},{0,3},{2,4},{3,5},{5,6},{4,7},{6,8},{7,9},{9,1... | collective-permute-start | bytes 2752520 | tf_op jit(solution)/shard_map/ppermute | solution.py:43
  59.7 12.5 %collective-permute-start.14 = (bf16[512,896]{1,0:T(8,128)(2,1)S(1)}, bf16[512,896]{1,0:T(8,128)(2,1)S(1)}, u32[]{:S(2)}, u32[]{:S(2)}) collective-permute-start(bf16[512,896]{1,0:T(8,128)(2,1)S(1)} %collective-permute-done.12.m1), channel_id=1, source_target_pairs={{65,0},{64,1},{6,2},{7,3},{69,4},{68,5},{10,6},{11,7},{73,8},{72,9... | collective-permute-start | bytes 2752520 | tf_op jit(solution)/shard_map/ppermute | solution.py:43
  61.6 10.6 %collective-permute-start.17 = (bf16[512,896]{1,0:T(8,128)(2,1)S(1)}, bf16[512,896]{1,0:T(8,128)(2,1)S(1)}, u32[]{:S(2)}, u32[]{:S(2)}) collective-permute-start(bf16[512,896]{1,0:T(8,128)(2,1)S(1)} %collective-permute-done.16), channel_id=1, source_target_pairs={{0,2},{2,0},{1,3},{3,1},{4,6},{6,4},{5,7},{7,5},{8,10},{10,8},{9,1... | collective-permute-start | bytes 2752520 | tf_op jit(solution)/shard_map/ppermute | solution.py:48
  88.1 26.9 %collective-permute-start.22 = (bf16[512,896]{1,0:T(8,128)(2,1)S(1)}, bf16[512,896]{1,0:T(8,128)(2,1)S(1)}, u32[]{:S(2)}, u32[]{:S(2)}) collective-permute-start(bf16[512,896]{1,0:T(8,128)(2,1)S(1)} %get-tuple-element.30), channel_id=1, source_target_pairs={{65,0},{64,1},{6,2},{7,3},{69,4},{68,5},{10,6},{11,7},{73,8},{72,9... | collective-permute-start | bytes 2752520 | tf_op jit(solution)/shard_map/ppermute | solution.py:43
  91.4 23.6 %collective-permute-start.23 = (bf16[512,896]{1,0:T(8,128)(2,1)S(1)}, bf16[512,896]{1,0:T(8,128)(2,1)S(1)}, u32[]{:S(2)}, u32[]{:S(2)}) collective-permute-start(bf16[512,896]{1,0:T(8,128)(2,1)S(1)} %get-tuple-element.29), channel_id=1, source_target_pairs={{64,0},{65,1},{10,2},{11,3},{68,4},{69,5},{14,6},{15,7},{72,8},{73... | collective-permute-start | bytes 2752520 | tf_op jit(solution)/shard_map/ppermute | solution.py:43
  92.8 22.3 %collective-permute-start.21 = (bf16[512,896]{1,0:T(8,128)(2,1)S(1)}, bf16[512,896]{1,0:T(8,128)(2,1)S(1)}, u32[]{:S(2)}, u32[]{:S(2)}) collective-permute-start(bf16[512,896]{1,0:T(8,128)(2,1)S(1)} %get-tuple-element.36), channel_id=1, source_target_pairs={{1,0},{0,1},{14,2},{15,3},{5,4},{4,5},{2,6},{3,7},{9,8},{8,9},{6,1... | collective-permute-start | bytes 2752520 | tf_op jit(solution)/shard_map/ppermute | solution.py:43
  96.4 22.9 %collective-permute-start.27 = (bf16[320,1792]{1,0:T(8,128)(2,1)S(1)}, bf16[320,1792]{1,0:T(8,128)(2,1)S(1)}, u32[]{:S(2)}, u32[]{:S(2)}) collective-permute-start(bf16[320,1792]{1,0:T(8,128)(2,1)S(1)} %pad_maximum_fusion), channel_id=1, source_target_pairs={{0,2},{2,0},{1,3},{3,1},{4,6},{6,4},{5,7},{7,5},{8,10},{10,8},{9,1... | collective-permute-start | bytes 3440648 | tf_op jit(solution)/shard_map/ppermute | solution.py:48
  115.6 6.8 %collective-permute-start.24 = (bf16[128,896]{1,0:T(8,128)(2,1)S(1)}, bf16[128,896]{1,0:T(8,128)(2,1)S(1)}, u32[]{:S(2)}, u32[]{:S(2)}) collective-permute-start(bf16[128,896]{1,0:T(8,128)(2,1)S(1)} %get-tuple-element.39), channel_id=1, source_target_pairs={{12,0},{13,1},{3,2},{2,3},{0,4},{1,5},{7,6},{6,7},{4,8},{5,9},{11,... | collective-permute-start | bytes 688136 | tf_op jit(solution)/shard_map/ppermute | solution.py:43
  117.0 8.6 %collective-permute-start.25 = (bf16[128,896]{1,0:T(8,128)(2,1)S(1)}, bf16[128,896]{1,0:T(8,128)(2,1)}, u32[]{:S(2)}, u32[]{:S(2)}) collective-permute-start(bf16[128,896]{1,0:T(8,128)(2,1)S(1)} %get-tuple-element.40), channel_id=1, source_target_pairs={{4,0},{5,1},{67,2},{66,3},{8,4},{9,5},{71,6},{70,7},{12,8},{13,9},... | collective-permute-start | bytes 688136 | tf_op jit(solution)/shard_map/ppermute | solution.py:43
  118.2 7.4 %collective-permute-start.26 = (bf16[128,896]{1,0:T(8,128)(2,1)S(1)}, bf16[128,896]{1,0:T(8,128)(2,1)}, u32[]{:S(2)}, u32[]{:S(2)}) collective-permute-start(bf16[128,896]{1,0:T(8,128)(2,1)S(1)} %get-tuple-element.41), channel_id=1, source_target_pairs={{8,0},{9,1},{66,2},{67,3},{12,4},{13,5},{70,6},{71,7},{0,8},{1,9},... | collective-permute-start | bytes 688136 | tf_op jit(solution)/shard_map/ppermute | solution.py:43
  119.7 7.9 %collective-permute-start.28 = (bf16[80,1792]{1,0:T(8,128)(2,1)S(1)}, bf16[80,1792]{1,0:T(8,128)(2,1)S(1)}, u32[]{:S(2)}, u32[]{:S(2)}) collective-permute-start(bf16[80,1792]{1,0:T(8,128)(2,1)S(1)} %get-tuple-element.68), channel_id=1, source_target_pairs={{0,16},{16,32},{32,48},{48,0},{1,17},{17,33},{33,49},{49,1},{2,18}... | collective-permute-start | bytes 860168 | tf_op jit(solution)/shard_map/ppermute | solution.py:48
  119.7 8.6 %collective-permute-start.29 = (bf16[80,1792]{1,0:T(8,128)(2,1)S(1)}, bf16[80,1792]{1,0:T(8,128)(2,1)S(1)}, u32[]{:S(2)}, u32[]{:S(2)}) collective-permute-start(bf16[80,1792]{1,0:T(8,128)(2,1)S(1)} %get-tuple-element.70), channel_id=1, source_target_pairs={{0,48},{16,0},{32,16},{48,32},{1,49},{17,1},{33,17},{49,33},{2,50}... | collective-permute-start | bytes 860168 | tf_op jit(solution)/shard_map/ppermute | solution.py:48
  122.4 0.7 copy-start.3
  123.1 10.4 %collective-permute-start.30 = (bf16[80,1792]{1,0:T(8,128)(2,1)S(1)}, bf16[80,1792]{1,0:T(8,128)(2,1)S(1)}, u32[]{:S(2)}, u32[]{:S(2)}) collective-permute-start(bf16[80,1792]{1,0:T(8,128)(2,1)S(1)} %get-tuple-element.69), channel_id=1, source_target_pairs={{0,32},{16,48},{32,0},{48,16},{1,33},{17,49},{33,1},{49,17},{2,34}... | collective-permute-start | bytes 860168 | tf_op jit(solution)/shard_map/ppermute | solution.py:48

commit v3 on v2

--- a/solution.py
+++ b/solution.py
@@ -89,7 +89,7 @@
     )(side.reshape(1), gate_weight, up_weight, down_weight)
 
 
-def assemble_body(core_ref, m0, m1, m2, m3, r0, r1, r2, r3, x0_ref, x1_ref, c0_ref, c1_ref):
+def assemble_body(core_ref, m0, m1, m2, m3, r0, r1, r2, r3, x_ref, c_ref):
     mine, received = (m0, m1, m2, m3), (r0, r1, r2, r3)
     half = m0.shape[1]
     t = m3.shape[0] // 4
@@ -104,8 +104,6 @@
             for g, y, f in itertools.product(range(2), range(4), range(2)):
                 block = g * 4 + y if k == 0 else y * 2 + g
                 z = position[g, f]
-                x_ref, c_ref = ((x0_ref, c0_ref), (x1_ref, c1_ref))[block // 4]
-                block = block % 4
                 rows, cols = slice(block * t, (block + 1) * t), slice(f * half, (f + 1) * half)
                 x_ref[rows, cols] = inputs[z][y * t : (y + 1) * t]
                 c_ref[rows, cols] = cotangent[y][z * t : (z + 1) * t]
@@ -113,13 +111,13 @@
 
 def assemble(core, mine, received):
     rows, half = mine[3].shape
-    shape = jax.ShapeDtypeStruct((rows, 2 * half), BF16)
+    shape = jax.ShapeDtypeStruct((2 * rows, 2 * half), BF16)
     return pl.pallas_call(
         assemble_body,
-        out_shape=(shape,) * 4,
+        out_shape=(shape,) * 2,
         in_specs=[SMEM] + [VMEM] * 8,
-        out_specs=(VMEM,) * 4,
-        compiler_params=pltpu.CompilerParams(vmem_limit_bytes=30 * 1024 * 1024),
+        out_specs=(VMEM,) * 2,
+        compiler_params=pltpu.CompilerParams(vmem_limit_bytes=4 * 1024 * 1024),
         cost_estimate=pl.CostEstimate(flops=4_000_000, bytes_accessed=15_000_000, transcendentals=0),
         name="assemble",
     )(core.reshape(1), *mine, *received)
@@ -134,6 +132,7 @@
     keep = jnp.where(core == 0, inputs, cotangent)
     give = jnp.where(core == 0, cotangent, inputs)
     first = cat([keep, shift(give, CORE, 1)])
+    first, on_left = hold((first, side == 0))
     f, b = fetch(first, "y+", "P"), fetch(first, "y-", "Q")
     far = fetch(first, "y2", "PQ")
     g_own = hold(cat([v[:t] for v in (first, f, b, far)]))
@@ -142,6 +141,7 @@
     b_other = fetch(g_other, "Q", "y-")
     a_other = fetch(g_other, "P", "y+")
     b_own = fetch(g_own, "Q", "y-")
+    n = 4 * t
     mine = (g_own, a_own, b_own, fetch(a_own, "Q", "y+"))
     received = (
         shift(g_other, CORE, 1),
@@ -160,7 +160,8 @@
     wd = hold(cat([w[2 * ROWS :] for w in pieces]))
     ff = wd.shape[0]
 
-    x0, x1, c0, c1 = assemble(core, mine, received)
+    x, c = assemble(core, mine, received)
+    x0, x1, c0, c1 = x[:n], x[n:], c[:n], c[n:]
 
     def hidden_grads(x, c):
         gate = rdot(wgu[:ff], x)
@@ -195,12 +196,7 @@
     got_fwd = fetch(fwd_part, "P", "y-")
     dg0, dg1, own_part, fwd_part = hold((dg0, dg1, own_part, fwd_part))
 
-    gg = hold(
-        (
-            jnp.dot(dg0, x0, preferred_element_type=F32)
-            + jnp.dot(dg1, x1, preferred_element_type=F32)
-        ).astype(BF16)
-    )
+    gg = hold(jnp.dot(cat([dg0, dg1], axis=1), x, preferred_element_type=F32).astype(BF16))
     r = ROWS
     own = cat([gg[2 * k * r : (2 * k + 1) * r] for k in range(4)])
     theirs = cat([gg[(2 * k + 1) * r : (2 * k + 2) * r] for k in range(4)])
@@ -220,7 +216,7 @@
     )
 
     gw = gw[: gate_weight.shape[0]]
-    gate_grad = jnp.where(side == 0, gw, cat([gw[:, half:], gw[:, :half]], axis=1))
+    gate_grad = jnp.where(on_left, gw, cat([gw[:, half:], gw[:, :half]], axis=1))
     return input_grad, gate_grad
 
 

time: 137 us -> 138 us (level); the launches traced: 134 us -> 138 us
  waiting for transfers between devices: 53 us -> 58.8 us
  starting transfers between devices: 51.8 us -> 49.5 us
  local copies, waits for them, and re-layouts: 4.89 us -> 6.49 us
    ppermute x15, starting transfers between devices: 27.7 us -> 20.5 us  [fetch(): return lax.ppermute(x, PLANE, pairs)]
    ppermute x15, waiting for transfers between devices: 42.3 us -> 47.2 us  [fetch(): return lax.ppermute(x, PLANE, pairs)]
    ppermute x16, starting transfers between devices: 24 us -> 28.9 us  [shift(): return lax.ppermute(x, axis, [(i, (i - by) % n) for i in range(n)])]
    unnamed x24 -> x22, local copies, waits for them, and re-layouts: 4.03 us -> 5.34 us
  transfers between devices with their start and end apart: 31 -> 31, of which waited for: 13 -> 15; matrix products, arithmetic and copies ran while one was open for 5% -> 11% of each run, Pallas kernels for 0% -> 0%
where the time goes in v3:
time: 138 us
  waiting for transfers between devices  58.8 us (43%)
  starting transfers between devices  49.5 us (36%)
  matrix products  16.8 us (12%)
  local copies, waits for them, and re-layouts  6.49 us (5%)
  other arithmetic  4.73 us (3%)
    ppermute x15, waiting for transfers between devices, fetch(): return lax.ppermute(x, PLANE, pairs)  47.2 us
    ppermute x16, starting transfers between devices, shift(): return lax.ppermute(x, axis, [(i, (i - by) % n) for i in range(n)])  28.9 us
    ppermute x15, starting transfers between devices, fetch(): return lax.ppermute(x, PLANE, pairs)  20.5 us
    ppermute x16, waiting for transfers between devices, shift(): return lax.ppermute(x, axis, [(i, (i - by) % n) for i in range(n)])  11.6 us
    dot_general x6, matrix products, rdot(): lax.dot_general(left, right, (((1,), (1,)), ((), ())), preferred_element_...  9.09 us
    unnamed x22, local copies, waits for them, and re-layouts  5.34 us
    dot_general x2, matrix products, input_partials(): lax.dot_general(cat([dgate, dup]), wgu, (((0,), (0,)), ((), ())), preferr...  5.16 us
  transfers between devices with their start and end apart: 31, of which 15 were waited for; matrix products, arithmetic and copies ran while one was open for 11% of the time, Pallas kernels for 0%

profile of v3, /device:TPU:1, one launch (start us, length us, event | category | flops | bytes accessed | tf_op | source)
XLA Modules:
  0.0 138.1 jit_solution(15187892846230407904)
XLA Ops:
  0.6 1.1 broadcast_select_fusion.1
  1.7 1.5 %collective-permute-start.8 = (bf16[128,896]{1,0:T(8,128)(2,1)S(1)}, bf16[128,896]{1,0:T(8,128)(2,1)S(1)}, u32[]{:S(2)}, u32[]{:S(2)}) collective-permute-start(bf16[128,896]{1,0:T(8,128)(2,1)S(1)} %get-tuple-element.98), channel_id=1, source_target_pairs={{0,2},{2,0},{1,3},{3,1},{4,6},{6,4},{5,7},{7,5},{8,10},{10,8},{9,1... | collective-permute-start | bytes 688136 | tf_op jit(solution)/shard_map/ppermute | solution.py:48
  3.2 1.0 copy-done
  4.2 1.0 copy-done.1
  5.1 1.0 copy-done.2
  6.1 0.1 prepare.1
  6.3 2.7 %collective-permute-start.1 = (bf16[240,1792]{1,0:T(8,128)(2,1)S(1)}, bf16[240,1792]{1,0:T(8,128)(2,1)S(1)}, u32[]{:S(2)}, u32[]{:S(2)}) collective-permute-start(bf16[240,1792]{1,0:T(8,128)(2,1)S(1)} %prepare.1), channel_id=1, source_target_pairs={{0,48},{16,0},{32,16},{48,32},{1,49},{17,1},{33,17},{49,33},{2,50}... | collective-permute-start | bytes 2580488 | tf_op jit(solution)/shard_map/ppermute | solution.py:48
  9.0 3.7 %collective-permute-start.11 = (bf16[256,896]{1,0:T(8,128)(2,1)S(1)}, bf16[256,896]{1,0:T(8,128)(2,1)S(1)}, u32[]{:S(2)}, u32[]{:S(2)}) collective-permute-start(bf16[256,896]{1,0:T(8,128)(2,1)S(1)} %pad_maximum_fusion.3), channel_id=1, source_target_pairs={{8,0},{9,1},{66,2},{67,3},{12,4},{13,5},{70,6},{71,7},{0,8},{1,9},... | collective-permute-start | bytes 1376264 | tf_op jit(solution)/shard_map/ppermute | solution.py:43
  12.7 0.5 collective-permute-start.10
  13.2 5.6 %collective-permute-done.11 = bf16[256,896]{1,0:T(8,128)(2,1)S(1)} collective-permute-done((bf16[256,896]{1,0:T(8,128)(2,1)S(1)}, bf16[256,896]{1,0:T(8,128)(2,1)S(1)}, u32[]{:S(2)}, u32[]{:S(2)}) %collective-permute-start.11) | collective-permute-done | bytes 458784 | tf_op jit(solution)/shard_map/ppermute | solution.py:43
  18.9 1.0 collective-permute-start.9
  19.9 3.8 %collective-permute-done.10 = bf16[256,896]{1,0:T(8,128)(2,1)S(1)} collective-permute-done((bf16[256,896]{1,0:T(8,128)(2,1)S(1)}, bf16[256,896]{1,0:T(8,128)(2,1)S(1)}, u32[]{:S(2)}, u32[]{:S(2)}) %collective-permute-start.10) | collective-permute-done | bytes 458784 | tf_op jit(solution)/shard_map/ppermute | solution.py:43
  23.8 2.7 %collective-permute-done.9 = bf16[256,896]{1,0:T(8,128)(2,1)S(1)} collective-permute-done((bf16[256,896]{1,0:T(8,128)(2,1)S(1)}, bf16[256,896]{1,0:T(8,128)(2,1)S(1)}, u32[]{:S(2)}, u32[]{:S(2)}) %collective-permute-start.9) | collective-permute-done | bytes 458784 | tf_op jit(solution)/shard_map/ppermute | solution.py:43
  26.6 2.8 %collective-permute-start.12 = (bf16[512,896]{1,0:T(8,128)(2,1)S(1)}, bf16[512,896]{1,0:T(8,128)(2,1)S(1)}, u32[]{:S(2)}, u32[]{:S(2)}) collective-permute-start(bf16[512,896]{1,0:T(8,128)(2,1)S(1)} %pad_maximum_fusion.1.m0), channel_id=1, source_target_pairs={{1,0},{0,1},{6,2},{7,3},{5,4},{4,5},{10,6},{11,7},{9,8},{8,9},{14,... | collective-permute-start | bytes 2752520 | tf_op jit(solution)/shard_map/ppermute | solution.py:43
  29.6 2.7 %collective-permute-start.6 = (bf16[128,1792]{1,0:T(8,128)(2,1)S(1)}, bf16[128,1792]{1,0:T(8,128)(2,1)S(1)}, u32[]{:S(2)}, u32[]{:S(2)}) collective-permute-start(bf16[128,1792]{1,0:T(8,128)(2,1)S(1)} %slice.340), channel_id=1, source_target_pairs={{0,48},{16,0},{32,16},{48,32},{1,49},{17,1},{33,17},{49,33},{2,50}... | collective-permute-start | bytes 1376264 | tf_op jit(solution)/shard_map/ppermute | solution.py:48
  32.4 4.6 %collective-permute-start.2 = (bf16[240,1792]{1,0:T(8,128)(2,1)S(1)}, bf16[240,1792]{1,0:T(8,128)(2,1)S(1)}, u32[]{:S(2)}, u32[]{:S(2)}) collective-permute-start(bf16[240,1792]{1,0:T(8,128)(2,1)S(1)} %collective-permute-done.1), channel_id=1, source_target_pairs={{0,2},{2,0},{1,3},{3,1},{4,6},{6,4},{5,7},{7,5},{8,10},{10,8},{9,1... | collective-permute-start | bytes 2580488 | tf_op jit(solution)/shard_map/ppermute | solution.py:48
  37.1 1.0 slice_dynamic-update-slice_fusion.14
  38.1 5.0 %collective-permute-start.15 = (bf16[512,896]{1,0:T(8,128)(2,1)S(1)}, bf16[512,896]{1,0:T(8,128)(2,1)S(1)}, u32[]{:S(2)}, u32[]{:S(2)}) collective-permute-start(bf16[512,896]{1,0:T(8,128)(2,1)S(1)} %pad_maximum_fusion.2), channel_id=1, source_target_pairs={{0,2},{2,0},{1,3},{3,1},{4,6},{6,4},{5,7},{7,5},{8,10},{10,8},{9,1... | collective-permute-start | bytes 2752520 | tf_op jit(solution)/shard_map/ppermute | solution.py:48
  43.1 0.6 collective-permute-start.18
  43.8 5.1 %collective-permute-start.4 = (bf16[240,1792]{1,0:T(8,128)(2,1)S(1)}, bf16[240,1792]{1,0:T(8,128)(2,1)S(1)}, u32[]{:S(2)}, u32[]{:S(2)}) collective-permute-start(bf16[240,1792]{1,0:T(8,128)(2,1)S(1)} %collective-permute-done.3), channel_id=1, source_target_pairs={{0,2},{2,0},{1,3},{3,1},{4,6},{6,4},{5,7},{7,5},{8,10},{10,8},{9,1... | collective-permute-start | bytes 2580488 | tf_op jit(solution)/shard_map/ppermute | solution.py:48
  48.9 2.0 %collective-permute-done.4 = bf16[240,1792]{1,0:T(8,128)(2,1)S(1)} collective-permute-done((bf16[240,1792]{1,0:T(8,128)(2,1)S(1)}, bf16[240,1792]{1,0:T(8,128)(2,1)S(1)}, u32[]{:S(2)}, u32[]{:S(2)}) %collective-permute-start.4) | collective-permute-done | bytes 860192 | tf_op jit(solution)/shard_map/ppermute | solution.py:48
  50.9 0.4 collective-permute-start.7
  51.3 6.2 %collective-permute-done.18 = bf16[512,896]{1,0:T(8,128)(2,1)S(1)} collective-permute-done((bf16[512,896]{1,0:T(8,128)(2,1)S(1)}, bf16[512,896]{1,0:T(8,128)(2,1)S(1)}, u32[]{:S(2)}, u32[]{:S(2)}) %collective-permute-start.18) | collective-permute-done | bytes 917536 | tf_op jit(solution)/shard_map/ppermute | solution.py:43
  57.5 1.5 %collective-permute-start.16 = (bf16[512,896]{1,0:T(8,128)(2,1)S(1)}, bf16[512,896]{1,0:T(8,128)(2,1)S(1)}, u32[]{:S(2)}, u32[]{:S(2)}) collective-permute-start(bf16[512,896]{1,0:T(8,128)(2,1)S(1)} %pad_maximum_fusion.2), channel_id=1, source_target_pairs={{1,0},{0,1},{6,2},{7,3},{5,4},{4,5},{10,6},{11,7},{9,8},{8,9},{14,... | collective-permute-start | bytes 2752520 | tf_op jit(solution)/shard_map/ppermute | solution.py:43
  58.9 1.7 %collective-permute-start.19 = (bf16[512,896]{1,0:T(8,128)(2,1)S(1)}, bf16[512,896]{1,0:T(8,128)(2,1)S(1)}, u32[]{:S(2)}, u32[]{:S(2)}) collective-permute-start(bf16[512,896]{1,0:T(8,128)(2,1)S(1)} %collective-permute-done.18), channel_id=1, source_target_pairs={{0,2},{2,0},{1,3},{3,1},{4,6},{6,4},{5,7},{7,5},{8,10},{10,8},{9,1... | collective-permute-start | bytes 2752520 | tf_op jit(solution)/shard_map/ppermute | solution.py:48
  60.7 1.1 slice_dynamic-update-slice_fusion.22
  62.0 0.7 collective-permute-start.20
  62.7 2.8 %collective-permute-start.14 = (bf16[512,896]{1,0:T(8,128)(2,1)S(1)}, bf16[512,896]{1,0:T(8,128)(2,1)S(1)}, u32[]{:S(2)}, u32[]{:S(2)}) collective-permute-start(bf16[512,896]{1,0:T(8,128)(2,1)S(1)} %collective-permute-done.12.m1), channel_id=1, source_target_pairs={{65,0},{64,1},{6,2},{7,3},{69,4},{68,5},{10,6},{11,7},{73,8},{72,9... | collective-permute-start | bytes 2752520 | tf_op jit(solution)/shard_map/ppermute | solution.py:43
  65.6 4.4 %collective-permute-done.16 = bf16[512,896]{1,0:T(8,128)(2,1)S(1)} collective-permute-done((bf16[512,896]{1,0:T(8,128)(2,1)S(1)}, bf16[512,896]{1,0:T(8,128)(2,1)S(1)}, u32[]{:S(2)}, u32[]{:S(2)}) %collective-permute-start.16) | collective-permute-done | bytes 917536 | tf_op jit(solution)/shard_map/ppermute | solution.py:43
  70.0 4.0 %collective-permute-start.17 = (bf16[512,896]{1,0:T(8,128)(2,1)S(1)}, bf16[512,896]{1,0:T(8,128)(2,1)S(1)}, u32[]{:S(2)}, u32[]{:S(2)}) collective-permute-start(bf16[512,896]{1,0:T(8,128)(2,1)S(1)} %collective-permute-done.16), channel_id=1, source_target_pairs={{0,2},{2,0},{1,3},{3,1},{4,6},{6,4},{5,7},{7,5},{8,10},{10,8},{9,1... | collective-permute-start | bytes 2752520 | tf_op jit(solution)/shard_map/ppermute | solution.py:48
  74.1 5.4 %collective-permute-done.14.m3 = bf16[512,896]{1,0:T(8,128)(2,1)S(1)} collective-permute-done((bf16[512,896]{1,0:T(8,128)(2,1)S(1)}, bf16[512,896]{1,0:T(8,128)(2,1)S(1)}, u32[]{:S(2)}, u32[]{:S(2)}) %collective-permute-start.14) | collective-permute-done | bytes 917536 | tf_op jit(solution)/shard_map/ppermute | solution.py:43
  79.5 3.6 %collective-permute-done.20.r3 = bf16[512,896]{1,0:T(8,128)(2,1)S(1)} collective-permute-done((bf16[512,896]{1,0:T(8,128)(2,1)S(1)}, bf16[512,896]{1,0:T(8,128)(2,1)S(1)}, u32[]{:S(2)}, u32[]{:S(2)}) %collective-permute-start.20) | collective-permute-done | bytes 917536 | tf_op jit(solution)/shard_map/ppermute | solution.py:43
  83.2 0.7 assemble.1
  83.9 1.4 fusion.2
  85.3 1.5 %multiply_convert_fusion.1 = (bf16[640,512]{1,0:T(8,128)(2,1)S(1)}, f32[640,512]{1,0:T(8,128)S(1)}) fusion(f32[640,512]{1,0:T(8,128)S(1)} %fusion.2, bf16[640,1792]{1,0:T(8,128)(2,1)S(1)} %get-tuple-element.75, bf16[1024,1792]{1,0:T(8,128)(2,1)S(1)} %get-tuple-element.25), kind=kOutput, calls=%fused_computation.36 | convolution fusion | flops 1176371200 | bytes 7405568 | tf_op jit(solution)/shard_map/dot_general | solution.py:52
  86.8 1.7 %fusion.36 = bf16[640,512]{1,0:T(8,128)(2,1)S(1)} fusion(f32[640,512]{1,0:T(8,128)S(1)} %get-tuple-element.102, bf16[1024,1792]{1,0:T(8,128)(2,1)S(1)} %get-tuple-element.24, bf16[1280,1792]{1,0:T(8,128)(2,1)S(1)} %get-tuple-element.76, f32[640,512]{1,0:T(8,128)S(1)} %fusion.2), kind=kOutput, calls=%fused_computation.23 | convolution fusion | flops 1177681920 | bytes 7405568 | tf_op jit(solution)/shard_map/dot_general | solution.py:52
  88.5 2.6 %convolution_convert_fusion.2 = bf16[512,1792]{1,0:T(8,128)(2,1)S(1)} fusion(bf16[1280,1792]{1,0:T(8,128)(2,1)S(1)} %get-tuple-element.76, bf16[640,512]{1,0:T(8,128)(2,1)S(1)} %get-tuple-element.27, bf16[640,512]{1,0:T(8,128)(2,1)S(1)} %fusion.36), kind=kOutput, calls=%fused_computation.2 | convolution fusion | flops 2352349184 | bytes 7733248 | tf_op jit(solution)/shard_map/dot_general | solution.py:178
  91.5 0.4 slice_select_fusion.2
  91.9 2.6 %collective-permute-start.23 = (bf16[512,896]{1,0:T(8,128)(2,1)S(1)}, bf16[512,896]{1,0:T(8,128)(2,1)S(1)}, u32[]{:S(2)}, u32[]{:S(2)}) collective-permute-start(bf16[512,896]{1,0:T(8,128)(2,1)S(1)} %get-tuple-element.28), channel_id=1, source_target_pairs={{64,0},{65,1},{10,2},{11,3},{68,4},{69,5},{14,6},{15,7},{72,8},{73... | collective-permute-start | bytes 2752520 | tf_op jit(solution)/shard_map/ppermute | solution.py:43
  94.5 1.2 collective-permute-start.22
  95.7 1.4 fusion
  97.1 1.5 %multiply_convert_fusion = (bf16[640,512]{1,0:T(8,128)(2,1)S(1)}, f32[640,512]{1,0:T(8,128)S(1)}) fusion(f32[640,512]{1,0:T(8,128)S(1)} %fusion, bf16[640,1792]{1,0:T(8,128)(2,1)S(1)} %get-tuple-element.75, bf16[512,1792]{1,0:T(8,128)(2,1)S(1)} %slice.276), kind=kOutput, calls=%fused_computation.34 | convolution fusion | flops 1176371200 | bytes 7405568 | tf_op jit(solution)/shard_map/dot_general | solution.py:52
  98.6 1.7 %fusion.41 = bf16[640,512]{1,0:T(8,128)(2,1)S(1)} fusion(f32[640,512]{1,0:T(8,128)S(1)} %get-tuple-element.104, bf16[512,1792]{1,0:T(8,128)(2,1)S(1)} %slice.275, bf16[1280,1792]{1,0:T(8,128)(2,1)S(1)} %get-tuple-element.76, f32[640,512]{1,0:T(8,128)S(1)} %fusion), kind=kOutput, calls=%fused_computation.24 | convolution fusion | flops 1177681920 | bytes 7405568 | tf_op jit(solution)/shard_map/dot_general | solution.py:52
  100.3 2.6 %convolution_convert_fusion.1 = bf16[512,1792]{1,0:T(8,128)(2,1)S(1)} fusion(bf16[1280,1792]{1,0:T(8,128)(2,1)S(1)} %get-tuple-element.76, bf16[640,512]{1,0:T(8,128)(2,1)S(1)} %get-tuple-element.33, bf16[640,512]{1,0:T(8,128)(2,1)S(1)} %fusion.41), kind=kOutput, calls=%fused_computation.1 | convolution fusion | flops 2352349184 | bytes 7733248 | tf_op jit(solution)/shard_map/dot_general | solution.py:178
  103.0 0.4 slice_select_fusion
  103.5 0.3 collective-permute-start.21
  103.8 2.5 %convolution_convert_fusion = bf16[640,1792]{1,0:T(8,128)(2,1)S(1)} fusion(bf16[1024,1792]{1,0:T(8,128)(2,1)S(1)} %get-tuple-element.24, bf16[640,512]{1,0:T(8,128)(2,1)S(1)} %fusion.36, bf16[640,512]{1,0:T(8,128)(2,1)S(1)} %fusion.41), kind=kOutput, calls=%fused_computation | convolution fusion | flops 2352578560 | bytes 7274496 | tf_op jit(solution)/shard_map/dot_general | solution.py:199
  106.4 0.2 fusion.56
  106.7 9.9 %collective-permute-done.22 = bf16[512,896]{1,0:T(8,128)(2,1)S(1)} collective-permute-done((bf16[512,896]{1,0:T(8,128)(2,1)S(1)}, bf16[512,896]{1,0:T(8,128)(2,1)S(1)}, u32[]{:S(2)}, u32[]{:S(2)}) %collective-permute-start.22) | collective-permute-done | bytes 917536 | tf_op jit(solution)/shard_map/ppermute | solution.py:43
  116.6 0.4 collective-permute-done.21
  117.0 0.5 add_convert_fusion.1
  117.5 1.2 collective-permute-start.26
  118.7 1.0 collective-permute-start.25
  119.7 0.5 collective-permute-start.24
  120.3 0.3 add_convert_fusion
  120.7 0.9 collective-permute-start.29
  121.7 2.4 %collective-permute-done.26 = bf16[128,896]{1,0:T(8,128)(2,1)S(1)} collective-permute-done((bf16[128,896]{1,0:T(8,128)(2,1)S(1)}, bf16[128,896]{1,0:T(8,128)(2,1)S(1)}, u32[]{:S(2)}, u32[]{:S(2)}) %collective-permute-start.26) | collective-permute-done | bytes 229408 | tf_op jit(solution)/shard_map/ppermute | solution.py:43
  124.1 2.6 %collective-permute-done.25 = bf16[128,896]{1,0:T(8,128)(2,1)S(1)} collective-permute-done((bf16[128,896]{1,0:T(8,128)(2,1)S(1)}, bf16[128,896]{1,0:T(8,128)(2,1)S(1)}, u32[]{:S(2)}, u32[]{:S(2)}) %collective-permute-start.25) | collective-permute-done | bytes 229408 | tf_op jit(solution)/shard_map/ppermute | solution.py:43
  126.7 0.8 add_convert_fusion.3
  127.6 1.8 %collective-permute-done.30 = bf16[80,1792]{1,0:T(8,128)(2,1)S(1)} collective-permute-done((bf16[80,1792]{1,0:T(8,128)(2,1)S(1)}, bf16[80,1792]{1,0:T(8,128)(2,1)S(1)}, u32[]{:S(2)}, u32[]{:S(2)}) %collective-permute-start.30) | collective-permute-done | bytes 286752 | tf_op jit(solution)/shard_map/ppermute | solution.py:48
  129.3 5.2 %collective-permute-done.29 = bf16[80,1792]{1,0:T(8,128)(2,1)S(1)} collective-permute-done((bf16[80,1792]{1,0:T(8,128)(2,1)S(1)}, bf16[80,1792]{1,0:T(8,128)(2,1)S(1)}, u32[]{:S(2)}, u32[]{:S(2)}) %collective-permute-start.29) | collective-permute-done | bytes 286752 | tf_op jit(solution)/shard_map/ppermute | solution.py:48
  134.5 2.6 %collective-permute-done.28 = bf16[80,1792]{1,0:T(8,128)(2,1)S(1)} collective-permute-done((bf16[80,1792]{1,0:T(8,128)(2,1)S(1)}, bf16[80,1792]{1,0:T(8,128)(2,1)S(1)}, u32[]{:S(2)}, u32[]{:S(2)}) %collective-permute-start.28) | collective-permute-done | bytes 286752 | tf_op jit(solution)/shard_map/ppermute | solution.py:48
  137.2 0.1 add_convert_fusion.2
  137.3 0.8 slice_select_fusion.4
  (61 shorter events, 2.1 us)
Async XLA Ops:
  1.7 7.2 %collective-permute-start.8 = (bf16[128,896]{1,0:T(8,128)(2,1)S(1)}, bf16[128,896]{1,0:T(8,128)(2,1)S(1)}, u32[]{:S(2)}, u32[]{:S(2)}) collective-permute-start(bf16[128,896]{1,0:T(8,128)(2,1)S(1)} %get-tuple-element.98), channel_id=1, source_target_pairs={{0,2},{2,0},{1,3},{3,1},{4,6},{6,4},{5,7},{7,5},{8,10},{10,8},{9,1... | collective-permute-start | bytes 688136 | tf_op jit(solution)/shard_map/ppermute | solution.py:48
  3.2 1.0 copy-start
  4.2 1.0 copy-start.1
  5.1 1.0 copy-start.2
  6.2 26.2 %collective-permute-start = (bf16[240,1792]{1,0:T(8,128)(2,1)S(1)}, bf16[240,1792]{1,0:T(8,128)(2,1)}, u32[]{:S(2)}, u32[]{:S(2)}) collective-permute-start(bf16[240,1792]{1,0:T(8,128)(2,1)S(1)} %prepare.1), channel_id=1, source_target_pairs={{0,2},{2,0},{1,3},{3,1},{4,6},{6,4},{5,7},{7,5},{8,10},{10,8},{9,1... | collective-permute-start | bytes 2580488 | tf_op jit(solution)/shard_map/ppermute | solution.py:48
  6.3 23.2 %collective-permute-start.1 = (bf16[240,1792]{1,0:T(8,128)(2,1)S(1)}, bf16[240,1792]{1,0:T(8,128)(2,1)S(1)}, u32[]{:S(2)}, u32[]{:S(2)}) collective-permute-start(bf16[240,1792]{1,0:T(8,128)(2,1)S(1)} %prepare.1), channel_id=1, source_target_pairs={{0,48},{16,0},{32,16},{48,32},{1,49},{17,1},{33,17},{49,33},{2,50}... | collective-permute-start | bytes 2580488 | tf_op jit(solution)/shard_map/ppermute | solution.py:48
  9.0 23.4 %collective-permute-start.3 = (bf16[240,1792]{1,0:T(8,128)(2,1)S(1)}, bf16[240,1792]{1,0:T(8,128)(2,1)S(1)}, u32[]{:S(2)}, u32[]{:S(2)}) collective-permute-start(bf16[240,1792]{1,0:T(8,128)(2,1)S(1)} %prepare.1), channel_id=1, source_target_pairs={{0,16},{16,32},{32,48},{48,0},{1,17},{17,33},{33,49},{49,1},{2,18}... | collective-permute-start | bytes 2580488 | tf_op jit(solution)/shard_map/ppermute | solution.py:48
  9.0 9.9 %collective-permute-start.11 = (bf16[256,896]{1,0:T(8,128)(2,1)S(1)}, bf16[256,896]{1,0:T(8,128)(2,1)S(1)}, u32[]{:S(2)}, u32[]{:S(2)}) collective-permute-start(bf16[256,896]{1,0:T(8,128)(2,1)S(1)} %pad_maximum_fusion.3), channel_id=1, source_target_pairs={{8,0},{9,1},{66,2},{67,3},{12,4},{13,5},{70,6},{71,7},{0,8},{1,9},... | collective-permute-start | bytes 1376264 | tf_op jit(solution)/shard_map/ppermute | solution.py:43
  12.7 11.1 %collective-permute-start.10 = (bf16[256,896]{1,0:T(8,128)(2,1)S(1)}, bf16[256,896]{1,0:T(8,128)(2,1)S(1)}, u32[]{:S(2)}, u32[]{:S(2)}) collective-permute-start(bf16[256,896]{1,0:T(8,128)(2,1)S(1)} %pad_maximum_fusion.3), channel_id=1, source_target_pairs={{12,0},{13,1},{67,2},{66,3},{0,4},{1,5},{71,6},{70,7},{4,8},{5,9},... | collective-permute-start | bytes 1376264 | tf_op jit(solution)/shard_map/ppermute | solution.py:43
  18.9 7.6 %collective-permute-start.9 = (bf16[256,896]{1,0:T(8,128)(2,1)S(1)}, bf16[256,896]{1,0:T(8,128)(2,1)S(1)}, u32[]{:S(2)}, u32[]{:S(2)}) collective-permute-start(bf16[256,896]{1,0:T(8,128)(2,1)S(1)} %pad_maximum_fusion.3), channel_id=1, source_target_pairs={{4,0},{5,1},{3,2},{2,3},{8,4},{9,5},{7,6},{6,7},{12,8},{13,9},{11,... | collective-permute-start | bytes 1376264 | tf_op jit(solution)/shard_map/ppermute | solution.py:43
  26.6 35.4 %collective-permute-start.12 = (bf16[512,896]{1,0:T(8,128)(2,1)S(1)}, bf16[512,896]{1,0:T(8,128)(2,1)S(1)}, u32[]{:S(2)}, u32[]{:S(2)}) collective-permute-start(bf16[512,896]{1,0:T(8,128)(2,1)S(1)} %pad_maximum_fusion.1.m0), channel_id=1, source_target_pairs={{1,0},{0,1},{6,2},{7,3},{5,4},{4,5},{10,6},{11,7},{9,8},{8,9},{14,... | collective-permute-start | bytes 2752520 | tf_op jit(solution)/shard_map/ppermute | solution.py:43
  29.4 33.3 %collective-permute-start.13 = (bf16[512,896]{1,0:T(8,128)(2,1)S(1)}, bf16[512,896]{1,0:T(8,128)(2,1)S(1)}, u32[]{:S(2)}, u32[]{:S(2)}) collective-permute-start(bf16[512,896]{1,0:T(8,128)(2,1)S(1)} %pad_maximum_fusion.1.m0), channel_id=1, source_target_pairs={{65,0},{64,1},{14,2},{15,3},{69,4},{68,5},{2,6},{3,7},{73,8},{72,9... | collective-permute-start | bytes 2752520 | tf_op jit(solution)/shard_map/ppermute | solution.py:43
  29.6 8.5 %collective-permute-start.6 = (bf16[128,1792]{1,0:T(8,128)(2,1)S(1)}, bf16[128,1792]{1,0:T(8,128)(2,1)S(1)}, u32[]{:S(2)}, u32[]{:S(2)}) collective-permute-start(bf16[128,1792]{1,0:T(8,128)(2,1)S(1)} %slice.340), channel_id=1, source_target_pairs={{0,48},{16,0},{32,16},{48,32},{1,49},{17,1},{33,17},{49,33},{2,50}... | collective-permute-start | bytes 1376264 | tf_op jit(solution)/shard_map/ppermute | solution.py:48
  32.4 10.7 %collective-permute-start.5 = (bf16[112,1792]{1,0:T(8,128)(2,1)S(1)}, bf16[112,1792]{1,0:T(8,128)(2,1)S(1)}, u32[]{:S(2)}, u32[]{:S(2)}) collective-permute-start(bf16[112,1792]{1,0:T(8,128)(2,1)S(1)} %slice.338), channel_id=1, source_target_pairs={{0,16},{16,32},{32,48},{48,0},{1,17},{17,33},{33,49},{49,1},{2,18}... | collective-permute-start | bytes 1204232 | tf_op jit(solution)/shard_map/ppermute | solution.py:48
  32.4 11.3 %collective-permute-start.2 = (bf16[240,1792]{1,0:T(8,128)(2,1)S(1)}, bf16[240,1792]{1,0:T(8,128)(2,1)S(1)}, u32[]{:S(2)}, u32[]{:S(2)}) collective-permute-start(bf16[240,1792]{1,0:T(8,128)(2,1)S(1)} %collective-permute-done.1), channel_id=1, source_target_pairs={{0,2},{2,0},{1,3},{3,1},{4,6},{6,4},{5,7},{7,5},{8,10},{10,8},{9,1... | collective-permute-start | bytes 2580488 | tf_op jit(solution)/shard_map/ppermute | solution.py:48
  38.1 36.0 %collective-permute-start.15 = (bf16[512,896]{1,0:T(8,128)(2,1)S(1)}, bf16[512,896]{1,0:T(8,128)(2,1)S(1)}, u32[]{:S(2)}, u32[]{:S(2)}) collective-permute-start(bf16[512,896]{1,0:T(8,128)(2,1)S(1)} %pad_maximum_fusion.2), channel_id=1, source_target_pairs={{0,2},{2,0},{1,3},{3,1},{4,6},{6,4},{5,7},{7,5},{8,10},{10,8},{9,1... | collective-permute-start | bytes 2752520 | tf_op jit(solution)/shard_map/ppermute | solution.py:48
  43.1 14.4 %collective-permute-start.18 = (bf16[512,896]{1,0:T(8,128)(2,1)S(1)}, bf16[512,896]{1,0:T(8,128)(2,1)S(1)}, u32[]{:S(2)}, u32[]{:S(2)}) collective-permute-start(bf16[512,896]{1,0:T(8,128)(2,1)S(1)} %pad_maximum_fusion.2), channel_id=1, source_target_pairs={{65,0},{64,1},{14,2},{15,3},{69,4},{68,5},{2,6},{3,7},{73,8},{72,9... | collective-permute-start | bytes 2752520 | tf_op jit(solution)/shard_map/ppermute | solution.py:43
  43.8 7.1 %collective-permute-start.4 = (bf16[240,1792]{1,0:T(8,128)(2,1)S(1)}, bf16[240,1792]{1,0:T(8,128)(2,1)S(1)}, u32[]{:S(2)}, u32[]{:S(2)}) collective-permute-start(bf16[240,1792]{1,0:T(8,128)(2,1)S(1)} %collective-permute-done.3), channel_id=1, source_target_pairs={{0,2},{2,0},{1,3},{3,1},{4,6},{6,4},{5,7},{7,5},{8,10},{10,8},{9,1... | collective-permute-start | bytes 2580488 | tf_op jit(solution)/shard_map/ppermute | solution.py:48
  50.9 8.0 %collective-permute-start.7 = (bf16[240,1792]{1,0:T(8,128)(2,1)S(1)}, bf16[240,1792]{1,0:T(8,128)(2,1)S(1)}, u32[]{:S(2)}, u32[]{:S(2)}) collective-permute-start(bf16[240,1792]{1,0:T(8,128)(2,1)S(1)} %constant_dynamic-update-slice_fusion), channel_id=1, source_target_pairs={{0,2},{2,0},{1,3},{3,1},{4,6},{6,4},{5,7},{7,5},{8,10},{10,8},{9,1... | collective-permute-start | bytes 2580488 | tf_op jit(solution)/shard_map/ppermute | solution.py:48
  57.5 12.5 %collective-permute-start.16 = (bf16[512,896]{1,0:T(8,128)(2,1)S(1)}, bf16[512,896]{1,0:T(8,128)(2,1)S(1)}, u32[]{:S(2)}, u32[]{:S(2)}) collective-permute-start(bf16[512,896]{1,0:T(8,128)(2,1)S(1)} %pad_maximum_fusion.2), channel_id=1, source_target_pairs={{1,0},{0,1},{6,2},{7,3},{5,4},{4,5},{10,6},{11,7},{9,8},{8,9},{14,... | collective-permute-start | bytes 2752520 | tf_op jit(solution)/shard_map/ppermute | solution.py:43
  58.9 20.6 %collective-permute-start.19 = (bf16[512,896]{1,0:T(8,128)(2,1)S(1)}, bf16[512,896]{1,0:T(8,128)(2,1)S(1)}, u32[]{:S(2)}, u32[]{:S(2)}) collective-permute-start(bf16[512,896]{1,0:T(8,128)(2,1)S(1)} %collective-permute-done.18), channel_id=1, source_target_pairs={{0,2},{2,0},{1,3},{3,1},{4,6},{6,4},{5,7},{7,5},{8,10},{10,8},{9,1... | collective-permute-start | bytes 2752520 | tf_op jit(solution)/shard_map/ppermute | solution.py:48
  62.0 21.2 %collective-permute-start.20 = (bf16[512,896]{1,0:T(8,128)(2,1)S(1)}, bf16[512,896]{1,0:T(8,128)(2,1)S(1)}, u32[]{:S(2)}, u32[]{:S(2)}) collective-permute-start(bf16[512,896]{1,0:T(8,128)(2,1)S(1)} %collective-permute-done.18), channel_id=1, source_target_pairs={{14,0},{15,1},{1,2},{0,3},{2,4},{3,5},{5,6},{4,7},{6,8},{7,9},{9,1... | collective-permute-start | bytes 2752520 | tf_op jit(solution)/shard_map/ppermute | solution.py:43
  62.7 16.8 %collective-permute-start.14 = (bf16[512,896]{1,0:T(8,128)(2,1)S(1)}, bf16[512,896]{1,0:T(8,128)(2,1)S(1)}, u32[]{:S(2)}, u32[]{:S(2)}) collective-permute-start(bf16[512,896]{1,0:T(8,128)(2,1)S(1)} %collective-permute-done.12.m1), channel_id=1, source_target_pairs={{65,0},{64,1},{6,2},{7,3},{69,4},{68,5},{10,6},{11,7},{73,8},{72,9... | collective-permute-start | bytes 2752520 | tf_op jit(solution)/shard_map/ppermute | solution.py:43
  70.0 9.5 %collective-permute-start.17 = (bf16[512,896]{1,0:T(8,128)(2,1)S(1)}, bf16[512,896]{1,0:T(8,128)(2,1)S(1)}, u32[]{:S(2)}, u32[]{:S(2)}) collective-permute-start(bf16[512,896]{1,0:T(8,128)(2,1)S(1)} %collective-permute-done.16), channel_id=1, source_target_pairs={{0,2},{2,0},{1,3},{3,1},{4,6},{6,4},{5,7},{7,5},{8,10},{10,8},{9,1... | collective-permute-start | bytes 2752520 | tf_op jit(solution)/shard_map/ppermute | solution.py:48
  91.9 14.8 %collective-permute-start.23 = (bf16[512,896]{1,0:T(8,128)(2,1)S(1)}, bf16[512,896]{1,0:T(8,128)(2,1)S(1)}, u32[]{:S(2)}, u32[]{:S(2)}) collective-permute-start(bf16[512,896]{1,0:T(8,128)(2,1)S(1)} %get-tuple-element.28), channel_id=1, source_target_pairs={{64,0},{65,1},{10,2},{11,3},{68,4},{69,5},{14,6},{15,7},{72,8},{73... | collective-permute-start | bytes 2752520 | tf_op jit(solution)/shard_map/ppermute | solution.py:43
  94.5 22.2 %collective-permute-start.22 = (bf16[512,896]{1,0:T(8,128)(2,1)S(1)}, bf16[512,896]{1,0:T(8,128)(2,1)S(1)}, u32[]{:S(2)}, u32[]{:S(2)}) collective-permute-start(bf16[512,896]{1,0:T(8,128)(2,1)S(1)} %get-tuple-element.29), channel_id=1, source_target_pairs={{65,0},{64,1},{6,2},{7,3},{69,4},{68,5},{10,6},{11,7},{73,8},{72,9... | collective-permute-start | bytes 2752520 | tf_op jit(solution)/shard_map/ppermute | solution.py:43
  103.5 13.5 %collective-permute-start.21 = (bf16[512,896]{1,0:T(8,128)(2,1)S(1)}, bf16[512,896]{1,0:T(8,128)(2,1)S(1)}, u32[]{:S(2)}, u32[]{:S(2)}) collective-permute-start(bf16[512,896]{1,0:T(8,128)(2,1)S(1)} %get-tuple-element.35), channel_id=1, source_target_pairs={{1,0},{0,1},{14,2},{15,3},{5,4},{4,5},{2,6},{3,7},{9,8},{8,9},{6,1... | collective-permute-start | bytes 2752520 | tf_op jit(solution)/shard_map/ppermute | solution.py:43
  106.6 13.7 %collective-permute-start.27 = (bf16[320,1792]{1,0:T(8,128)(2,1)S(1)}, bf16[320,1792]{1,0:T(8,128)(2,1)S(1)}, u32[]{:S(2)}, u32[]{:S(2)}) collective-permute-start(bf16[320,1792]{1,0:T(8,128)(2,1)S(1)} %pad_maximum_fusion), channel_id=1, source_target_pairs={{0,2},{2,0},{1,3},{3,1},{4,6},{6,4},{5,7},{7,5},{8,10},{10,8},{9,1... | collective-permute-start | bytes 3440648 | tf_op jit(solution)/shard_map/ppermute | solution.py:48
  117.5 6.6 %collective-permute-start.26 = (bf16[128,896]{1,0:T(8,128)(2,1)S(1)}, bf16[128,896]{1,0:T(8,128)(2,1)S(1)}, u32[]{:S(2)}, u32[]{:S(2)}) collective-permute-start(bf16[128,896]{1,0:T(8,128)(2,1)S(1)} %get-tuple-element.40), channel_id=1, source_target_pairs={{8,0},{9,1},{66,2},{67,3},{12,4},{13,5},{70,6},{71,7},{0,8},{1,9},... | collective-permute-start | bytes 688136 | tf_op jit(solution)/shard_map/ppermute | solution.py:43
  118.7 8.0 %collective-permute-start.25 = (bf16[128,896]{1,0:T(8,128)(2,1)S(1)}, bf16[128,896]{1,0:T(8,128)(2,1)S(1)}, u32[]{:S(2)}, u32[]{:S(2)}) collective-permute-start(bf16[128,896]{1,0:T(8,128)(2,1)S(1)} %get-tuple-element.39), channel_id=1, source_target_pairs={{4,0},{5,1},{67,2},{66,3},{8,4},{9,5},{71,6},{70,7},{12,8},{13,9},... | collective-permute-start | bytes 688136 | tf_op jit(solution)/shard_map/ppermute | solution.py:43
  119.7 7.0 %collective-permute-start.24 = (bf16[128,896]{1,0:T(8,128)(2,1)S(1)}, bf16[128,896]{1,0:T(8,128)(2,1)S(1)}, u32[]{:S(2)}, u32[]{:S(2)}) collective-permute-start(bf16[128,896]{1,0:T(8,128)(2,1)S(1)} %get-tuple-element.38), channel_id=1, source_target_pairs={{12,0},{13,1},{3,2},{2,3},{0,4},{1,5},{7,6},{6,7},{4,8},{5,9},{11,... | collective-permute-start | bytes 688136 | tf_op jit(solution)/shard_map/ppermute | solution.py:43
  120.6 8.7 %collective-permute-start.30 = (bf16[80,1792]{1,0:T(8,128)(2,1)S(1)}, bf16[80,1792]{1,0:T(8,128)(2,1)S(1)}, u32[]{:S(2)}, u32[]{:S(2)}) collective-permute-start(bf16[80,1792]{1,0:T(8,128)(2,1)S(1)} %get-tuple-element.69), channel_id=1, source_target_pairs={{0,32},{16,48},{32,0},{48,16},{1,33},{17,49},{33,1},{49,17},{2,34}... | collective-permute-start | bytes 860168 | tf_op jit(solution)/shard_map/ppermute | solution.py:48
  120.7 13.8 %collective-permute-start.29 = (bf16[80,1792]{1,0:T(8,128)(2,1)S(1)}, bf16[80,1792]{1,0:T(8,128)(2,1)S(1)}, u32[]{:S(2)}, u32[]{:S(2)}) collective-permute-start(bf16[80,1792]{1,0:T(8,128)(2,1)S(1)} %get-tuple-element.70), channel_id=1, source_target_pairs={{0,48},{16,0},{32,16},{48,32},{1,49},{17,1},{33,17},{49,33},{2,50}... | collective-permute-start | bytes 860168 | tf_op jit(solution)/shard_map/ppermute | solution.py:48
  124.1 13.1 %collective-permute-start.28 = (bf16[80,1792]{1,0:T(8,128)(2,1)S(1)}, bf16[80,1792]{1,0:T(8,128)(2,1)S(1)}, u32[]{:S(2)}, u32[]{:S(2)}) collective-permute-start(bf16[80,1792]{1,0:T(8,128)(2,1)S(1)} %get-tuple-element.68), channel_id=1, source_target_pairs={{0,16},{16,32},{32,48},{48,0},{1,17},{17,33},{33,49},{49,1},{2,18}... | collective-permute-start | bytes 860168 | tf_op jit(solution)/shard_map/ppermute | solution.py:48

commit v4 on v3

--- a/solution.py
+++ b/solution.py
@@ -192,16 +192,18 @@
     got_back = fetch(back_part, "Q", "y+")
     x0, c0, far_part, back_part = hold((x0, c0, far_part, back_part))
     dg0, du0 = hidden_grads(x0, c0)
+    r = ROWS
+    dgate = cat([dg0, dg1], axis=1)
+    dg_own = cat([dgate[2 * k * r : (2 * k + 1) * r] for k in range(4)])
+    dg_theirs = cat([dgate[(2 * k + 1) * r : (2 * k + 2) * r] for k in range(4)])
+    dg_own, dg_theirs = hold((dg_own, dg_theirs))
+    theirs = hold(jnp.dot(dg_theirs, x, preferred_element_type=F32).astype(BF16))
+    theirs = shift(theirs, CORE, 1)
     own_part, fwd_part = input_partials(dg0, du0, (0, 1))
     got_fwd = fetch(fwd_part, "P", "y-")
-    dg0, dg1, own_part, fwd_part = hold((dg0, dg1, own_part, fwd_part))
-
-    gg = hold(jnp.dot(cat([dg0, dg1], axis=1), x, preferred_element_type=F32).astype(BF16))
+    own = hold(jnp.dot(dg_own, x, preferred_element_type=F32).astype(BF16))
+    cg = hold(total(own, theirs))
     r = ROWS
-    own = cat([gg[2 * k * r : (2 * k + 1) * r] for k in range(4)])
-    theirs = cat([gg[(2 * k + 1) * r : (2 * k + 2) * r] for k in range(4)])
-    theirs = shift(theirs, CORE, 1)
-    cg = hold(total(own, theirs))
     gw = total(
         cg[:r],
         shift(cg[r : 2 * r], X, -1),

time: 138 us -> 139 us (level)
    unnamed x22 -> x23, local copies, waits for them, and re-layouts: 5.34 us -> 5.43 us
where the time goes in v4:
time: 139 us; the launch traced here: 138 us
  waiting for transfers between devices  58.5 us (42%)
  starting transfers between devices  49.5 us (36%)
  matrix products  16.9 us (12%)
  local copies, waits for them, and re-layouts  6.6 us (5%)
  other arithmetic  4.74 us (3%)
    ppermute x15, waiting for transfers between devices, fetch(): return lax.ppermute(x, PLANE, pairs)  46.9 us
    ppermute x16, starting transfers between devices, shift(): return lax.ppermute(x, axis, [(i, (i - by) % n) for i in range(n)])  28.9 us
    ppermute x15, starting transfers between devices, fetch(): return lax.ppermute(x, PLANE, pairs)  20.5 us
    ppermute x16, waiting for transfers between devices, shift(): return lax.ppermute(x, axis, [(i, (i - by) % n) for i in range(n)])  11.6 us
    dot_general x6, matrix products, rdot(): lax.dot_general(left, right, (((1,), (1,)), ((), ())), preferred_element_...  9.09 us
    unnamed x23, local copies, waits for them, and re-layouts  5.43 us
    dot_general x2, matrix products, input_partials(): lax.dot_general(cat([dgate, dup]), wgu, (((0,), (0,)), ((), ())), preferr...  5.16 us
  transfers between devices with their start and end apart: 31, of which 15 were waited for; matrix products, arithmetic and copies ran while one was open for 11% of the time, Pallas kernels for 0%

profile of v4, /device:TPU:1, one launch (start us, length us, event | category | flops | bytes accessed | tf_op | source)
XLA Modules:
  0.0 138.2 jit_solution(11636879422850456735)
XLA Ops:
  0.6 1.1 broadcast_select_fusion.1
  1.7 1.5 %collective-permute-start.8 = (bf16[128,896]{1,0:T(8,128)(2,1)S(1)}, bf16[128,896]{1,0:T(8,128)(2,1)S(1)}, u32[]{:S(2)}, u32[]{:S(2)}) collective-permute-start(bf16[128,896]{1,0:T(8,128)(2,1)S(1)} %get-tuple-element.96), channel_id=1, source_target_pairs={{0,2},{2,0},{1,3},{3,1},{4,6},{6,4},{5,7},{7,5},{8,10},{10,8},{9,1... | collective-permute-start | bytes 688136 | tf_op jit(solution)/shard_map/ppermute | solution.py:48
  3.2 1.0 copy-done
  4.2 1.0 copy-done.1
  5.1 1.0 copy-done.2
  6.1 0.1 prepare.1
  6.3 2.7 %collective-permute-start.1 = (bf16[240,1792]{1,0:T(8,128)(2,1)S(1)}, bf16[240,1792]{1,0:T(8,128)(2,1)S(1)}, u32[]{:S(2)}, u32[]{:S(2)}) collective-permute-start(bf16[240,1792]{1,0:T(8,128)(2,1)S(1)} %prepare.1), channel_id=1, source_target_pairs={{0,48},{16,0},{32,16},{48,32},{1,49},{17,1},{33,17},{49,33},{2,50}... | collective-permute-start | bytes 2580488 | tf_op jit(solution)/shard_map/ppermute | solution.py:48
  9.0 3.7 %collective-permute-start.11 = (bf16[256,896]{1,0:T(8,128)(2,1)S(1)}, bf16[256,896]{1,0:T(8,128)(2,1)S(1)}, u32[]{:S(2)}, u32[]{:S(2)}) collective-permute-start(bf16[256,896]{1,0:T(8,128)(2,1)S(1)} %pad_maximum_fusion.4), channel_id=1, source_target_pairs={{8,0},{9,1},{66,2},{67,3},{12,4},{13,5},{70,6},{71,7},{0,8},{1,9},... | collective-permute-start | bytes 1376264 | tf_op jit(solution)/shard_map/ppermute | solution.py:43
  12.7 0.5 collective-permute-start.10
  13.2 5.6 %collective-permute-done.11 = bf16[256,896]{1,0:T(8,128)(2,1)S(1)} collective-permute-done((bf16[256,896]{1,0:T(8,128)(2,1)S(1)}, bf16[256,896]{1,0:T(8,128)(2,1)S(1)}, u32[]{:S(2)}, u32[]{:S(2)}) %collective-permute-start.11) | collective-permute-done | bytes 458784 | tf_op jit(solution)/shard_map/ppermute | solution.py:43
  18.9 1.0 collective-permute-start.9
  19.9 3.8 %collective-permute-done.10 = bf16[256,896]{1,0:T(8,128)(2,1)S(1)} collective-permute-done((bf16[256,896]{1,0:T(8,128)(2,1)S(1)}, bf16[256,896]{1,0:T(8,128)(2,1)S(1)}, u32[]{:S(2)}, u32[]{:S(2)}) %collective-permute-start.10) | collective-permute-done | bytes 458784 | tf_op jit(solution)/shard_map/ppermute | solution.py:43
  23.8 2.7 %collective-permute-done.9 = bf16[256,896]{1,0:T(8,128)(2,1)S(1)} collective-permute-done((bf16[256,896]{1,0:T(8,128)(2,1)S(1)}, bf16[256,896]{1,0:T(8,128)(2,1)S(1)}, u32[]{:S(2)}, u32[]{:S(2)}) %collective-permute-start.9) | collective-permute-done | bytes 458784 | tf_op jit(solution)/shard_map/ppermute | solution.py:43
  26.6 2.8 %collective-permute-start.12 = (bf16[512,896]{1,0:T(8,128)(2,1)S(1)}, bf16[512,896]{1,0:T(8,128)(2,1)S(1)}, u32[]{:S(2)}, u32[]{:S(2)}) collective-permute-start(bf16[512,896]{1,0:T(8,128)(2,1)S(1)} %pad_maximum_fusion.m0), channel_id=1, source_target_pairs={{1,0},{0,1},{6,2},{7,3},{5,4},{4,5},{10,6},{11,7},{9,8},{8,9},{14,... | collective-permute-start | bytes 2752520 | tf_op jit(solution)/shard_map/ppermute | solution.py:43
  29.6 2.7 %collective-permute-start.6 = (bf16[128,1792]{1,0:T(8,128)(2,1)S(1)}, bf16[128,1792]{1,0:T(8,128)(2,1)S(1)}, u32[]{:S(2)}, u32[]{:S(2)}) collective-permute-start(bf16[128,1792]{1,0:T(8,128)(2,1)S(1)} %slice.340), channel_id=1, source_target_pairs={{0,48},{16,0},{32,16},{48,32},{1,49},{17,1},{33,17},{49,33},{2,50}... | collective-permute-start | bytes 1376264 | tf_op jit(solution)/shard_map/ppermute | solution.py:48
  32.4 4.6 %collective-permute-start.2 = (bf16[240,1792]{1,0:T(8,128)(2,1)S(1)}, bf16[240,1792]{1,0:T(8,128)(2,1)S(1)}, u32[]{:S(2)}, u32[]{:S(2)}) collective-permute-start(bf16[240,1792]{1,0:T(8,128)(2,1)S(1)} %collective-permute-done.1), channel_id=1, source_target_pairs={{0,2},{2,0},{1,3},{3,1},{4,6},{6,4},{5,7},{7,5},{8,10},{10,8},{9,1... | collective-permute-start | bytes 2580488 | tf_op jit(solution)/shard_map/ppermute | solution.py:48
  37.1 1.0 slice_dynamic-update-slice_fusion.14
  38.1 5.0 %collective-permute-start.15 = (bf16[512,896]{1,0:T(8,128)(2,1)S(1)}, bf16[512,896]{1,0:T(8,128)(2,1)S(1)}, u32[]{:S(2)}, u32[]{:S(2)}) collective-permute-start(bf16[512,896]{1,0:T(8,128)(2,1)S(1)} %pad_maximum_fusion.1), channel_id=1, source_target_pairs={{0,2},{2,0},{1,3},{3,1},{4,6},{6,4},{5,7},{7,5},{8,10},{10,8},{9,1... | collective-permute-start | bytes 2752520 | tf_op jit(solution)/shard_map/ppermute | solution.py:48
  43.1 0.6 collective-permute-start.18
  43.8 5.1 %collective-permute-start.4 = (bf16[240,1792]{1,0:T(8,128)(2,1)S(1)}, bf16[240,1792]{1,0:T(8,128)(2,1)S(1)}, u32[]{:S(2)}, u32[]{:S(2)}) collective-permute-start(bf16[240,1792]{1,0:T(8,128)(2,1)S(1)} %collective-permute-done.3), channel_id=1, source_target_pairs={{0,2},{2,0},{1,3},{3,1},{4,6},{6,4},{5,7},{7,5},{8,10},{10,8},{9,1... | collective-permute-start | bytes 2580488 | tf_op jit(solution)/shard_map/ppermute | solution.py:48
  48.9 2.0 %collective-permute-done.4 = bf16[240,1792]{1,0:T(8,128)(2,1)S(1)} collective-permute-done((bf16[240,1792]{1,0:T(8,128)(2,1)S(1)}, bf16[240,1792]{1,0:T(8,128)(2,1)S(1)}, u32[]{:S(2)}, u32[]{:S(2)}) %collective-permute-start.4) | collective-permute-done | bytes 860192 | tf_op jit(solution)/shard_map/ppermute | solution.py:48
  50.9 0.4 collective-permute-start.7
  51.3 6.2 %collective-permute-done.18 = bf16[512,896]{1,0:T(8,128)(2,1)S(1)} collective-permute-done((bf16[512,896]{1,0:T(8,128)(2,1)S(1)}, bf16[512,896]{1,0:T(8,128)(2,1)S(1)}, u32[]{:S(2)}, u32[]{:S(2)}) %collective-permute-start.18) | collective-permute-done | bytes 917536 | tf_op jit(solution)/shard_map/ppermute | solution.py:43
  57.5 1.5 %collective-permute-start.16 = (bf16[512,896]{1,0:T(8,128)(2,1)S(1)}, bf16[512,896]{1,0:T(8,128)(2,1)S(1)}, u32[]{:S(2)}, u32[]{:S(2)}) collective-permute-start(bf16[512,896]{1,0:T(8,128)(2,1)S(1)} %pad_maximum_fusion.1), channel_id=1, source_target_pairs={{1,0},{0,1},{6,2},{7,3},{5,4},{4,5},{10,6},{11,7},{9,8},{8,9},{14,... | collective-permute-start | bytes 2752520 | tf_op jit(solution)/shard_map/ppermute | solution.py:43
  58.9 1.7 %collective-permute-start.19 = (bf16[512,896]{1,0:T(8,128)(2,1)S(1)}, bf16[512,896]{1,0:T(8,128)(2,1)S(1)}, u32[]{:S(2)}, u32[]{:S(2)}) collective-permute-start(bf16[512,896]{1,0:T(8,128)(2,1)S(1)} %collective-permute-done.18), channel_id=1, source_target_pairs={{0,2},{2,0},{1,3},{3,1},{4,6},{6,4},{5,7},{7,5},{8,10},{10,8},{9,1... | collective-permute-start | bytes 2752520 | tf_op jit(solution)/shard_map/ppermute | solution.py:48
  60.7 1.1 slice_dynamic-update-slice_fusion.22
  62.0 0.7 collective-permute-start.20
  62.7 2.8 %collective-permute-start.14 = (bf16[512,896]{1,0:T(8,128)(2,1)S(1)}, bf16[512,896]{1,0:T(8,128)(2,1)S(1)}, u32[]{:S(2)}, u32[]{:S(2)}) collective-permute-start(bf16[512,896]{1,0:T(8,128)(2,1)S(1)} %collective-permute-done.12.m1), channel_id=1, source_target_pairs={{65,0},{64,1},{6,2},{7,3},{69,4},{68,5},{10,6},{11,7},{73,8},{72,9... | collective-permute-start | bytes 2752520 | tf_op jit(solution)/shard_map/ppermute | solution.py:43
  65.6 4.4 %collective-permute-done.16 = bf16[512,896]{1,0:T(8,128)(2,1)S(1)} collective-permute-done((bf16[512,896]{1,0:T(8,128)(2,1)S(1)}, bf16[512,896]{1,0:T(8,128)(2,1)S(1)}, u32[]{:S(2)}, u32[]{:S(2)}) %collective-permute-start.16) | collective-permute-done | bytes 917536 | tf_op jit(solution)/shard_map/ppermute | solution.py:43
  70.0 4.0 %collective-permute-start.17 = (bf16[512,896]{1,0:T(8,128)(2,1)S(1)}, bf16[512,896]{1,0:T(8,128)(2,1)S(1)}, u32[]{:S(2)}, u32[]{:S(2)}) collective-permute-start(bf16[512,896]{1,0:T(8,128)(2,1)S(1)} %collective-permute-done.16), channel_id=1, source_target_pairs={{0,2},{2,0},{1,3},{3,1},{4,6},{6,4},{5,7},{7,5},{8,10},{10,8},{9,1... | collective-permute-start | bytes 2752520 | tf_op jit(solution)/shard_map/ppermute | solution.py:48
  74.1 5.4 %collective-permute-done.14.m3 = bf16[512,896]{1,0:T(8,128)(2,1)S(1)} collective-permute-done((bf16[512,896]{1,0:T(8,128)(2,1)S(1)}, bf16[512,896]{1,0:T(8,128)(2,1)S(1)}, u32[]{:S(2)}, u32[]{:S(2)}) %collective-permute-start.14) | collective-permute-done | bytes 917536 | tf_op jit(solution)/shard_map/ppermute | solution.py:43
  79.5 3.6 %collective-permute-done.20.r3 = bf16[512,896]{1,0:T(8,128)(2,1)S(1)} collective-permute-done((bf16[512,896]{1,0:T(8,128)(2,1)S(1)}, bf16[512,896]{1,0:T(8,128)(2,1)S(1)}, u32[]{:S(2)}, u32[]{:S(2)}) %collective-permute-start.20) | collective-permute-done | bytes 917536 | tf_op jit(solution)/shard_map/ppermute | solution.py:43
  83.2 0.7 assemble.1
  83.9 1.4 fusion.2
  85.3 1.5 %multiply_convert_fusion.1 = (bf16[640,512]{1,0:T(8,128)(2,1)S(1)}, f32[640,512]{1,0:T(8,128)S(1)}) fusion(f32[640,512]{1,0:T(8,128)S(1)} %fusion.2, bf16[640,1792]{1,0:T(8,128)(2,1)S(1)} %get-tuple-element.73, bf16[1024,1792]{1,0:T(8,128)(2,1)S(1)} %get-tuple-element.24), kind=kOutput, calls=%fused_computation.34 | convolution fusion | flops 1176371200 | bytes 7405568 | tf_op jit(solution)/shard_map/dot_general | solution.py:52
  86.8 1.7 %fusion.36 = bf16[640,512]{1,0:T(8,128)(2,1)S(1)} fusion(f32[640,512]{1,0:T(8,128)S(1)} %get-tuple-element.100, bf16[1024,1792]{1,0:T(8,128)(2,1)S(1)} %get-tuple-element.23, bf16[1280,1792]{1,0:T(8,128)(2,1)S(1)} %get-tuple-element.74, f32[640,512]{1,0:T(8,128)S(1)} %fusion.2), kind=kOutput, calls=%fused_computation.24 | convolution fusion | flops 1177681920 | bytes 7405568 | tf_op jit(solution)/shard_map/dot_general | solution.py:52
  88.5 2.6 %convolution_convert_fusion.1 = bf16[512,1792]{1,0:T(8,128)(2,1)S(1)} fusion(bf16[1280,1792]{1,0:T(8,128)(2,1)S(1)} %get-tuple-element.74, bf16[640,512]{1,0:T(8,128)(2,1)S(1)} %get-tuple-element.26, bf16[640,512]{1,0:T(8,128)(2,1)S(1)} %fusion.36), kind=kOutput, calls=%fused_computation.1 | convolution fusion | flops 2352349184 | bytes 7733248 | tf_op jit(solution)/shard_map/dot_general | solution.py:178
  91.5 0.4 slice_select_fusion.2
  91.9 2.6 %collective-permute-start.23 = (bf16[512,896]{1,0:T(8,128)(2,1)S(1)}, bf16[512,896]{1,0:T(8,128)(2,1)S(1)}, u32[]{:S(2)}, u32[]{:S(2)}) collective-permute-start(bf16[512,896]{1,0:T(8,128)(2,1)S(1)} %get-tuple-element.27), channel_id=1, source_target_pairs={{64,0},{65,1},{10,2},{11,3},{68,4},{69,5},{14,6},{15,7},{72,8},{73... | collective-permute-start | bytes 2752520 | tf_op jit(solution)/shard_map/ppermute | solution.py:43
  94.5 1.2 collective-permute-start.22
  95.7 1.4 fusion
  97.1 1.5 %multiply_convert_fusion = (bf16[640,512]{1,0:T(8,128)(2,1)S(1)}, f32[640,512]{1,0:T(8,128)S(1)}) fusion(f32[640,512]{1,0:T(8,128)S(1)} %fusion, bf16[640,1792]{1,0:T(8,128)(2,1)S(1)} %get-tuple-element.73, bf16[512,1792]{1,0:T(8,128)(2,1)S(1)} %slice.276), kind=kOutput, calls=%fused_computation.32 | convolution fusion | flops 1176371200 | bytes 7405568 | tf_op jit(solution)/shard_map/dot_general | solution.py:52
  98.6 1.7 %fusion.41 = bf16[640,512]{1,0:T(8,128)(2,1)S(1)} fusion(f32[640,512]{1,0:T(8,128)S(1)} %get-tuple-element.102, bf16[512,1792]{1,0:T(8,128)(2,1)S(1)} %slice.275, bf16[1280,1792]{1,0:T(8,128)(2,1)S(1)} %get-tuple-element.74, f32[640,512]{1,0:T(8,128)S(1)} %fusion), kind=kOutput, calls=%fused_computation.25 | convolution fusion | flops 1177681920 | bytes 7405568 | tf_op jit(solution)/shard_map/dot_general | solution.py:52
  100.3 2.6 %convolution_convert_fusion = bf16[512,1792]{1,0:T(8,128)(2,1)S(1)} fusion(bf16[1280,1792]{1,0:T(8,128)(2,1)S(1)} %get-tuple-element.74, bf16[640,512]{1,0:T(8,128)(2,1)S(1)} %get-tuple-element.32, bf16[640,512]{1,0:T(8,128)(2,1)S(1)} %fusion.41), kind=kOutput, calls=%fused_computation | convolution fusion | flops 2352349184 | bytes 7733248 | tf_op jit(solution)/shard_map/dot_general | solution.py:178
  103.1 0.4 slice_select_fusion
  103.6 0.3 collective-permute-start.21
  104.2 1.3 convolution_convert_fusion.2
  105.7 1.3 convolution_convert_fusion.3
  107.0 9.6 %collective-permute-done.22 = bf16[512,896]{1,0:T(8,128)(2,1)S(1)} collective-permute-done((bf16[512,896]{1,0:T(8,128)(2,1)S(1)}, bf16[512,896]{1,0:T(8,128)(2,1)S(1)}, u32[]{:S(2)}, u32[]{:S(2)}) %collective-permute-start.22) | collective-permute-done | bytes 917536 | tf_op jit(solution)/shard_map/ppermute | solution.py:43
  116.6 0.4 collective-permute-done.21
  117.1 0.5 add_convert_fusion.1
  117.6 1.2 collective-permute-start.26
  118.8 1.0 collective-permute-start.25
  119.8 0.5 collective-permute-start.24
  120.4 0.3 add_convert_fusion
  120.8 0.9 collective-permute-start.29
  121.7 2.4 %collective-permute-done.26 = bf16[128,896]{1,0:T(8,128)(2,1)S(1)} collective-permute-done((bf16[128,896]{1,0:T(8,128)(2,1)S(1)}, bf16[128,896]{1,0:T(8,128)(2,1)S(1)}, u32[]{:S(2)}, u32[]{:S(2)}) %collective-permute-start.26) | collective-permute-done | bytes 229408 | tf_op jit(solution)/shard_map/ppermute | solution.py:43
  124.2 2.6 %collective-permute-done.25 = bf16[128,896]{1,0:T(8,128)(2,1)S(1)} collective-permute-done((bf16[128,896]{1,0:T(8,128)(2,1)S(1)}, bf16[128,896]{1,0:T(8,128)(2,1)S(1)}, u32[]{:S(2)}, u32[]{:S(2)}) %collective-permute-start.25) | collective-permute-done | bytes 229408 | tf_op jit(solution)/shard_map/ppermute | solution.py:43
  126.8 0.8 add_convert_fusion.3
  127.6 1.8 %collective-permute-done.30 = bf16[80,1792]{1,0:T(8,128)(2,1)S(1)} collective-permute-done((bf16[80,1792]{1,0:T(8,128)(2,1)S(1)}, bf16[80,1792]{1,0:T(8,128)(2,1)S(1)}, u32[]{:S(2)}, u32[]{:S(2)}) %collective-permute-start.30) | collective-permute-done | bytes 286752 | tf_op jit(solution)/shard_map/ppermute | solution.py:48
  129.4 5.2 %collective-permute-done.29 = bf16[80,1792]{1,0:T(8,128)(2,1)S(1)} collective-permute-done((bf16[80,1792]{1,0:T(8,128)(2,1)S(1)}, bf16[80,1792]{1,0:T(8,128)(2,1)S(1)}, u32[]{:S(2)}, u32[]{:S(2)}) %collective-permute-start.29) | collective-permute-done | bytes 286752 | tf_op jit(solution)/shard_map/ppermute | solution.py:48
  134.6 2.6 %collective-permute-done.28 = bf16[80,1792]{1,0:T(8,128)(2,1)S(1)} collective-permute-done((bf16[80,1792]{1,0:T(8,128)(2,1)S(1)}, bf16[80,1792]{1,0:T(8,128)(2,1)S(1)}, u32[]{:S(2)}, u32[]{:S(2)}) %collective-permute-start.28) | collective-permute-done | bytes 286752 | tf_op jit(solution)/shard_map/ppermute | solution.py:48
  137.2 0.2 add_convert_fusion.2
  137.4 0.8 slice_select_fusion.4
  (65 shorter events, 2.3 us)
Async XLA Ops:
  1.7 7.2 %collective-permute-start.8 = (bf16[128,896]{1,0:T(8,128)(2,1)S(1)}, bf16[128,896]{1,0:T(8,128)(2,1)S(1)}, u32[]{:S(2)}, u32[]{:S(2)}) collective-permute-start(bf16[128,896]{1,0:T(8,128)(2,1)S(1)} %get-tuple-element.96), channel_id=1, source_target_pairs={{0,2},{2,0},{1,3},{3,1},{4,6},{6,4},{5,7},{7,5},{8,10},{10,8},{9,1... | collective-permute-start | bytes 688136 | tf_op jit(solution)/shard_map/ppermute | solution.py:48
  3.2 1.0 copy-start
  4.2 1.0 copy-start.1
  5.1 1.0 copy-start.2
  6.2 26.2 %collective-permute-start = (bf16[240,1792]{1,0:T(8,128)(2,1)S(1)}, bf16[240,1792]{1,0:T(8,128)(2,1)}, u32[]{:S(2)}, u32[]{:S(2)}) collective-permute-start(bf16[240,1792]{1,0:T(8,128)(2,1)S(1)} %prepare.1), channel_id=1, source_target_pairs={{0,2},{2,0},{1,3},{3,1},{4,6},{6,4},{5,7},{7,5},{8,10},{10,8},{9,1... | collective-permute-start | bytes 2580488 | tf_op jit(solution)/shard_map/ppermute | solution.py:48
  6.3 23.2 %collective-permute-start.1 = (bf16[240,1792]{1,0:T(8,128)(2,1)S(1)}, bf16[240,1792]{1,0:T(8,128)(2,1)S(1)}, u32[]{:S(2)}, u32[]{:S(2)}) collective-permute-start(bf16[240,1792]{1,0:T(8,128)(2,1)S(1)} %prepare.1), channel_id=1, source_target_pairs={{0,48},{16,0},{32,16},{48,32},{1,49},{17,1},{33,17},{49,33},{2,50}... | collective-permute-start | bytes 2580488 | tf_op jit(solution)/shard_map/ppermute | solution.py:48
  9.0 23.4 %collective-permute-start.3 = (bf16[240,1792]{1,0:T(8,128)(2,1)S(1)}, bf16[240,1792]{1,0:T(8,128)(2,1)S(1)}, u32[]{:S(2)}, u32[]{:S(2)}) collective-permute-start(bf16[240,1792]{1,0:T(8,128)(2,1)S(1)} %prepare.1), channel_id=1, source_target_pairs={{0,16},{16,32},{32,48},{48,0},{1,17},{17,33},{33,49},{49,1},{2,18}... | collective-permute-start | bytes 2580488 | tf_op jit(solution)/shard_map/ppermute | solution.py:48
  9.0 9.9 %collective-permute-start.11 = (bf16[256,896]{1,0:T(8,128)(2,1)S(1)}, bf16[256,896]{1,0:T(8,128)(2,1)S(1)}, u32[]{:S(2)}, u32[]{:S(2)}) collective-permute-start(bf16[256,896]{1,0:T(8,128)(2,1)S(1)} %pad_maximum_fusion.4), channel_id=1, source_target_pairs={{8,0},{9,1},{66,2},{67,3},{12,4},{13,5},{70,6},{71,7},{0,8},{1,9},... | collective-permute-start | bytes 1376264 | tf_op jit(solution)/shard_map/ppermute | solution.py:43
  12.7 11.1 %collective-permute-start.10 = (bf16[256,896]{1,0:T(8,128)(2,1)S(1)}, bf16[256,896]{1,0:T(8,128)(2,1)S(1)}, u32[]{:S(2)}, u32[]{:S(2)}) collective-permute-start(bf16[256,896]{1,0:T(8,128)(2,1)S(1)} %pad_maximum_fusion.4), channel_id=1, source_target_pairs={{12,0},{13,1},{67,2},{66,3},{0,4},{1,5},{71,6},{70,7},{4,8},{5,9},... | collective-permute-start | bytes 1376264 | tf_op jit(solution)/shard_map/ppermute | solution.py:43
  18.9 7.6 %collective-permute-start.9 = (bf16[256,896]{1,0:T(8,128)(2,1)S(1)}, bf16[256,896]{1,0:T(8,128)(2,1)S(1)}, u32[]{:S(2)}, u32[]{:S(2)}) collective-permute-start(bf16[256,896]{1,0:T(8,128)(2,1)S(1)} %pad_maximum_fusion.4), channel_id=1, source_target_pairs={{4,0},{5,1},{3,2},{2,3},{8,4},{9,5},{7,6},{6,7},{12,8},{13,9},{11,... | collective-permute-start | bytes 1376264 | tf_op jit(solution)/shard_map/ppermute | solution.py:43
  26.6 35.4 %collective-permute-start.12 = (bf16[512,896]{1,0:T(8,128)(2,1)S(1)}, bf16[512,896]{1,0:T(8,128)(2,1)S(1)}, u32[]{:S(2)}, u32[]{:S(2)}) collective-permute-start(bf16[512,896]{1,0:T(8,128)(2,1)S(1)} %pad_maximum_fusion.m0), channel_id=1, source_target_pairs={{1,0},{0,1},{6,2},{7,3},{5,4},{4,5},{10,6},{11,7},{9,8},{8,9},{14,... | collective-permute-start | bytes 2752520 | tf_op jit(solution)/shard_map/ppermute | solution.py:43
  29.4 33.3 %collective-permute-start.13 = (bf16[512,896]{1,0:T(8,128)(2,1)S(1)}, bf16[512,896]{1,0:T(8,128)(2,1)S(1)}, u32[]{:S(2)}, u32[]{:S(2)}) collective-permute-start(bf16[512,896]{1,0:T(8,128)(2,1)S(1)} %pad_maximum_fusion.m0), channel_id=1, source_target_pairs={{65,0},{64,1},{14,2},{15,3},{69,4},{68,5},{2,6},{3,7},{73,8},{72,9... | collective-permute-start | bytes 2752520 | tf_op jit(solution)/shard_map/ppermute | solution.py:43
  29.6 8.5 %collective-permute-start.6 = (bf16[128,1792]{1,0:T(8,128)(2,1)S(1)}, bf16[128,1792]{1,0:T(8,128)(2,1)S(1)}, u32[]{:S(2)}, u32[]{:S(2)}) collective-permute-start(bf16[128,1792]{1,0:T(8,128)(2,1)S(1)} %slice.340), channel_id=1, source_target_pairs={{0,48},{16,0},{32,16},{48,32},{1,49},{17,1},{33,17},{49,33},{2,50}... | collective-permute-start | bytes 1376264 | tf_op jit(solution)/shard_map/ppermute | solution.py:48
  32.4 10.7 %collective-permute-start.5 = (bf16[112,1792]{1,0:T(8,128)(2,1)S(1)}, bf16[112,1792]{1,0:T(8,128)(2,1)S(1)}, u32[]{:S(2)}, u32[]{:S(2)}) collective-permute-start(bf16[112,1792]{1,0:T(8,128)(2,1)S(1)} %slice.338), channel_id=1, source_target_pairs={{0,16},{16,32},{32,48},{48,0},{1,17},{17,33},{33,49},{49,1},{2,18}... | collective-permute-start | bytes 1204232 | tf_op jit(solution)/shard_map/ppermute | solution.py:48
  32.4 11.3 %collective-permute-start.2 = (bf16[240,1792]{1,0:T(8,128)(2,1)S(1)}, bf16[240,1792]{1,0:T(8,128)(2,1)S(1)}, u32[]{:S(2)}, u32[]{:S(2)}) collective-permute-start(bf16[240,1792]{1,0:T(8,128)(2,1)S(1)} %collective-permute-done.1), channel_id=1, source_target_pairs={{0,2},{2,0},{1,3},{3,1},{4,6},{6,4},{5,7},{7,5},{8,10},{10,8},{9,1... | collective-permute-start | bytes 2580488 | tf_op jit(solution)/shard_map/ppermute | solution.py:48
  38.1 36.0 %collective-permute-start.15 = (bf16[512,896]{1,0:T(8,128)(2,1)S(1)}, bf16[512,896]{1,0:T(8,128)(2,1)S(1)}, u32[]{:S(2)}, u32[]{:S(2)}) collective-permute-start(bf16[512,896]{1,0:T(8,128)(2,1)S(1)} %pad_maximum_fusion.1), channel_id=1, source_target_pairs={{0,2},{2,0},{1,3},{3,1},{4,6},{6,4},{5,7},{7,5},{8,10},{10,8},{9,1... | collective-permute-start | bytes 2752520 | tf_op jit(solution)/shard_map/ppermute | solution.py:48
  43.1 14.4 %collective-permute-start.18 = (bf16[512,896]{1,0:T(8,128)(2,1)S(1)}, bf16[512,896]{1,0:T(8,128)(2,1)S(1)}, u32[]{:S(2)}, u32[]{:S(2)}) collective-permute-start(bf16[512,896]{1,0:T(8,128)(2,1)S(1)} %pad_maximum_fusion.1), channel_id=1, source_target_pairs={{65,0},{64,1},{14,2},{15,3},{69,4},{68,5},{2,6},{3,7},{73,8},{72,9... | collective-permute-start | bytes 2752520 | tf_op jit(solution)/shard_map/ppermute | solution.py:43
  43.8 7.1 %collective-permute-start.4 = (bf16[240,1792]{1,0:T(8,128)(2,1)S(1)}, bf16[240,1792]{1,0:T(8,128)(2,1)S(1)}, u32[]{:S(2)}, u32[]{:S(2)}) collective-permute-start(bf16[240,1792]{1,0:T(8,128)(2,1)S(1)} %collective-permute-done.3), channel_id=1, source_target_pairs={{0,2},{2,0},{1,3},{3,1},{4,6},{6,4},{5,7},{7,5},{8,10},{10,8},{9,1... | collective-permute-start | bytes 2580488 | tf_op jit(solution)/shard_map/ppermute | solution.py:48
  50.9 8.0 %collective-permute-start.7 = (bf16[240,1792]{1,0:T(8,128)(2,1)S(1)}, bf16[240,1792]{1,0:T(8,128)(2,1)S(1)}, u32[]{:S(2)}, u32[]{:S(2)}) collective-permute-start(bf16[240,1792]{1,0:T(8,128)(2,1)S(1)} %constant_dynamic-update-slice_fusion), channel_id=1, source_target_pairs={{0,2},{2,0},{1,3},{3,1},{4,6},{6,4},{5,7},{7,5},{8,10},{10,8},{9,1... | collective-permute-start | bytes 2580488 | tf_op jit(solution)/shard_map/ppermute | solution.py:48
  57.5 12.5 %collective-permute-start.16 = (bf16[512,896]{1,0:T(8,128)(2,1)S(1)}, bf16[512,896]{1,0:T(8,128)(2,1)S(1)}, u32[]{:S(2)}, u32[]{:S(2)}) collective-permute-start(bf16[512,896]{1,0:T(8,128)(2,1)S(1)} %pad_maximum_fusion.1), channel_id=1, source_target_pairs={{1,0},{0,1},{6,2},{7,3},{5,4},{4,5},{10,6},{11,7},{9,8},{8,9},{14,... | collective-permute-start | bytes 2752520 | tf_op jit(solution)/shard_map/ppermute | solution.py:43
  58.9 20.6 %collective-permute-start.19 = (bf16[512,896]{1,0:T(8,128)(2,1)S(1)}, bf16[512,896]{1,0:T(8,128)(2,1)S(1)}, u32[]{:S(2)}, u32[]{:S(2)}) collective-permute-start(bf16[512,896]{1,0:T(8,128)(2,1)S(1)} %collective-permute-done.18), channel_id=1, source_target_pairs={{0,2},{2,0},{1,3},{3,1},{4,6},{6,4},{5,7},{7,5},{8,10},{10,8},{9,1... | collective-permute-start | bytes 2752520 | tf_op jit(solution)/shard_map/ppermute | solution.py:48
  62.0 21.2 %collective-permute-start.20 = (bf16[512,896]{1,0:T(8,128)(2,1)S(1)}, bf16[512,896]{1,0:T(8,128)(2,1)S(1)}, u32[]{:S(2)}, u32[]{:S(2)}) collective-permute-start(bf16[512,896]{1,0:T(8,128)(2,1)S(1)} %collective-permute-done.18), channel_id=1, source_target_pairs={{14,0},{15,1},{1,2},{0,3},{2,4},{3,5},{5,6},{4,7},{6,8},{7,9},{9,1... | collective-permute-start | bytes 2752520 | tf_op jit(solution)/shard_map/ppermute | solution.py:43
  62.7 16.8 %collective-permute-start.14 = (bf16[512,896]{1,0:T(8,128)(2,1)S(1)}, bf16[512,896]{1,0:T(8,128)(2,1)S(1)}, u32[]{:S(2)}, u32[]{:S(2)}) collective-permute-start(bf16[512,896]{1,0:T(8,128)(2,1)S(1)} %collective-permute-done.12.m1), channel_id=1, source_target_pairs={{65,0},{64,1},{6,2},{7,3},{69,4},{68,5},{10,6},{11,7},{73,8},{72,9... | collective-permute-start | bytes 2752520 | tf_op jit(solution)/shard_map/ppermute | solution.py:43
  70.0 9.5 %collective-permute-start.17 = (bf16[512,896]{1,0:T(8,128)(2,1)S(1)}, bf16[512,896]{1,0:T(8,128)(2,1)S(1)}, u32[]{:S(2)}, u32[]{:S(2)}) collective-permute-start(bf16[512,896]{1,0:T(8,128)(2,1)S(1)} %collective-permute-done.16), channel_id=1, source_target_pairs={{0,2},{2,0},{1,3},{3,1},{4,6},{6,4},{5,7},{7,5},{8,10},{10,8},{9,1... | collective-permute-start | bytes 2752520 | tf_op jit(solution)/shard_map/ppermute | solution.py:48
  91.9 15.1 %collective-permute-start.23 = (bf16[512,896]{1,0:T(8,128)(2,1)S(1)}, bf16[512,896]{1,0:T(8,128)(2,1)S(1)}, u32[]{:S(2)}, u32[]{:S(2)}) collective-permute-start(bf16[512,896]{1,0:T(8,128)(2,1)S(1)} %get-tuple-element.27), channel_id=1, source_target_pairs={{64,0},{65,1},{10,2},{11,3},{68,4},{69,5},{14,6},{15,7},{72,8},{73... | collective-permute-start | bytes 2752520 | tf_op jit(solution)/shard_map/ppermute | solution.py:43
  94.5 22.2 %collective-permute-start.22 = (bf16[512,896]{1,0:T(8,128)(2,1)S(1)}, bf16[512,896]{1,0:T(8,128)(2,1)S(1)}, u32[]{:S(2)}, u32[]{:S(2)}) collective-permute-start(bf16[512,896]{1,0:T(8,128)(2,1)S(1)} %get-tuple-element.28), channel_id=1, source_target_pairs={{65,0},{64,1},{6,2},{7,3},{69,4},{68,5},{10,6},{11,7},{73,8},{72,9... | collective-permute-start | bytes 2752520 | tf_op jit(solution)/shard_map/ppermute | solution.py:43
  103.6 13.5 %collective-permute-start.21 = (bf16[512,896]{1,0:T(8,128)(2,1)S(1)}, bf16[512,896]{1,0:T(8,128)(2,1)S(1)}, u32[]{:S(2)}, u32[]{:S(2)}) collective-permute-start(bf16[512,896]{1,0:T(8,128)(2,1)S(1)} %get-tuple-element.34), channel_id=1, source_target_pairs={{1,0},{0,1},{14,2},{15,3},{5,4},{4,5},{2,6},{3,7},{9,8},{8,9},{6,1... | collective-permute-start | bytes 2752520 | tf_op jit(solution)/shard_map/ppermute | solution.py:43
  105.6 14.8 %collective-permute-start.27 = (bf16[320,1792]{1,0:T(8,128)(2,1)S(1)}, bf16[320,1792]{1,0:T(8,128)(2,1)S(1)}, u32[]{:S(2)}, u32[]{:S(2)}) collective-permute-start(bf16[320,1792]{1,0:T(8,128)(2,1)S(1)} %convolution_convert_fusion.2), channel_id=1, source_target_pairs={{0,2},{2,0},{1,3},{3,1},{4,6},{6,4},{5,7},{7,5},{8,10},{10,8},{9,1... | collective-permute-start | bytes 3440648 | tf_op jit(solution)/shard_map/ppermute | solution.py:48
  117.6 6.6 %collective-permute-start.26 = (bf16[128,896]{1,0:T(8,128)(2,1)S(1)}, bf16[128,896]{1,0:T(8,128)(2,1)S(1)}, u32[]{:S(2)}, u32[]{:S(2)}) collective-permute-start(bf16[128,896]{1,0:T(8,128)(2,1)S(1)} %get-tuple-element.38), channel_id=1, source_target_pairs={{8,0},{9,1},{66,2},{67,3},{12,4},{13,5},{70,6},{71,7},{0,8},{1,9},... | collective-permute-start | bytes 688136 | tf_op jit(solution)/shard_map/ppermute | solution.py:43
  118.8 8.0 %collective-permute-start.25 = (bf16[128,896]{1,0:T(8,128)(2,1)S(1)}, bf16[128,896]{1,0:T(8,128)(2,1)S(1)}, u32[]{:S(2)}, u32[]{:S(2)}) collective-permute-start(bf16[128,896]{1,0:T(8,128)(2,1)S(1)} %get-tuple-element.37), channel_id=1, source_target_pairs={{4,0},{5,1},{67,2},{66,3},{8,4},{9,5},{71,6},{70,7},{12,8},{13,9},... | collective-permute-start | bytes 688136 | tf_op jit(solution)/shard_map/ppermute | solution.py:43
  119.8 7.0 %collective-permute-start.24 = (bf16[128,896]{1,0:T(8,128)(2,1)S(1)}, bf16[128,896]{1,0:T(8,128)(2,1)S(1)}, u32[]{:S(2)}, u32[]{:S(2)}) collective-permute-start(bf16[128,896]{1,0:T(8,128)(2,1)S(1)} %get-tuple-element.36), channel_id=1, source_target_pairs={{12,0},{13,1},{3,2},{2,3},{0,4},{1,5},{7,6},{6,7},{4,8},{5,9},{11,... | collective-permute-start | bytes 688136 | tf_op jit(solution)/shard_map/ppermute | solution.py:43
  120.7 8.7 %collective-permute-start.30 = (bf16[80,1792]{1,0:T(8,128)(2,1)S(1)}, bf16[80,1792]{1,0:T(8,128)(2,1)S(1)}, u32[]{:S(2)}, u32[]{:S(2)}) collective-permute-start(bf16[80,1792]{1,0:T(8,128)(2,1)S(1)} %get-tuple-element.67), channel_id=1, source_target_pairs={{0,32},{16,48},{32,0},{48,16},{1,33},{17,49},{33,1},{49,17},{2,34}... | collective-permute-start | bytes 860168 | tf_op jit(solution)/shard_map/ppermute | solution.py:48
  120.8 13.8 %collective-permute-start.29 = (bf16[80,1792]{1,0:T(8,128)(2,1)S(1)}, bf16[80,1792]{1,0:T(8,128)(2,1)S(1)}, u32[]{:S(2)}, u32[]{:S(2)}) collective-permute-start(bf16[80,1792]{1,0:T(8,128)(2,1)S(1)} %get-tuple-element.68), channel_id=1, source_target_pairs={{0,48},{16,0},{32,16},{48,32},{1,49},{17,1},{33,17},{49,33},{2,50}... | collective-permute-start | bytes 860168 | tf_op jit(solution)/shard_map/ppermute | solution.py:48
  124.2 13.1 %collective-permute-start.28 = (bf16[80,1792]{1,0:T(8,128)(2,1)S(1)}, bf16[80,1792]{1,0:T(8,128)(2,1)S(1)}, u32[]{:S(2)}, u32[]{:S(2)}) collective-permute-start(bf16[80,1792]{1,0:T(8,128)(2,1)S(1)} %get-tuple-element.66), channel_id=1, source_target_pairs={{0,16},{16,32},{32,48},{48,0},{1,17},{17,33},{33,49},{49,1},{2,18}... | collective-permute-start | bytes 860168 | tf_op jit(solution)/shard_map/ppermute | solution.py:48

commit v5 on v4

--- a/solution.py
+++ b/solution.py
@@ -152,10 +152,14 @@
 
     own_w = prepare(side, gate_weight, up_weight, down_weight)
     wf, wb = shift(own_w, X, 1), shift(own_w, X, -1)
-    wff = cat([shift(wf[:128], X, 1), shift(wb[128:], X, -1)])
     pieces = []
-    for w in (own_w, wf, wb, wff):
+    for w in (own_w, wf, wb):
         pieces += [w, shift(w, CORE, 1)]
+    wff = shift(wf[:128], X, 1), shift(wb[128:], X, -1)
+    *wff, pieces[3], pieces[5], pass_b = hold((*wff, pieces[3], pieces[5], received[2]))
+    received = (*received[:2], pass_b, received[3])
+    wff = cat(wff)
+    pieces += [wff, shift(wff, CORE, 1)]
     wgu = hold(cat([w[:ROWS] for w in pieces] + [w[ROWS : 2 * ROWS] for w in pieces]))
     wd = hold(cat([w[2 * ROWS :] for w in pieces]))
     ff = wd.shape[0]

time: 139 us -> 134 us (0.964)
  the two profiles are of different devices: /device:TPU:1 before, /device:TPU:0 now
where the time goes in v5:
time: 134 us
  waiting for transfers between devices  71.8 us (54%)
  starting transfers between devices  37 us (28%)
  matrix products  16.9 us (13%)
  other arithmetic  4.81 us (4%)
  local copies, waits for them, and re-layouts  1.75 us (1%)
    ppermute x15, waiting for transfers between devices, fetch(): return lax.ppermute(x, PLANE, pairs)  50.4 us
    ppermute x15, starting transfers between devices, fetch(): return lax.ppermute(x, PLANE, pairs)  24.9 us
    ppermute x16, waiting for transfers between devices, shift(): return lax.ppermute(x, axis, [(i, (i - by) % n) for i in range(n)])  21.4 us
    ppermute x16, starting transfers between devices, shift(): return lax.ppermute(x, axis, [(i, (i - by) % n) for i in range(n)])  12.1 us
    dot_general x6, matrix products, rdot(): lax.dot_general(left, right, (((1,), (1,)), ((), ())), preferred_element_...  9.05 us
    dot_general x2, matrix products, input_partials(): lax.dot_general(cat([dgate, dup]), wgu, (((0,), (0,)), ((), ())), preferr...  5.16 us
  transfers between devices with their start and end apart: 31, of which 15 were waited for; matrix products, arithmetic and copies ran while one was open for 10% of the time, Pallas kernels for 1%

profile of v5, /device:TPU:0, one launch (start us, length us, event | category | flops | bytes accessed | tf_op | source)
XLA Modules:
  0.0 134.2 jit_solution(3962494006721716031)
XLA Ops:
  0.7 1.2 broadcast_select_fusion.1
  1.8 0.1 collective-permute-start.7
  1.9 1.5 %collective-permute-done.7 = bf16[128,896]{1,0:T(8,128)(2,1)S(1)} collective-permute-done((bf16[128,896]{1,0:T(8,128)(2,1)S(1)}, bf16[128,896]{1,0:T(8,128)(2,1)S(1)}, u32[]{:S(2)}, u32[]{:S(2)}) %collective-permute-start.7) | collective-permute-done | bytes 229408 | tf_op jit(solution)/shard_map/ppermute | solution.py:48
  3.5 3.4 %collective-permute-start.10 = (bf16[256,896]{1,0:T(8,128)(2,1)S(1)}, bf16[256,896]{1,0:T(8,128)(2,1)S(1)}, u32[]{:S(2)}, u32[]{:S(2)}) collective-permute-start(bf16[256,896]{1,0:T(8,128)(2,1)S(1)} %pad_maximum_fusion.4), channel_id=1, source_target_pairs={{8,0},{9,1},{66,2},{67,3},{12,4},{13,5},{70,6},{71,7},{0,8},{1,9},... | collective-permute-start | bytes 1376264 | tf_op jit(solution)/shard_map/ppermute | solution.py:43
  6.8 0.1 prepare.1
  7.0 2.8 %collective-permute-start.1 = (bf16[240,1792]{1,0:T(8,128)(2,1)S(1)}, bf16[240,1792]{1,0:T(8,128)(2,1)S(1)}, u32[]{:S(2)}, u32[]{:S(2)}) collective-permute-start(bf16[240,1792]{1,0:T(8,128)(2,1)S(1)} %prepare.1), channel_id=1, source_target_pairs={{0,48},{16,0},{32,16},{48,32},{1,49},{17,1},{33,17},{49,33},{2,50}... | collective-permute-start | bytes 2580488 | tf_op jit(solution)/shard_map/ppermute | solution.py:48
  9.8 0.7 collective-permute-start.9
  10.5 2.6 %collective-permute-start.8 = (bf16[256,896]{1,0:T(8,128)(2,1)S(1)}, bf16[256,896]{1,0:T(8,128)(2,1)S(1)}, u32[]{:S(2)}, u32[]{:S(2)}) collective-permute-start(bf16[256,896]{1,0:T(8,128)(2,1)S(1)} %pad_maximum_fusion.4), channel_id=1, source_target_pairs={{4,0},{5,1},{3,2},{2,3},{8,4},{9,5},{7,6},{6,7},{12,8},{13,9},{11,... | collective-permute-start | bytes 1376264 | tf_op jit(solution)/shard_map/ppermute | solution.py:43
  13.1 0.4 collective-permute-done.10
  13.6 5.9 %collective-permute-done.9 = bf16[256,896]{1,0:T(8,128)(2,1)S(1)} collective-permute-done((bf16[256,896]{1,0:T(8,128)(2,1)S(1)}, bf16[256,896]{1,0:T(8,128)(2,1)S(1)}, u32[]{:S(2)}, u32[]{:S(2)}) %collective-permute-start.9) | collective-permute-done | bytes 458784 | tf_op jit(solution)/shard_map/ppermute | solution.py:43
  19.7 4.1 %collective-permute-start.11 = (bf16[512,896]{1,0:T(8,128)(2,1)S(1)}, bf16[512,896]{1,0:T(8,128)(2,1)S(1)}, u32[]{:S(2)}, u32[]{:S(2)}) collective-permute-start(bf16[512,896]{1,0:T(8,128)(2,1)S(1)} %pad_maximum_fusion), channel_id=1, source_target_pairs={{65,0},{64,1},{14,2},{15,3},{69,4},{68,5},{2,6},{3,7},{73,8},{72,9... | collective-permute-start | bytes 2752520 | tf_op jit(solution)/shard_map/ppermute | solution.py:43
  23.8 5.1 %collective-permute-done.1 = bf16[240,1792]{1,0:T(8,128)(2,1)S(1)} collective-permute-done((bf16[240,1792]{1,0:T(8,128)(2,1)S(1)}, bf16[240,1792]{1,0:T(8,128)(2,1)S(1)}, u32[]{:S(2)}, u32[]{:S(2)}) %collective-permute-start.1) | collective-permute-done | bytes 860192 | tf_op jit(solution)/shard_map/ppermute | solution.py:48
  28.9 3.8 %collective-permute-start.2 = (bf16[128,1792]{1,0:T(8,128)(2,1)S(1)}, bf16[128,1792]{1,0:T(8,128)(2,1)S(1)}, u32[]{:S(2)}, u32[]{:S(2)}) collective-permute-start(bf16[128,1792]{1,0:T(8,128)(2,1)S(1)} %slice.335), channel_id=1, source_target_pairs={{0,48},{16,0},{32,16},{48,32},{1,49},{17,1},{33,17},{49,33},{2,50}... | collective-permute-start | bytes 1376264 | tf_op jit(solution)/shard_map/ppermute | solution.py:48
  32.8 1.1 collective-permute-start.18
  34.0 1.1 collective-permute-start.14
  35.1 9.5 %collective-permute-done.4 = bf16[112,1792]{1,0:T(8,128)(2,1)S(1)} collective-permute-done((bf16[112,1792]{1,0:T(8,128)(2,1)S(1)}, bf16[112,1792]{1,0:T(8,128)(2,1)S(1)}, u32[]{:S(2)}, u32[]{:S(2)}) %collective-permute-start.4) | collective-permute-done | bytes 401440 | tf_op jit(solution)/shard_map/ppermute | solution.py:48
  44.6 0.5 collective-permute-start.6
  45.1 0.1 collective-permute-start.12
  45.3 10.8 %collective-permute-done.14.m1 = bf16[512,896]{1,0:T(8,128)(2,1)S(1)} collective-permute-done((bf16[512,896]{1,0:T(8,128)(2,1)S(1)}, bf16[512,896]{1,0:T(8,128)(2,1)S(1)}, u32[]{:S(2)}, u32[]{:S(2)}) %collective-permute-start.14) | collective-permute-done | bytes 917536 | tf_op jit(solution)/shard_map/ppermute | solution.py:43
  56.1 0.7 collective-permute-start.15
  56.8 0.4 collective-permute-start.20
  57.2 2.6 %collective-permute-start.16 = (bf16[512,896]{1,0:T(8,128)(2,1)S(1)}, bf16[512,896]{1,0:T(8,128)(2,1)S(1)}, u32[]{:S(2)}, u32[]{:S(2)}) collective-permute-start(bf16[512,896]{1,0:T(8,128)(2,1)S(1)} %collective-permute-done.14.m1), channel_id=1, source_target_pairs={{65,0},{64,1},{6,2},{7,3},{69,4},{68,5},{10,6},{11,7},{73,8},{72,9... | collective-permute-start | bytes 2752520 | tf_op jit(solution)/shard_map/ppermute | solution.py:43
  59.9 0.3 collective-permute-start.19
  60.2 10.5 %collective-permute-done.15.m2 = bf16[512,896]{1,0:T(8,128)(2,1)S(1)} collective-permute-done((bf16[512,896]{1,0:T(8,128)(2,1)S(1)}, bf16[512,896]{1,0:T(8,128)(2,1)S(1)}, u32[]{:S(2)}, u32[]{:S(2)}) %collective-permute-start.15) | collective-permute-done | bytes 917536 | tf_op jit(solution)/shard_map/ppermute | solution.py:43
  70.7 9.8 %collective-permute-done.16.m3 = bf16[512,896]{1,0:T(8,128)(2,1)S(1)} collective-permute-done((bf16[512,896]{1,0:T(8,128)(2,1)S(1)}, bf16[512,896]{1,0:T(8,128)(2,1)S(1)}, u32[]{:S(2)}, u32[]{:S(2)}) %collective-permute-start.16) | collective-permute-done | bytes 917536 | tf_op jit(solution)/shard_map/ppermute | solution.py:43
  80.5 0.7 assemble.1
  81.3 0.1 slice.275
  81.4 0.1 slice.276
  82.1 1.4 %fusion.2 = f32[640,512]{1,0:T(8,128)S(1)} fusion(bf16[1280,1792]{1,0:T(8,128)(2,1)S(1)} %get-tuple-element.84, bf16[1024,1792]{1,0:T(8,128)(2,1)S(1)} %get-tuple-element.33), kind=kOutput, calls=%fused_computation.7 | convolution fusion | flops 1174405120 | bytes 5439488 | tf_op jit(solution)/shard_map/dot_general | solution.py:52
  83.4 1.5 %multiply_convert_fusion.1 = (bf16[640,512]{1,0:T(8,128)(2,1)S(1)}, f32[640,512]{1,0:T(8,128)S(1)}) fusion(f32[640,512]{1,0:T(8,128)S(1)} %fusion.2, bf16[640,1792]{1,0:T(8,128)(2,1)S(1)} %get-tuple-element.83, bf16[1024,1792]{1,0:T(8,128)(2,1)S(1)} %get-tuple-element.34), kind=kOutput, calls=%fused_computation.34 | convolution fusion | flops 1176371200 | bytes 7405568 | tf_op jit(solution)/shard_map/dot_general | solution.py:52
  84.9 1.6 %fusion.36 = bf16[640,512]{1,0:T(8,128)(2,1)S(1)} fusion(f32[640,512]{1,0:T(8,128)S(1)} %get-tuple-element.110, bf16[1024,1792]{1,0:T(8,128)(2,1)S(1)} %get-tuple-element.33, bf16[1280,1792]{1,0:T(8,128)(2,1)S(1)} %get-tuple-element.84, f32[640,512]{1,0:T(8,128)S(1)} %fusion.2), kind=kOutput, calls=%fused_computation.24 | convolution fusion | flops 1177681920 | bytes 7405568 | tf_op jit(solution)/shard_map/dot_general | solution.py:52
  86.6 2.6 %convolution_convert_fusion.1 = bf16[512,1792]{1,0:T(8,128)(2,1)S(1)} fusion(bf16[1280,1792]{1,0:T(8,128)(2,1)S(1)} %get-tuple-element.84, bf16[640,512]{1,0:T(8,128)(2,1)S(1)} %get-tuple-element.36, bf16[640,512]{1,0:T(8,128)(2,1)S(1)} %fusion.36), kind=kOutput, calls=%fused_computation.1 | convolution fusion | flops 2352349184 | bytes 7733248 | tf_op jit(solution)/shard_map/dot_general | solution.py:182
  89.2 0.1 fusion.54
  89.4 0.4 slice_select_fusion.2
  89.8 0.1 collective-permute-start.23
  89.9 2.5 %collective-permute-start.22 = (bf16[512,896]{1,0:T(8,128)(2,1)S(1)}, bf16[512,896]{1,0:T(8,128)(2,1)S(1)}, u32[]{:S(2)}, u32[]{:S(2)}) collective-permute-start(bf16[512,896]{1,0:T(8,128)(2,1)S(1)} %get-tuple-element.38), channel_id=1, source_target_pairs={{65,0},{64,1},{6,2},{7,3},{69,4},{68,5},{10,6},{11,7},{73,8},{72,9... | collective-permute-start | bytes 2752520 | tf_op jit(solution)/shard_map/ppermute | solution.py:43
  92.3 1.4 %fusion = f32[640,512]{1,0:T(8,128)S(1)} fusion(bf16[512,1792]{1,0:T(8,128)(2,1)S(1)} %slice.275, bf16[1280,1792]{1,0:T(8,128)(2,1)S(1)} %get-tuple-element.84), kind=kOutput, calls=%fused_computation.5 | convolution fusion | flops 1174405120 | bytes 5439488 | tf_op jit(solution)/shard_map/dot_general | solution.py:52
  93.7 1.5 %multiply_convert_fusion = (bf16[640,512]{1,0:T(8,128)(2,1)S(1)}, f32[640,512]{1,0:T(8,128)S(1)}) fusion(f32[640,512]{1,0:T(8,128)S(1)} %fusion, bf16[640,1792]{1,0:T(8,128)(2,1)S(1)} %get-tuple-element.83, bf16[512,1792]{1,0:T(8,128)(2,1)S(1)} %slice.276), kind=kOutput, calls=%fused_computation.32 | convolution fusion | flops 1176371200 | bytes 7405568 | tf_op jit(solution)/shard_map/dot_general | solution.py:52
  95.2 1.7 %fusion.41 = bf16[640,512]{1,0:T(8,128)(2,1)S(1)} fusion(f32[640,512]{1,0:T(8,128)S(1)} %get-tuple-element.112, bf16[512,1792]{1,0:T(8,128)(2,1)S(1)} %slice.275, bf16[1280,1792]{1,0:T(8,128)(2,1)S(1)} %get-tuple-element.84, f32[640,512]{1,0:T(8,128)S(1)} %fusion), kind=kOutput, calls=%fused_computation.25 | convolution fusion | flops 1177681920 | bytes 7405568 | tf_op jit(solution)/shard_map/dot_general | solution.py:52
  96.9 2.6 %convolution_convert_fusion = bf16[512,1792]{1,0:T(8,128)(2,1)S(1)} fusion(bf16[1280,1792]{1,0:T(8,128)(2,1)S(1)} %get-tuple-element.84, bf16[640,512]{1,0:T(8,128)(2,1)S(1)} %get-tuple-element.42, bf16[640,512]{1,0:T(8,128)(2,1)S(1)} %fusion.41), kind=kOutput, calls=%fused_computation | convolution fusion | flops 2352349184 | bytes 7733248 | tf_op jit(solution)/shard_map/dot_general | solution.py:182
  99.5 0.1 fusion.52
  99.8 0.4 slice_select_fusion
  100.2 1.1 collective-permute-start.21
  101.4 0.1 fusion.56
  101.6 1.3 %convolution_convert_fusion.2 = bf16[320,1792]{1,0:T(8,128)(2,1)S(1)} fusion(bf16[320,1024]{1,0:T(8,128)(2,1)S(1)} %pad_maximum_fusion.3, bf16[1024,1792]{1,0:T(8,128)(2,1)S(1)} %get-tuple-element.33), kind=kOutput, calls=%fused_computation.2 | convolution fusion | flops 1174978560 | bytes 5472256 | tf_op jit(solution)/shard_map/dot_general | solution.py:204
  102.9 0.1 collective-permute-start.27
  103.0 1.3 %convolution_convert_fusion.3 = bf16[320,1792]{1,0:T(8,128)(2,1)S(1)} fusion(bf16[320,1024]{1,0:T(8,128)(2,1)S(1)} %pad_maximum_fusion.2, bf16[1024,1792]{1,0:T(8,128)(2,1)S(1)} %get-tuple-element.33), kind=kOutput, calls=%fused_computation.3 | convolution fusion | flops 1174978560 | bytes 5472256 | tf_op jit(solution)/shard_map/dot_general | solution.py:208
  104.4 0.5 collective-permute-done.23
  104.9 9.9 %collective-permute-done.22 = bf16[512,896]{1,0:T(8,128)(2,1)S(1)} collective-permute-done((bf16[512,896]{1,0:T(8,128)(2,1)S(1)}, bf16[512,896]{1,0:T(8,128)(2,1)S(1)}, u32[]{:S(2)}, u32[]{:S(2)}) %collective-permute-start.22) | collective-permute-done | bytes 917536 | tf_op jit(solution)/shard_map/ppermute | solution.py:43
  114.8 0.5 add_convert_fusion.1
  115.3 1.8 %collective-permute-start.26 = (bf16[128,896]{1,0:T(8,128)(2,1)S(1)}, bf16[128,896]{1,0:T(8,128)(2,1)S(1)}, u32[]{:S(2)}, u32[]{:S(2)}) collective-permute-start(bf16[128,896]{1,0:T(8,128)(2,1)S(1)} %get-tuple-element.48), channel_id=1, source_target_pairs={{8,0},{9,1},{66,2},{67,3},{12,4},{13,5},{70,6},{71,7},{0,8},{1,9},... | collective-permute-start | bytes 688136 | tf_op jit(solution)/shard_map/ppermute | solution.py:43
  117.1 2.9 %collective-permute-start.25 = (bf16[128,896]{1,0:T(8,128)(2,1)S(1)}, bf16[128,896]{1,0:T(8,128)(2,1)S(1)}, u32[]{:S(2)}, u32[]{:S(2)}) collective-permute-start(bf16[128,896]{1,0:T(8,128)(2,1)S(1)} %get-tuple-element.47), channel_id=1, source_target_pairs={{4,0},{5,1},{67,2},{66,3},{8,4},{9,5},{71,6},{70,7},{12,8},{13,9},... | collective-permute-start | bytes 688136 | tf_op jit(solution)/shard_map/ppermute | solution.py:43
  119.9 0.3 add_convert_fusion
  120.3 1.7 %collective-permute-start.30 = (bf16[80,1792]{1,0:T(8,128)(2,1)S(1)}, bf16[80,1792]{1,0:T(8,128)(2,1)S(1)}, u32[]{:S(2)}, u32[]{:S(2)}) collective-permute-start(bf16[80,1792]{1,0:T(8,128)(2,1)S(1)} %get-tuple-element.77), channel_id=1, source_target_pairs={{0,32},{16,48},{32,0},{48,16},{1,33},{17,49},{33,1},{49,17},{2,34}... | collective-permute-start | bytes 860168 | tf_op jit(solution)/shard_map/ppermute | solution.py:48
  122.0 1.9 %collective-permute-start.29 = (bf16[80,1792]{1,0:T(8,128)(2,1)S(1)}, bf16[80,1792]{1,0:T(8,128)(2,1)S(1)}, u32[]{:S(2)}, u32[]{:S(2)}) collective-permute-start(bf16[80,1792]{1,0:T(8,128)(2,1)S(1)} %get-tuple-element.78), channel_id=1, source_target_pairs={{0,48},{16,0},{32,16},{48,32},{1,49},{17,1},{33,17},{49,33},{2,50}... | collective-permute-start | bytes 860168 | tf_op jit(solution)/shard_map/ppermute | solution.py:48
  123.9 0.8 collective-permute-start.28
  124.7 0.8 collective-permute-done.25
  125.5 1.7 %collective-permute-done.24 = bf16[128,896]{1,0:T(8,128)(2,1)S(1)} collective-permute-done((bf16[128,896]{1,0:T(8,128)(2,1)S(1)}, bf16[128,896]{1,0:T(8,128)(2,1)S(1)}, u32[]{:S(2)}, u32[]{:S(2)}) %collective-permute-start.24) | collective-permute-done | bytes 229408 | tf_op jit(solution)/shard_map/ppermute | solution.py:43
  127.2 0.8 add_convert_fusion.3
  128.0 0.6 collective-permute-done.30
  128.5 3.9 %collective-permute-done.29 = bf16[80,1792]{1,0:T(8,128)(2,1)S(1)} collective-permute-done((bf16[80,1792]{1,0:T(8,128)(2,1)S(1)}, bf16[80,1792]{1,0:T(8,128)(2,1)S(1)}, u32[]{:S(2)}, u32[]{:S(2)}) %collective-permute-start.29) | collective-permute-done | bytes 286752 | tf_op jit(solution)/shard_map/ppermute | solution.py:48
  132.4 0.8 collective-permute-done.28
  133.2 0.2 add_convert_fusion.2
  133.4 0.8 slice_select_fusion.4
  (65 shorter events, 1.7 us)
Async XLA Ops:
  0.6 6.2 %copy-start = (bf16[74,1792]{1,0:T(8,128)(2,1)S(1)}, bf16[74,1792]{1,0:T(8,128)(2,1)}, u32[]{:S(2)}) copy-start(bf16[74,1792]{1,0:T(8,128)(2,1)} %g_ref.1) | copy-start | bytes 795652
  0.6 6.2 %copy-start.1 = (bf16[74,1792]{1,0:T(8,128)(2,1)S(1)}, bf16[74,1792]{1,0:T(8,128)(2,1)}, u32[]{:S(2)}) copy-start(bf16[74,1792]{1,0:T(8,128)(2,1)} %u_ref.1) | copy-start | bytes 795652
  0.7 6.2 %copy-start.2 = (bf16[74,1792]{1,0:T(8,128)(2,1)S(1)}, bf16[74,1792]{1,0:T(8,128)(2,1)}, u32[]{:S(2)}) copy-start(bf16[74,1792]{1,0:T(8,128)(2,1)} %d_ref.1) | copy-start | bytes 795652
  1.8 1.6 %collective-permute-start.7 = (bf16[128,896]{1,0:T(8,128)(2,1)S(1)}, bf16[128,896]{1,0:T(8,128)(2,1)S(1)}, u32[]{:S(2)}, u32[]{:S(2)}) collective-permute-start(bf16[128,896]{1,0:T(8,128)(2,1)S(1)} %get-tuple-element.106), channel_id=1, source_target_pairs={{0,2},{2,0},{1,3},{3,1},{4,6},{6,4},{5,7},{7,5},{8,10},{10,8},{9,1... | collective-permute-start | bytes 688136 | tf_op jit(solution)/shard_map/ppermute | solution.py:48
  3.5 10.1 %collective-permute-start.10 = (bf16[256,896]{1,0:T(8,128)(2,1)S(1)}, bf16[256,896]{1,0:T(8,128)(2,1)S(1)}, u32[]{:S(2)}, u32[]{:S(2)}) collective-permute-start(bf16[256,896]{1,0:T(8,128)(2,1)S(1)} %pad_maximum_fusion.4), channel_id=1, source_target_pairs={{8,0},{9,1},{66,2},{67,3},{12,4},{13,5},{70,6},{71,7},{0,8},{1,9},... | collective-permute-start | bytes 1376264 | tf_op jit(solution)/shard_map/ppermute | solution.py:43
  7.0 21.9 %collective-permute-start.1 = (bf16[240,1792]{1,0:T(8,128)(2,1)S(1)}, bf16[240,1792]{1,0:T(8,128)(2,1)S(1)}, u32[]{:S(2)}, u32[]{:S(2)}) collective-permute-start(bf16[240,1792]{1,0:T(8,128)(2,1)S(1)} %prepare.1), channel_id=1, source_target_pairs={{0,48},{16,0},{32,16},{48,32},{1,49},{17,1},{33,17},{49,33},{2,50}... | collective-permute-start | bytes 2580488 | tf_op jit(solution)/shard_map/ppermute | solution.py:48
  9.8 22.9 %collective-permute-start.3 = (bf16[240,1792]{1,0:T(8,128)(2,1)S(1)}, bf16[240,1792]{1,0:T(8,128)(2,1)S(1)}, u32[]{:S(2)}, u32[]{:S(2)}) collective-permute-start(bf16[240,1792]{1,0:T(8,128)(2,1)S(1)} %prepare.1), channel_id=1, source_target_pairs={{0,16},{16,32},{32,48},{48,0},{1,17},{17,33},{33,49},{49,1},{2,18}... | collective-permute-start | bytes 2580488 | tf_op jit(solution)/shard_map/ppermute | solution.py:48
  9.8 9.7 %collective-permute-start.9 = (bf16[256,896]{1,0:T(8,128)(2,1)S(1)}, bf16[256,896]{1,0:T(8,128)(2,1)S(1)}, u32[]{:S(2)}, u32[]{:S(2)}) collective-permute-start(bf16[256,896]{1,0:T(8,128)(2,1)S(1)} %pad_maximum_fusion.4), channel_id=1, source_target_pairs={{12,0},{13,1},{67,2},{66,3},{0,4},{1,5},{71,6},{70,7},{4,8},{5,9},... | collective-permute-start | bytes 1376264 | tf_op jit(solution)/shard_map/ppermute | solution.py:43
  10.5 9.1 %collective-permute-start.8 = (bf16[256,896]{1,0:T(8,128)(2,1)S(1)}, bf16[256,896]{1,0:T(8,128)(2,1)S(1)}, u32[]{:S(2)}, u32[]{:S(2)}) collective-permute-start(bf16[256,896]{1,0:T(8,128)(2,1)S(1)} %pad_maximum_fusion.4), channel_id=1, source_target_pairs={{4,0},{5,1},{3,2},{2,3},{8,4},{9,5},{7,6},{6,7},{12,8},{13,9},{11,... | collective-permute-start | bytes 1376264 | tf_op jit(solution)/shard_map/ppermute | solution.py:43
  19.7 25.4 %collective-permute-start.11 = (bf16[512,896]{1,0:T(8,128)(2,1)S(1)}, bf16[512,896]{1,0:T(8,128)(2,1)S(1)}, u32[]{:S(2)}, u32[]{:S(2)}) collective-permute-start(bf16[512,896]{1,0:T(8,128)(2,1)S(1)} %pad_maximum_fusion), channel_id=1, source_target_pairs={{65,0},{64,1},{14,2},{15,3},{69,4},{68,5},{2,6},{3,7},{73,8},{72,9... | collective-permute-start | bytes 2752520 | tf_op jit(solution)/shard_map/ppermute | solution.py:43
  23.8 10.2 %collective-permute-start = (bf16[240,1792]{1,0:T(8,128)(2,1)S(1)}, bf16[240,1792]{1,0:T(8,128)(2,1)S(1)}, u32[]{:S(2)}, u32[]{:S(2)}) collective-permute-start(bf16[240,1792]{1,0:T(8,128)(2,1)S(1)} %prepare.1), channel_id=1, source_target_pairs={{0,2},{2,0},{1,3},{3,1},{4,6},{6,4},{5,7},{7,5},{8,10},{10,8},{9,1... | collective-permute-start | bytes 2580488 | tf_op jit(solution)/shard_map/ppermute | solution.py:48
  28.9 15.7 %collective-permute-start.2 = (bf16[128,1792]{1,0:T(8,128)(2,1)S(1)}, bf16[128,1792]{1,0:T(8,128)(2,1)S(1)}, u32[]{:S(2)}, u32[]{:S(2)}) collective-permute-start(bf16[128,1792]{1,0:T(8,128)(2,1)S(1)} %slice.335), channel_id=1, source_target_pairs={{0,48},{16,0},{32,16},{48,32},{1,49},{17,1},{33,17},{49,33},{2,50}... | collective-permute-start | bytes 1376264 | tf_op jit(solution)/shard_map/ppermute | solution.py:48
  32.7 11.9 %collective-permute-start.4 = (bf16[112,1792]{1,0:T(8,128)(2,1)S(1)}, bf16[112,1792]{1,0:T(8,128)(2,1)S(1)}, u32[]{:S(2)}, u32[]{:S(2)}) collective-permute-start(bf16[112,1792]{1,0:T(8,128)(2,1)S(1)} %slice.336), channel_id=1, source_target_pairs={{0,16},{16,32},{32,48},{48,0},{1,17},{17,33},{33,49},{49,1},{2,18}... | collective-permute-start | bytes 1204232 | tf_op jit(solution)/shard_map/ppermute | solution.py:48
  32.8 24.0 %collective-permute-start.18 = (bf16[512,896]{1,0:T(8,128)(2,1)S(1)}, bf16[512,896]{1,0:T(8,128)(2,1)S(1)}, u32[]{:S(2)}, u32[]{:S(2)}) collective-permute-start(bf16[512,896]{1,0:T(8,128)(2,1)S(1)} %pad_maximum_fusion), channel_id=1, source_target_pairs={{1,0},{0,1},{6,2},{7,3},{5,4},{4,5},{10,6},{11,7},{9,8},{8,9},{14,... | collective-permute-start | bytes 2752520 | tf_op jit(solution)/shard_map/ppermute | solution.py:43
  34.0 22.1 %collective-permute-start.14 = (bf16[512,896]{1,0:T(8,128)(2,1)S(1)}, bf16[512,896]{1,0:T(8,128)(2,1)S(1)}, u32[]{:S(2)}, u32[]{:S(2)}) collective-permute-start(bf16[512,896]{1,0:T(8,128)(2,1)S(1)} %pad_maximum_fusion.1.m0), channel_id=1, source_target_pairs={{1,0},{0,1},{6,2},{7,3},{5,4},{4,5},{10,6},{11,7},{9,8},{8,9},{14,... | collective-permute-start | bytes 2752520 | tf_op jit(solution)/shard_map/ppermute | solution.py:43
  44.6 12.2 %collective-permute-start.5 = (bf16[240,1792]{1,0:T(8,128)(2,1)S(1)}, bf16[240,1792]{1,0:T(8,128)(2,1)S(1)}, u32[]{:S(2)}, u32[]{:S(2)}) collective-permute-start(bf16[240,1792]{1,0:T(8,128)(2,1)S(1)} %collective-permute-done.1), channel_id=1, source_target_pairs={{0,2},{2,0},{1,3},{3,1},{4,6},{6,4},{5,7},{7,5},{8,10},{10,8},{9,1... | collective-permute-start | bytes 2580488 | tf_op jit(solution)/shard_map/ppermute | solution.py:48
  44.6 12.6 %collective-permute-start.6 = (bf16[240,1792]{1,0:T(8,128)(2,1)S(1)}, bf16[240,1792]{1,0:T(8,128)(2,1)S(1)}, u32[]{:S(2)}, u32[]{:S(2)}) collective-permute-start(bf16[240,1792]{1,0:T(8,128)(2,1)S(1)} %collective-permute-done.3), channel_id=1, source_target_pairs={{0,2},{2,0},{1,3},{3,1},{4,6},{6,4},{5,7},{7,5},{8,10},{10,8},{9,1... | collective-permute-start | bytes 2580488 | tf_op jit(solution)/shard_map/ppermute | solution.py:48
  45.1 14.8 %collective-permute-start.12 = (bf16[512,896]{1,0:T(8,128)(2,1)S(1)}, bf16[512,896]{1,0:T(8,128)(2,1)S(1)}, u32[]{:S(2)}, u32[]{:S(2)}) collective-permute-start(bf16[512,896]{1,0:T(8,128)(2,1)S(1)} %collective-permute-done.11), channel_id=1, source_target_pairs={{0,2},{2,0},{1,3},{3,1},{4,6},{6,4},{5,7},{7,5},{8,10},{10,8},{9,1... | collective-permute-start | bytes 2752520 | tf_op jit(solution)/shard_map/ppermute | solution.py:48
  56.1 14.6 %collective-permute-start.15 = (bf16[512,896]{1,0:T(8,128)(2,1)S(1)}, bf16[512,896]{1,0:T(8,128)(2,1)S(1)}, u32[]{:S(2)}, u32[]{:S(2)}) collective-permute-start(bf16[512,896]{1,0:T(8,128)(2,1)S(1)} %pad_maximum_fusion.1.m0), channel_id=1, source_target_pairs={{65,0},{64,1},{14,2},{15,3},{69,4},{68,5},{2,6},{3,7},{73,8},{72,9... | collective-permute-start | bytes 2752520 | tf_op jit(solution)/shard_map/ppermute | solution.py:43
  56.8 13.9 %collective-permute-start.17 = (bf16[512,896]{1,0:T(8,128)(2,1)S(1)}, bf16[512,896]{1,0:T(8,128)(2,1)S(1)}, u32[]{:S(2)}, u32[]{:S(2)}) collective-permute-start(bf16[512,896]{1,0:T(8,128)(2,1)S(1)} %pad_maximum_fusion), channel_id=1, source_target_pairs={{0,2},{2,0},{1,3},{3,1},{4,6},{6,4},{5,7},{7,5},{8,10},{10,8},{9,1... | collective-permute-start | bytes 2752520 | tf_op jit(solution)/shard_map/ppermute | solution.py:48
  56.8 23.7 %collective-permute-start.20 = (bf16[512,896]{1,0:T(8,128)(2,1)S(1)}, bf16[512,896]{1,0:T(8,128)(2,1)S(1)}, u32[]{:S(2)}, u32[]{:S(2)}) collective-permute-start(bf16[512,896]{1,0:T(8,128)(2,1)S(1)} %collective-permute-done.11), channel_id=1, source_target_pairs={{14,0},{15,1},{1,2},{0,3},{2,4},{3,5},{5,6},{4,7},{6,8},{7,9},{9,1... | collective-permute-start | bytes 2752520 | tf_op jit(solution)/shard_map/ppermute | solution.py:43
  57.2 23.3 %collective-permute-start.16 = (bf16[512,896]{1,0:T(8,128)(2,1)S(1)}, bf16[512,896]{1,0:T(8,128)(2,1)S(1)}, u32[]{:S(2)}, u32[]{:S(2)}) collective-permute-start(bf16[512,896]{1,0:T(8,128)(2,1)S(1)} %collective-permute-done.14.m1), channel_id=1, source_target_pairs={{65,0},{64,1},{6,2},{7,3},{69,4},{68,5},{10,6},{11,7},{73,8},{72,9... | collective-permute-start | bytes 2752520 | tf_op jit(solution)/shard_map/ppermute | solution.py:43
  59.9 20.7 %collective-permute-start.19 = (bf16[512,896]{1,0:T(8,128)(2,1)S(1)}, bf16[512,896]{1,0:T(8,128)(2,1)S(1)}, u32[]{:S(2)}, u32[]{:S(2)}) collective-permute-start(bf16[512,896]{1,0:T(8,128)(2,1)S(1)} %collective-permute-done.18), channel_id=1, source_target_pairs={{0,2},{2,0},{1,3},{3,1},{4,6},{6,4},{5,7},{7,5},{8,10},{10,8},{9,1... | collective-permute-start | bytes 2752520 | tf_op jit(solution)/shard_map/ppermute | solution.py:48
  70.7 10.9 %collective-permute-start.13 = (bf16[240,1792]{1,0:T(8,128)(2,1)S(1)}, bf16[240,1792]{1,0:T(8,128)(2,1)S(1)}, u32[]{:S(2)}, u32[]{:S(2)}) collective-permute-start(bf16[240,1792]{1,0:T(8,128)(2,1)S(1)} %constant_dynamic-update-slice_fusion), channel_id=1, source_target_pairs={{0,2},{2,0},{1,3},{3,1},{4,6},{6,4},{5,7},{7,5},{8,10},{10,8},{9,1... | collective-permute-start | bytes 2580488 | tf_op jit(solution)/shard_map/ppermute | solution.py:48
  89.8 15.1 %collective-permute-start.23 = (bf16[512,896]{1,0:T(8,128)(2,1)S(1)}, bf16[512,896]{1,0:T(8,128)(2,1)S(1)}, u32[]{:S(2)}, u32[]{:S(2)}) collective-permute-start(bf16[512,896]{1,0:T(8,128)(2,1)S(1)} %get-tuple-element.37), channel_id=1, source_target_pairs={{64,0},{65,1},{10,2},{11,3},{68,4},{69,5},{14,6},{15,7},{72,8},{73... | collective-permute-start | bytes 2752520 | tf_op jit(solution)/shard_map/ppermute | solution.py:43
  89.9 24.9 %collective-permute-start.22 = (bf16[512,896]{1,0:T(8,128)(2,1)S(1)}, bf16[512,896]{1,0:T(8,128)(2,1)S(1)}, u32[]{:S(2)}, u32[]{:S(2)}) collective-permute-start(bf16[512,896]{1,0:T(8,128)(2,1)S(1)} %get-tuple-element.38), channel_id=1, source_target_pairs={{65,0},{64,1},{6,2},{7,3},{69,4},{68,5},{10,6},{11,7},{73,8},{72,9... | collective-permute-start | bytes 2752520 | tf_op jit(solution)/shard_map/ppermute | solution.py:43
  100.2 14.6 %collective-permute-start.21 = (bf16[512,896]{1,0:T(8,128)(2,1)S(1)}, bf16[512,896]{1,0:T(8,128)(2,1)S(1)}, u32[]{:S(2)}, u32[]{:S(2)}) collective-permute-start(bf16[512,896]{1,0:T(8,128)(2,1)S(1)} %get-tuple-element.44), channel_id=1, source_target_pairs={{1,0},{0,1},{14,2},{15,3},{5,4},{4,5},{2,6},{3,7},{9,8},{8,9},{6,1... | collective-permute-start | bytes 2752520 | tf_op jit(solution)/shard_map/ppermute | solution.py:43
  102.9 17.0 %collective-permute-start.27 = (bf16[320,1792]{1,0:T(8,128)(2,1)S(1)}, bf16[320,1792]{1,0:T(8,128)(2,1)S(1)}, u32[]{:S(2)}, u32[]{:S(2)}) collective-permute-start(bf16[320,1792]{1,0:T(8,128)(2,1)S(1)} %convolution_convert_fusion.2), channel_id=1, source_target_pairs={{0,2},{2,0},{1,3},{3,1},{4,6},{6,4},{5,7},{7,5},{8,10},{10,8},{9,1... | collective-permute-start | bytes 3440648 | tf_op jit(solution)/shard_map/ppermute | solution.py:48
  115.3 8.6 %collective-permute-start.26 = (bf16[128,896]{1,0:T(8,128)(2,1)S(1)}, bf16[128,896]{1,0:T(8,128)(2,1)S(1)}, u32[]{:S(2)}, u32[]{:S(2)}) collective-permute-start(bf16[128,896]{1,0:T(8,128)(2,1)S(1)} %get-tuple-element.48), channel_id=1, source_target_pairs={{8,0},{9,1},{66,2},{67,3},{12,4},{13,5},{70,6},{71,7},{0,8},{1,9},... | collective-permute-start | bytes 688136 | tf_op jit(solution)/shard_map/ppermute | solution.py:43
  117.1 8.4 %collective-permute-start.25 = (bf16[128,896]{1,0:T(8,128)(2,1)S(1)}, bf16[128,896]{1,0:T(8,128)(2,1)S(1)}, u32[]{:S(2)}, u32[]{:S(2)}) collective-permute-start(bf16[128,896]{1,0:T(8,128)(2,1)S(1)} %get-tuple-element.47), channel_id=1, source_target_pairs={{4,0},{5,1},{67,2},{66,3},{8,4},{9,5},{71,6},{70,7},{12,8},{13,9},... | collective-permute-start | bytes 688136 | tf_op jit(solution)/shard_map/ppermute | solution.py:43
  119.9 7.2 %collective-permute-start.24 = (bf16[128,896]{1,0:T(8,128)(2,1)S(1)}, bf16[128,896]{1,0:T(8,128)(2,1)S(1)}, u32[]{:S(2)}, u32[]{:S(2)}) collective-permute-start(bf16[128,896]{1,0:T(8,128)(2,1)S(1)} %get-tuple-element.46), channel_id=1, source_target_pairs={{12,0},{13,1},{3,2},{2,3},{0,4},{1,5},{7,6},{6,7},{4,8},{5,9},{11,... | collective-permute-start | bytes 688136 | tf_op jit(solution)/shard_map/ppermute | solution.py:43
  120.3 8.2 %collective-permute-start.30 = (bf16[80,1792]{1,0:T(8,128)(2,1)S(1)}, bf16[80,1792]{1,0:T(8,128)(2,1)S(1)}, u32[]{:S(2)}, u32[]{:S(2)}) collective-permute-start(bf16[80,1792]{1,0:T(8,128)(2,1)S(1)} %get-tuple-element.77), channel_id=1, source_target_pairs={{0,32},{16,48},{32,0},{48,16},{1,33},{17,49},{33,1},{49,17},{2,34}... | collective-permute-start | bytes 860168 | tf_op jit(solution)/shard_map/ppermute | solution.py:48
  122.0 10.4 %collective-permute-start.29 = (bf16[80,1792]{1,0:T(8,128)(2,1)S(1)}, bf16[80,1792]{1,0:T(8,128)(2,1)S(1)}, u32[]{:S(2)}, u32[]{:S(2)}) collective-permute-start(bf16[80,1792]{1,0:T(8,128)(2,1)S(1)} %get-tuple-element.78), channel_id=1, source_target_pairs={{0,48},{16,0},{32,16},{48,32},{1,49},{17,1},{33,17},{49,33},{2,50}... | collective-permute-start | bytes 860168 | tf_op jit(solution)/shard_map/ppermute | solution.py:48
  123.9 9.3 %collective-permute-start.28 = (bf16[80,1792]{1,0:T(8,128)(2,1)S(1)}, bf16[80,1792]{1,0:T(8,128)(2,1)S(1)}, u32[]{:S(2)}, u32[]{:S(2)}) collective-permute-start(bf16[80,1792]{1,0:T(8,128)(2,1)S(1)} %get-tuple-element.76), channel_id=1, source_target_pairs={{0,16},{16,32},{32,48},{48,0},{1,17},{17,33},{33,49},{49,1},{2,18}... | collective-permute-start | bytes 860168 | tf_op jit(solution)/shard_map/ppermute | solution.py:48
